TPU v7x, 32 devices: a whole 2x2x4 slice. The times are simulated.
32 devices in a mesh: seq: 32 (over z, y, x, core), head: 1.
Axes of the slice: x: 2, y: 2, z: 4, core: 2. Of those that a mesh axis runs over, the one named last changes fastest.
Arguments:
- hidden: bfloat16 [4096, 1024], P('seq'), may hold values from -6 to 6
- query_weight: bfloat16 [1024, 512], P(None, 'head'), may hold values from -0.1875 to 0.1875
- key_weight: bfloat16 [1024, 512], P(None, 'head'), may hold values from -0.1875 to 0.1875
- values: bfloat16 [4096, 512], P('seq', 'head'), may hold values from -6 to 6
- grad_out: bfloat16 [4096, 512], P('seq', 'head'), may hold values from -6 to 6
- random_feats: float32 [8, 64, 256], P('head'), may hold values from -4 to 4
Outputs:
- grad_hidden: float32 [4096, 1024], P('seq')
- grad_values: bfloat16 [4096, 512], P('seq', 'head')
- grad_query_weight: float32 [1024, 512], P('seq', 'head')
- grad_key_weight: float32 [1024, 512], P('seq', 'head')
All inputs are finite; a program needn't handle non-finite values.
Results may differ from a plain program's by a relative error of at most 0.0038.
Values sent between devices are 32-bit elements; how exact they have to be, the bound alone decides.
No kernel may reach another device: no remote copies, remote signals or barrier semaphores. Data moves between devices by JAX's collectives and lax.ppermute only.
A program may use at most 64 MiB of HBM per device.

v0:
```python
import functools

import jax
import jax.numpy as jnp
from jax import lax
from jax.experimental import pallas as pl
from jax.experimental.pallas import tpu as pltpu
from jax.sharding import PartitionSpec as P


F32, BF16 = jnp.float32, jnp.bfloat16
NN = (((1,), (0,)), ((), ()))
NT = (((1,), (1,)), ((), ()))
TN = (((0,), (0,)), ((), ()))


def shape(*dims, dtype=F32):
    return jax.ShapeDtypeStruct(dims, dtype)


def split(value):
    high = value.astype(BF16)
    return high, (value - high.astype(F32)).astype(BF16)


def dot1(left, right, dims):
    return lax.dot_general(left, right, dims, preferred_element_type=F32)


def dot3(left, right, dims):
    lh, ll = left
    rh, rl = right
    return dot1(lh, rh, dims) + (dot1(lh, rl, dims) + dot1(ll, rh, dims))


def dot2(left, right, dims):
    rh, rl = right
    return dot1(left, rh, dims) + dot1(left, rl, dims)


CHUNK = 2
LIMIT = 24 << 20


def chunks(ref):
    step = min(CHUNK, ref.shape[0])
    return [slice(t, t + step) for t in range(0, ref.shape[0], step)]


def rows_of(ref, at, lanes=slice(None)):
    value = ref[at, :, lanes]
    return value.reshape(value.shape[0] * value.shape[1], value.shape[2])


def put(ref, at, value, lanes=slice(None)):
    ref[at, :, lanes] = value.reshape((at.stop - at.start, -1) + value.shape[1:])


def call(body, outs, *args, scratch=(), entry=(), final=False, loose=0):
    vmem = pl.BlockSpec(memory_space=pltpu.VMEM)
    specs = [vmem] * (len(entry) + len(args))
    args = [pltpu.with_memory_space_constraint(arg, pltpu.VMEM) for arg in args]
    args = list(entry) + args
    held = outs if final else jax.tree.map(lambda out: pltpu.VMEM(out.shape, out.dtype), outs)
    out_specs = jax.tree.map(lambda _: vmem, outs)
    if loose:
        held = tuple(pltpu.HBM(o.shape, o.dtype) for o in outs[:loose]) + held[loose:]
        out_specs = (pl.BlockSpec(memory_space=pl.ANY),) * loose + out_specs[loose:]
    return pl.pallas_call(
        body,
        out_shape=held,
        in_specs=specs,
        out_specs=out_specs,
        scratch_shapes=list(scratch),
        compiler_params=pltpu.CompilerParams(vmem_limit_bytes=LIMIT),
    )(*args)


def pack_pair(packed, first, second, dh):
    for h in range(packed.shape[0]):
        cols = slice(h * dh, (h + 1) * dh)
        packed[h, :, 0:dh] = first[:, cols]
        packed[h, :, dh : 2 * dh] = second[:, cols].astype(F32)


def project_key(hid, wk, val, packed, rows, weight, value, held, sems, *, dh, scale):
    step = 2 * dh
    count = weight.shape[0]
    loads = [
        pltpu.make_async_copy(hid, rows, sems.at[0]),
        pltpu.make_async_copy(val, value, sems.at[1]),
    ]
    for i in range(count):
        cols = wk.at[:, i * step : (i + 1) * step]
        loads.append(pltpu.make_async_copy(cols, weight.at[i], sems.at[2 + i]))
    for load in loads:
        load.start()
    loads[0].wait()
    loads[1].wait()
    stores = []
    for i in range(count):
        loads[2 + i].wait()
        key = dot1(rows[...], weight[i], NN) * scale
        items = value[:, i * step : (i + 1) * step].astype(F32)
        for j in range(2):
            held[2 * i + j, :, 0:dh] = key[:, j * dh : (j + 1) * dh]
            held[2 * i + j, :, dh:step] = items[:, j * dh : (j + 1) * dh]
        at = slice(2 * i, 2 * i + 2)
        stores.append(pltpu.make_async_copy(held.at[at], packed.at[at], sems.at[2 + count + i]))
        stores[-1].start()
    for store in stores:
        store.wait()


def project_query(hid, wq, gout, packed, *, dh, scale):
    pack_pair(packed, dot1(hid[...], wq[...], NN) * scale, gout, dh)


def widen(hid, wide_a, wide_b):
    half = wide_a.shape[0]
    wide_a[...] = hid[0:half].astype(F32)
    wide_b[...] = hid[half:].astype(F32)


def inner_of(group):
    return lax.rem(lax.axis_index("seq"), group)


def feats_of(rows, table):
    logits = dot3(split(rows), table, NN)
    half = 0.5 * jnp.sum(rows * rows, axis=1, keepdims=True)
    return jnp.exp(logits - half) * table[0].shape[1] ** (-0.5)


def key_state(feats, mine, bfeat, state, *, dh):
    table = split(feats[inner_of(feats.shape[0])])
    total = jnp.zeros((dh, state.shape[1]), F32)
    normal = jnp.zeros((1, state.shape[1]), F32)
    for at in chunks(mine):
        value = rows_of(mine, at, slice(dh, 2 * dh)).astype(BF16)
        feat = feats_of(rows_of(mine, at, slice(0, dh)), table)
        put(bfeat, at, feat)
        total = total + dot2(value, split(feat), TN)
        normal = normal + jnp.sum(feat, axis=0, keepdims=True)
    state[0:dh] = total
    state[dh:] = jnp.broadcast_to(normal, (state.shape[0] - dh, state.shape[1]))


def query_feats(feats, mine, afeat, *, dh):
    table = split(feats[inner_of(feats.shape[0])])
    for at in chunks(mine):
        put(afeat, at, feats_of(rows_of(mine, at, slice(0, dh)), table))


def query_state(mine, afeat, *refs, dh):
    parts, (state, scaled, gstate) = refs[:-3], refs[-3:]
    summed = sum(part[...] for part in parts)
    state[...] = summed
    pair = split(summed)
    total = jnp.zeros(gstate.shape, F32)
    for at in chunks(mine):
        upstream = rows_of(mine, at, slice(dh, 2 * dh))
        feat = split(rows_of(afeat, at))
        both = dot3(feat, pair, NT)
        inv = 1.0 / both[:, dh : dh + 1]
        gn = upstream * inv
        gd = -jnp.sum(gn * both[:, :dh], axis=1, keepdims=True) * inv
        zeros = jnp.zeros((gn.shape[0], gstate.shape[0] - dh - 1), F32)
        rows = jnp.concatenate([gn, gd, zeros], axis=1)
        put(scaled, at, rows)
        total = total + dot3(split(rows), feat, TN)
    gstate[...] = total


def row_grad(rows, feat, grads, table):
    weighted = feat * grads
    back = dot3(split(weighted), table, NT)
    return back - rows * jnp.sum(weighted, axis=1, keepdims=True)


def query_grad(feats, mine, afeat, state, scaled, out, *, dh):
    table = split(feats[inner_of(feats.shape[0])])
    pair = split(state[...])
    for at in chunks(mine):
        grads = dot3(split(rows_of(scaled, at)), pair, NN)
        put(out, at, row_grad(rows_of(mine, at, slice(0, dh)), rows_of(afeat, at), grads, table))


def emit_blocks(outer_index, total, held, outs):
    outer, _, width = held.shape
    for o in range(outer):
        held[o] = total[:, o * width : (o + 1) * width]
    for s, out in enumerate(outs):
        for i in range(out.shape[0]):
            out[i] = held[outer_index ^ (i * len(outs) + s)]


def gather_rows(*refs):
    blocks, rows_all = refs[:-1], refs[-1]
    group = len(blocks) // 2
    half = blocks[0].shape[0]
    inner = inner_of(group)
    for j in range(group):
        start = pl.multiple_of((inner ^ j) * 2 * half, 2 * half)
        for side in range(2):
            rows = blocks[2 * j + side][...].astype(BF16)
            rows_all[pl.ds(start + side * half, half), :] = rows


def key_grad(feats, mine, bfeat, dq, rows_all, *refs, dh, scale, count):
    parts, back, outs = refs[:count], refs[count], refs[count + 1 : -4]
    left, held, sent, sems = refs[-4:]
    group = mine.shape[0]
    copies = []
    table = split(feats[inner_of(feats.shape[0])])
    summed = sum(part[...] for part in parts)
    pair = split(summed[:dh])
    normal = summed[dh : dh + 1]
    tok = mine.shape[1]
    for at in chunks(mine):
        value = rows_of(mine, at, slice(dh, 2 * dh)).astype(BF16)
        grads = dot2(value, pair, NN) + normal
        feat = rows_of(bfeat, at)
        dv = dot3(split(feat), pair, NT)
        dk = row_grad(rows_of(mine, at, slice(0, dh)), feat, grads, table)
        both = jnp.concatenate([rows_of(dq, at), dk], axis=1) * scale
        left[at.start * tok : at.stop * tok, :] = both.astype(BF16)
        for t in range(at.start, at.stop):
            here = slice((t - at.start) * tok, (t - at.start + 1) * tok)
            sent[t, 0:tok, 0:dh] = dk[here]
            sent[t, 0:tok, dh : 2 * dh] = dv[here]
            sent[t, tok:, 0:dh] = dq[t, 0 : tok // 2]
            sent[t, tok:, dh : 2 * dh] = dq[t, tok // 2 :]
        copies.append(pltpu.make_async_copy(sent.at[at], back.at[at], sems.at[len(copies)]))
        copies[-1].start()
    outer_index = lax.axis_index("seq") // group
    emit_blocks(outer_index, dot1(left[...], rows_all[...], TN), held, outs)
    for copy in copies:
        copy.wait()


def finish_rows(wq, wk, back, grad_hidden, grad_values, *, scale):
    heads, rows, lanes = back.shape
    tok, dh = rows * 2 // 3, lanes // 2
    dqs, dks = [], []
    for h in range(heads):
        dks.append(back[h, 0:tok, 0:dh])
        dqs.append(jnp.concatenate([back[h, tok:, 0:dh], back[h, tok:, dh:]], axis=0))
        grad_values[:, h * dh : (h + 1) * dh] = back[h, 0:tok, dh:].astype(BF16)
    dq = (jnp.concatenate(dqs, axis=1) * scale).astype(BF16)
    dk = (jnp.concatenate(dks, axis=1) * scale).astype(BF16)
    grad_hidden[...] = dot1(dq, wq[...], NT) + dot1(dk, wk[...], NT)


def turn(*refs, count):
    parts, outs, flat = refs[:count], refs[count:-1], refs[-1]
    turned = sum(part[...] for part in parts).T
    group, rows, _ = flat.shape
    for i in range(group):
        flat[i] = turned[i * rows : (i + 1) * rows]
    inner = inner_of(group)
    for i, out in enumerate(outs):
        for j in range(out.shape[0]):
            out[j] = flat[inner ^ (2 * i + j)]


def join(*refs):
    firsts, last, (gq, gk), own = refs[:-4], refs[-4], refs[-3:-1], refs[-1]
    inner = inner_of(own.shape[0])
    for i, first in enumerate(firsts):
        own[inner ^ (2 * i)] = first[0]
        own[inner ^ (2 * i + 1)] = last[i]
    dh = own.shape[2] // 2
    for h in range(own.shape[0]):
        cols = slice(h * dh, (h + 1) * dh)
        gq[:, cols] = own[h, :, 0:dh]
        gk[:, cols] = own[h, :, dh:]


def make_shards(seq_count, head_count):
    def exchange(value, mask):
        return lax.ppermute(value, "seq", [(i, i ^ mask) for i in range(seq_count)])

    def inner_shards(hidden, query_weight, key_weight, values, grad_out, random_feats):
        tok, width = hidden.shape
        group, dh, feats = random_feats.shape
        outer = seq_count // group
        assert outer * group == seq_count and outer & (outer - 1) == 0
        assert group & (group - 1) == 0 and width % seq_count == 0
        scale = dh ** (-0.25)
        padded = dh + 8
        groups = [[o * group + i for i in range(group)] for o in range(outer)]
        radices = [2] * ((outer.bit_length() - 1) % 2) + [4] * ((outer.bit_length() - 1) // 2)

        def spread(value):
            return lax.all_to_all(
                value, "seq", 0, 0, axis_index_groups=groups, tiled=True
            )

        def plane_parts(value):
            parts, stride = [value], group
            for radix in radices:
                value = sum(parts)
                parts = [value] + [exchange(value, s * stride) for s in range(1, radix)]
                stride *= radix
            return parts

        def reduce_rows(sent):
            stride = group
            for i, radix in enumerate(radices):
                parts = [sent[0]] + [exchange(sent[s], s * stride) for s in range(1, radix)]
                stride *= radix
                if i + 1 < len(radices):
                    total = sum(parts)
                    total = total.reshape((-1, radices[i + 1]) + total.shape[1:])
                    sent = [total[:, s] for s in range(radices[i + 1])]
            return [part.reshape(part.shape[1:]) for part in parts]

        hbm = pl.BlockSpec(memory_space=pl.ANY)
        packed_kv = pl.pallas_call(
            functools.partial(project_key, dh=dh, scale=scale),
            out_shape=pltpu.HBM((group, tok, 2 * dh), F32),
            in_specs=[hbm] * 3,
            out_specs=hbm,
            scratch_shapes=[
                pltpu.VMEM((tok, width), BF16),
                pltpu.VMEM((group // 2, width, 2 * dh), BF16),
                pltpu.VMEM((tok, group * dh), BF16),
                pltpu.VMEM((group, tok, 2 * dh), F32),
                pltpu.SemaphoreType.DMA((2 + group,)),
            ],
            compiler_params=pltpu.CompilerParams(vmem_limit_bytes=LIMIT),
        )(*(pltpu.with_memory_space_constraint(x, pltpu.HBM) for x in (hidden, key_weight, values)))
        mine_kv = spread(packed_kv)
        packed_qg = call(
            functools.partial(project_query, dh=dh, scale=scale),
            shape(group, tok, 2 * dh),
            entry=(hidden, query_weight, grad_out),
        )
        mine_qg = spread(packed_qg)
        wide_a, wide_b = call(
            widen, (shape(tok // 2, width), shape(tok // 2, width)), entry=(hidden,)
        )

        bits = [1 << b for b in range(group.bit_length() - 1)]
        side_a = bits[1:] + bits[:1]
        side_b = bits[1:][::-1] + bits[:1]
        halves = [{0: wide_a}, {0: wide_b}]

        def gather_step(halves, k):
            return [
                side | {j ^ order[k]: exchange(item, order[k]) for j, item in side.items()}
                for side, order in zip(halves, (side_a, side_b))
            ]

        halves = gather_step(halves, 0)
        bfeat, state = call(
            functools.partial(key_state, dh=dh),
            (shape(group, tok, feats), shape(padded, feats)),
            mine_kv, entry=(random_feats,),
        )
        states = plane_parts(state)
        for k in range(1, len(bits) - 1):
            halves = gather_step(halves, k)
        afeat = call(
            functools.partial(query_feats, dh=dh),
            shape(group, tok, feats),
            mine_qg, entry=(random_feats,),
        )
        state, scaled, gstate = call(
            functools.partial(query_state, dh=dh),
            (shape(padded, feats), shape(group, tok, padded), shape(padded, feats)),
            mine_qg, afeat, *states,
        )
        gstates = plane_parts(gstate)
        dq = call(
            functools.partial(query_grad, dh=dh),
            shape(group, tok, dh),
            mine_qg, afeat, state, scaled, entry=(random_feats,),
        )
        halves = gather_step(halves, len(bits) - 1) if len(bits) > 1 else halves
        blocks = [side[j] for j in range(group) for side in halves]
        rows_all = call(gather_rows, shape(group * tok, width, dtype=BF16), *blocks)
        radix = radices[0]
        slabs = tuple(shape(outer // radix, 2 * dh, width // outer) for _ in range(radix))
        back, *sent = call(
            functools.partial(key_grad, dh=dh, scale=scale, count=len(gstates)),
            (shape(group, tok + tok // 2, 2 * dh),) + slabs,
            mine_kv, bfeat, dq, rows_all, *gstates, entry=(random_feats,), loose=1,
            scratch=[
                pltpu.VMEM((group * tok, 2 * dh), BF16),
                pltpu.VMEM((outer, 2 * dh, width // outer), F32),
                pltpu.VMEM((group, tok + tok // 2, 2 * dh), F32),
                pltpu.SemaphoreType.DMA((group,)),
            ],
        )
        parts = reduce_rows(sent)
        back = spread(back)
        grad_hidden, grad_values = call(
            functools.partial(finish_rows, scale=scale),
            (shape(tok, width), shape(tok, group * dh, dtype=BF16)),
            back, entry=(query_weight, key_weight), final=True,
        )
        if head_count > 1:
            grad_hidden = lax.psum(grad_hidden, "head")
        rows = width // seq_count
        mine, *others = call(
            functools.partial(turn, count=len(parts)),
            tuple(shape(2, rows, 2 * dh) for _ in range(group // 2)),
            *parts,
            scratch=[pltpu.VMEM((group, rows, 2 * dh), F32)],
        )
        firsts = [mine] + [exchange(item, 2 * i + 2) for i, item in enumerate(others)]
        last = exchange(jnp.stack([item[1] for item in firsts]), 1)
        grad_query_weight, grad_key_weight = call(
            join, (shape(rows, group * dh), shape(rows, group * dh)),
            *firsts, last, final=True,
            scratch=[pltpu.VMEM((group, rows, 2 * dh), F32)],
        )
        return (grad_hidden, grad_values, grad_query_weight, grad_key_weight)

    return inner_shards


def solution(mesh):
    placed = (
        P("seq", None),
        P(None, "head"),
        P(None, "head"),
        P("seq", "head"),
        P("seq", "head"),
        P("head", None, None),
    )
    return jax.shard_map(
        make_shards(mesh.shape["seq"], mesh.shape["head"]),
        mesh=mesh,
        in_specs=placed,
        out_specs=(P("seq", None), P("seq", "head"), P("seq", "head"), P("seq", "head")),
        check_vma=False,
    )
```

profile of v0, /device:TPU:0, one launch (start us, length us, event | category | flops | bytes accessed | tf_op | source)
XLA Modules:
  0.0 97.0 jit_solution(8433003102450555270)
XLA Ops:
  0.7 3.1 %shard_map.93 = f32[8,128,128]{2,1,0:T(8,128)} custom-call(bf16[128,1024]{1,0:T(8,128)(2,1)} %hid.5, bf16[1024,512]{1,0:T(8,128)(2,1)} %wk.3, bf16[128,512]{1,0:T(8,128)(2,1)} %val.1), custom_call_target="tpu_custom_call" | custom-call | tf_op jit(solution)/shard_map/pallas_call | solution.py:320
  3.8 5.3 %all-to-all-start = ((f32[8,128,128]{2,1,0:T(8,128)}), f32[8,128,128]{2,1,0:T(8,128)S(1)}, u32[]{:S(2)}, u32[]{:S(2)}) async-start(f32[8,128,128]{2,1,0:T(8,128)} %shard_map.93), calls=%async_computation | async-start | bytes 1048576 | tf_op jit(solution)/shard_map/all_to_all | solution.py:296
  9.2 2.1 %collective-permute-start.5 = (f32[64,1024]{1,0:T(8,128)S(1)}, f32[64,1024]{1,0:T(8,128)S(1)}, u32[]{:S(2)}, u32[]{:S(2)}) collective-permute-start(f32[64,1024]{1,0:T(8,128)S(1)} %get-tuple-element.28.refs_0_), channel_id=1, source_target_pairs={{0,2},{1,3},{2,0},{3,1},{4,6},{5,7},{6,4},{7,5},{8,10},{9,11},{10,... | collective-permute-start | bytes 786440 | tf_op jit(solution)/shard_map/ppermute | solution.py:282
  11.3 1.5 %collective-permute-start.10 = (f32[64,1024]{1,0:T(8,128)S(1)}, f32[64,1024]{1,0:T(8,128)}, u32[]{:S(2)}, u32[]{:S(2)}) collective-permute-start(f32[64,1024]{1,0:T(8,128)S(1)} %get-tuple-element.29.refs_1_), channel_id=1, source_target_pairs={{0,4},{1,5},{2,6},{3,7},{4,0},{5,1},{6,2},{7,3},{8,12},{9,13},{10,... | collective-permute-start | bytes 786440 | tf_op jit(solution)/shard_map/ppermute | solution.py:282
  12.7 0.6 collective-permute-start.9
  13.4 10.8 %collective-permute-done.5.refs_4_ = f32[64,1024]{1,0:T(8,128)S(1)} collective-permute-done((f32[64,1024]{1,0:T(8,128)S(1)}, f32[64,1024]{1,0:T(8,128)S(1)}, u32[]{:S(2)}, u32[]{:S(2)}) %collective-permute-start.5) | collective-permute-done | bytes 262176 | tf_op jit(solution)/shard_map/ppermute | solution.py:282
  24.2 1.4 %collective-permute-start.13 = (f32[64,1024]{1,0:T(8,128)S(1)}, f32[64,1024]{1,0:T(8,128)}, u32[]{:S(2)}, u32[]{:S(2)}) collective-permute-start(f32[64,1024]{1,0:T(8,128)S(1)} %collective-permute-done.5.refs_4_), channel_id=1, source_target_pairs={{0,4},{1,5},{2,6},{3,7},{4,0},{5,1},{6,2},{7,3},{8,12},{9,13},{10,... | collective-permute-start | bytes 786440 | tf_op jit(solution)/shard_map/ppermute | solution.py:282
  25.6 4.1 %collective-permute-done.9.refs_8_ = f32[64,1024]{1,0:T(8,128)S(1)} collective-permute-done((f32[64,1024]{1,0:T(8,128)S(1)}, f32[64,1024]{1,0:T(8,128)S(1)}, u32[]{:S(2)}, u32[]{:S(2)}) %collective-permute-start.9) | collective-permute-done | bytes 262176 | tf_op jit(solution)/shard_map/ppermute | solution.py:282
  29.8 0.9 collective-permute-start.14
  30.7 0.7 copy-done.8
  31.4 1.2 %shard_map.95 = f32[8,128,128]{2,1,0:T(8,128)} custom-call(bf16[128,1024]{1,0:T(8,128)(2,1)S(1)} %copy-done.3, bf16[1024,512]{1,0:T(8,128)(2,1)S(1)} %copy-done.1, bf16[128,512]{1,0:T(8,128)(2,1)S(1)} %copy-done.10), custom_call_target="tpu_custom_call" | custom-call | tf_op jit(solution)/shard_map/pallas_call | solution.py:69
  32.7 3.5 %all-to-all-start.1 = ((f32[8,128,128]{2,1,0:T(8,128)}), f32[8,128,128]{2,1,0:T(8,128)S(1)}, u32[]{:S(2)}, u32[]{:S(2)}) async-start(f32[8,128,128]{2,1,0:T(8,128)} %shard_map.95), calls=%async_computation.1 | async-start | bytes 1048576 | tf_op jit(solution)/shard_map/all_to_all | solution.py:296
  36.2 1.3 %shard_map.94 = (f32[8,128,256]{2,1,0:T(8,128)S(1)}, f32[72,256]{1,0:T(8,128)S(1)}) custom-call(f32[8,64,256]{2,1,0:T(8,128)S(1)} %copy-done, f32[8,128,128]{2,1,0:T(8,128)S(1)} %all-to-all-done.mine), custom_call_target="tpu_custom_call" | custom-call | tf_op jit(solution)/shard_map/pallas_call | solution.py:69
  37.5 1.0 %copy-done.4 = f32[8,128,256]{2,1,0:T(8,128)} copy-done((f32[8,128,256]{2,1,0:T(8,128)}, f32[8,128,256]{2,1,0:T(8,128)S(1)}, u32[]{:S(2)}) %copy-start.4) | copy-done | bytes 1048600
  38.5 1.6 %collective-permute-start = (f32[72,256]{1,0:T(8,128)S(1)}, f32[72,256]{1,0:T(8,128)S(1)}, u32[]{:S(2)}, u32[]{:S(2)}) collective-permute-start(f32[72,256]{1,0:T(8,128)S(1)} %get-tuple-element.25.refs_0_), channel_id=1, source_target_pairs={{0,8},{1,9},{2,10},{3,11},{4,12},{5,13},{6,14},{7,15},{8,0},{9,1},... | collective-permute-start | bytes 221192 | tf_op jit(solution)/shard_map/ppermute | solution.py:282
  40.1 0.2 collective-permute-start.7
  40.3 2.6 %collective-permute-start.1 = (f32[72,256]{1,0:T(8,128)S(1)}, f32[72,256]{1,0:T(8,128)S(1)}, u32[]{:S(2)}, u32[]{:S(2)}) collective-permute-start(f32[72,256]{1,0:T(8,128)S(1)} %get-tuple-element.25.refs_0_), channel_id=1, source_target_pairs={{0,16},{1,17},{2,18},{3,19},{4,20},{5,21},{6,22},{7,23},{8,24},{9,... | collective-permute-start | bytes 221192 | tf_op jit(solution)/shard_map/ppermute | solution.py:282
  42.9 0.2 collective-permute-start.2
  43.1 0.5 collective-permute-start.8
  43.6 5.8 %collective-permute-done.1.refs_2_ = f32[72,256]{1,0:T(8,128)S(1)} collective-permute-done((f32[72,256]{1,0:T(8,128)S(1)}, f32[72,256]{1,0:T(8,128)S(1)}, u32[]{:S(2)}, u32[]{:S(2)}) %collective-permute-start.1) | collective-permute-done | bytes 73760 | tf_op jit(solution)/shard_map/ppermute | solution.py:282
  49.4 0.6 copy-done.11
  50.1 0.6 copy-done.13
  50.7 0.5 collective-permute-start.16
  51.2 0.6 shard_map.96.afeat
  51.8 0.3 copy-done.12
  52.1 1.9 %shard_map.97 = (f32[72,256]{1,0:T(8,128)S(1)}, f32[8,128,72]{2,1,0:T(8,128)S(1)}, f32[72,256]{1,0:T(8,128)S(1)}) custom-call(f32[8,128,128]{2,1,0:T(8,128)S(1)} %all-to-all-done.1.mine, f32[8,128,256]{2,1,0:T(8,128)S(1)} %shard_map.96.afeat, f32[72,256]{1,0:T(8,128)S(1)} %get-tuple-element.25.refs_0_, f32[72,256]{1,0:T(8,128)S(1)} %collective-permute-done.refs_1_, ...), custom_call_target="tpu_custom_call" | custom-call | tf_op jit(solution)/shard_map/pallas_call | solution.py:69
  54.0 0.5 collective-permute-start.17
  54.5 2.7 %collective-permute-start.18 = (f32[72,256]{1,0:T(8,128)S(1)}, f32[72,256]{1,0:T(8,128)S(1)}, u32[]{:S(2)}, u32[]{:S(2)}) collective-permute-start(f32[72,256]{1,0:T(8,128)S(1)} %get-tuple-element.30.refs_0_), channel_id=1, source_target_pairs={{0,16},{1,17},{2,18},{3,19},{4,20},{5,21},{6,22},{7,23},{8,24},{9,... | collective-permute-start | bytes 221192 | tf_op jit(solution)/shard_map/ppermute | solution.py:282
  57.2 1.3 %collective-permute-start.19 = (f32[72,256]{1,0:T(8,128)S(1)}, f32[72,256]{1,0:T(8,128)S(1)}, u32[]{:S(2)}, u32[]{:S(2)}) collective-permute-start(f32[72,256]{1,0:T(8,128)S(1)} %get-tuple-element.30.refs_0_), channel_id=1, source_target_pairs={{0,24},{1,25},{2,26},{3,27},{4,28},{5,29},{6,30},{7,31},{8,16},{9,... | collective-permute-start | bytes 221192 | tf_op jit(solution)/shard_map/ppermute | solution.py:282
  58.5 1.2 %shard_map.98.dq = f32[8,128,64]{2,1,0:T(8,128)S(1)} custom-call(f32[8,64,256]{2,1,0:T(8,128)S(1)} %copy-done, f32[8,128,128]{2,1,0:T(8,128)S(1)} %all-to-all-done.1.mine, f32[8,128,256]{2,1,0:T(8,128)S(1)} %shard_map.96.afeat, f32[72,256]{1,0:T(8,128)S(1)} %get-tuple-element.26.state, f32[8,128,72]{2,1,0:T(8,128)S(1)} %get-tuple-element.27.scaled), custom_call_target="tpu_custom_call" | custom-call | tf_op jit(solution)/shard_map/pallas_call | solution.py:69
  59.8 2.0 %shard_map.100.rows_all = bf16[1024,1024]{1,0:T(8,128)(2,1)S(1)} custom-call(f32[64,1024]{1,0:T(8,128)S(1)} %get-tuple-element.28.refs_0_, f32[64,1024]{1,0:T(8,128)S(1)} %get-tuple-element.29.refs_1_, f32[64,1024]{1,0:T(8,128)} %collective-permute-done.3.refs_2_, f32[64,1024]{1,0:T(8,128)} %collective-permute-done.4.refs_3_, ...), custom_call_target="tpu_custom_call" | custom-call | tf_op jit(solution)/shard_map/pallas_call | solution.py:69
  61.8 0.9 collective-permute-done.18.refs_2_
  62.7 0.8 collective-permute-done.19.refs_3_
  63.5 2.6 %shard_map.101 = (f32[8,192,128]{2,1,0:T(8,128)}, f32[1,128,256]{2,1,0:T(8,128)S(1)}, f32[1,128,256]{2,1,0:T(8,128)S(1)}, f32[1,128,256]{2,1,0:T(8,128)S(1)}, f32[1,128,256]{2,1,0:T(8,128)S(1)}) custom-call(f32[8,64,256]{2,1,0:T(8,128)S(1)} %copy-done, f32[8,128,128]{2,1,0:T(8,128)S(1)} %all-to-all-done.mine, f32[8,128,256]{2,1,0:T(8,128)S(1)} %copy-done.5, ...), custom_call_target="tpu_custom_call" | custom-call | tf_op jit(solution)/shard_map/pallas_call | solution.py:69
  66.1 4.1 %all-to-all-start.2 = ((f32[8,192,128]{2,1,0:T(8,128)}), f32[8,192,128]{2,1,0:T(8,128)S(1)}, u32[]{:S(2)}, u32[]{:S(2)}) async-start(f32[8,192,128]{2,1,0:T(8,128)} %get-tuple-element.31), calls=%async_computation.2 | async-start | bytes 1572864 | tf_op jit(solution)/shard_map/all_to_all | solution.py:296
  70.2 1.7 %collective-permute-start.20 = (f32[1,128,256]{2,1,0:T(8,128)S(1)}, f32[1,128,256]{2,1,0:T(8,128)S(1)}, u32[]{:S(2)}, u32[]{:S(2)}) collective-permute-start(f32[1,128,256]{2,1,0:T(8,128)S(1)} %get-tuple-element.35), channel_id=1, source_target_pairs={{0,8},{1,9},{2,10},{3,11},{4,12},{5,13},{6,14},{7,15},{8,0},{9,1},... | collective-permute-start | bytes 393224 | tf_op jit(solution)/shard_map/ppermute | solution.py:282
  71.9 1.5 %collective-permute-start.21 = (f32[1,128,256]{2,1,0:T(8,128)S(1)}, f32[1,128,256]{2,1,0:T(8,128)S(1)}, u32[]{:S(2)}, u32[]{:S(2)}) collective-permute-start(f32[1,128,256]{2,1,0:T(8,128)S(1)} %get-tuple-element.36), channel_id=1, source_target_pairs={{0,16},{1,17},{2,18},{3,19},{4,20},{5,21},{6,22},{7,23},{8,24},{9,... | collective-permute-start | bytes 393224 | tf_op jit(solution)/shard_map/ppermute | solution.py:282
  73.5 1.1 %collective-permute-start.22 = (f32[1,128,256]{2,1,0:T(8,128)S(1)}, f32[1,128,256]{2,1,0:T(8,128)S(1)}, u32[]{:S(2)}, u32[]{:S(2)}) collective-permute-start(f32[1,128,256]{2,1,0:T(8,128)S(1)} %get-tuple-element.37), channel_id=1, source_target_pairs={{0,24},{1,25},{2,26},{3,27},{4,28},{5,29},{6,30},{7,31},{8,16},{9,... | collective-permute-start | bytes 393224 | tf_op jit(solution)/shard_map/ppermute | solution.py:282
  74.6 3.8 %collective-permute-done.20 = f32[1,128,256]{2,1,0:T(8,128)S(1)} collective-permute-done((f32[1,128,256]{2,1,0:T(8,128)S(1)}, f32[1,128,256]{2,1,0:T(8,128)S(1)}, u32[]{:S(2)}, u32[]{:S(2)}) %collective-permute-start.20) | collective-permute-done | bytes 131104 | tf_op jit(solution)/shard_map/ppermute | solution.py:282
  78.3 6.5 %collective-permute-done.21 = f32[1,128,256]{2,1,0:T(8,128)S(1)} collective-permute-done((f32[1,128,256]{2,1,0:T(8,128)S(1)}, f32[1,128,256]{2,1,0:T(8,128)S(1)}, u32[]{:S(2)}, u32[]{:S(2)}) %collective-permute-start.21) | collective-permute-done | bytes 131104 | tf_op jit(solution)/shard_map/ppermute | solution.py:282
  85.0 2.0 %collective-permute-start.23 = (f32[2,32,128]{2,1,0:T(8,128)S(1)}, f32[2,32,128]{2,1,0:T(8,128)S(1)}, u32[]{:S(2)}, u32[]{:S(2)}) collective-permute-start(f32[2,32,128]{2,1,0:T(8,128)S(1)} %get-tuple-element.39), channel_id=1, source_target_pairs={{0,2},{1,3},{2,0},{3,1},{4,6},{5,7},{6,4},{7,5},{8,10},{9,11},{10,... | collective-permute-start | bytes 98312 | tf_op jit(solution)/shard_map/ppermute | solution.py:282
  87.0 1.5 %collective-permute-start.24 = (f32[2,32,128]{2,1,0:T(8,128)S(1)}, f32[2,32,128]{2,1,0:T(8,128)S(1)}, u32[]{:S(2)}, u32[]{:S(2)}) collective-permute-start(f32[2,32,128]{2,1,0:T(8,128)S(1)} %get-tuple-element.40), channel_id=1, source_target_pairs={{0,4},{1,5},{2,6},{3,7},{4,0},{5,1},{6,2},{7,3},{8,12},{9,13},{10,... | collective-permute-start | bytes 98312 | tf_op jit(solution)/shard_map/ppermute | solution.py:282
  88.6 0.7 collective-permute-done.23.refs_1_
  89.3 1.7 %collective-permute-done.24.refs_2_ = f32[2,32,128]{2,1,0:T(8,128)S(1)} collective-permute-done((f32[2,32,128]{2,1,0:T(8,128)S(1)}, f32[2,32,128]{2,1,0:T(8,128)S(1)}, u32[]{:S(2)}, u32[]{:S(2)}) %collective-permute-start.24) | collective-permute-done | bytes 32800 | tf_op jit(solution)/shard_map/ppermute | solution.py:282
  90.9 2.4 %collective-permute-done.25.refs_3_ = f32[2,32,128]{2,1,0:T(8,128)S(1)} collective-permute-done((f32[2,32,128]{2,1,0:T(8,128)S(1)}, f32[2,32,128]{2,1,0:T(8,128)S(1)}, u32[]{:S(2)}, u32[]{:S(2)}) %collective-permute-start.25) | collective-permute-done | bytes 32800 | tf_op jit(solution)/shard_map/ppermute | solution.py:282
  93.4 1.2 %collective-permute-done.26.refs_4_ = f32[4,32,128]{2,1,0:T(8,128)S(1)} collective-permute-done((f32[4,32,128]{2,1,0:T(8,128)S(1)}, f32[4,32,128]{2,1,0:T(8,128)S(1)}, u32[]{:S(2)}, u32[]{:S(2)}) %collective-permute-start.26) | collective-permute-done | bytes 65568 | tf_op jit(solution)/shard_map/ppermute | solution.py:282
  94.6 0.7 shard_map.104
  95.4 1.6 %shard_map.102 = (f32[128,1024]{1,0:T(8,128)}, bf16[128,512]{1,0:T(8,128)(2,1)}) custom-call(bf16[1024,512]{1,0:T(8,128)(2,1)S(1)} %copy-done.1, bf16[1024,512]{1,0:T(8,128)(2,1)S(1)} %copy-done.2, f32[8,192,128]{2,1,0:T(8,128)S(1)} %all-to-all-done.2.back), custom_call_target="tpu_custom_call" | custom-call | tf_op jit(solution)/shard_map/pallas_call | solution.py:69
  (59 shorter events, 0.7 us)
Async XLA Ops:
  0.6 8.5 %copy-start.3 = (bf16[128,1024]{1,0:T(8,128)(2,1)S(1)}, bf16[128,1024]{1,0:T(8,128)(2,1)}, u32[]{:S(2)}) copy-start(bf16[128,1024]{1,0:T(8,128)(2,1)} %hid.5) | copy-start | bytes 786436
  0.6 30.8 %copy-start.10 = (bf16[128,512]{1,0:T(8,128)(2,1)S(1)}, bf16[128,512]{1,0:T(8,128)(2,1)}, u32[]{:S(2)}) copy-start(bf16[128,512]{1,0:T(8,128)(2,1)} %gout.1) | copy-start | bytes 393220
  0.7 30.8 %copy-start.1 = (bf16[1024,512]{1,0:T(8,128)(2,1)S(1)}, bf16[1024,512]{1,0:T(8,128)(2,1)}, u32[]{:S(2)}) copy-start(bf16[1024,512]{1,0:T(8,128)(2,1)} %wq.3) | copy-start | bytes 3145732
  3.8 32.4 %copy-start = (f32[8,64,256]{2,1,0:T(8,128)S(1)}, f32[8,64,256]{2,1,0:T(8,128)}, u32[]{:S(2)}) copy-start(f32[8,64,256]{2,1,0:T(8,128)} %feats.7) | copy-start | bytes 1572868
  3.8 28.9 %all-to-all-start = ((f32[8,128,128]{2,1,0:T(8,128)}), f32[8,128,128]{2,1,0:T(8,128)S(1)}, u32[]{:S(2)}, u32[]{:S(2)}) async-start(f32[8,128,128]{2,1,0:T(8,128)} %shard_map.93), calls=%async_computation | async-start | bytes 1048576 | tf_op jit(solution)/shard_map/all_to_all | solution.py:296
  9.2 14.9 %collective-permute-start.5 = (f32[64,1024]{1,0:T(8,128)S(1)}, f32[64,1024]{1,0:T(8,128)S(1)}, u32[]{:S(2)}, u32[]{:S(2)}) collective-permute-start(f32[64,1024]{1,0:T(8,128)S(1)} %get-tuple-element.28.refs_0_), channel_id=1, source_target_pairs={{0,2},{1,3},{2,0},{3,1},{4,6},{5,7},{6,4},{7,5},{8,10},{9,11},{10,... | collective-permute-start | bytes 786440 | tf_op jit(solution)/shard_map/ppermute | solution.py:282
  11.3 13.0 %collective-permute-start.10 = (f32[64,1024]{1,0:T(8,128)S(1)}, f32[64,1024]{1,0:T(8,128)}, u32[]{:S(2)}, u32[]{:S(2)}) collective-permute-start(f32[64,1024]{1,0:T(8,128)S(1)} %get-tuple-element.29.refs_1_), channel_id=1, source_target_pairs={{0,4},{1,5},{2,6},{3,7},{4,0},{5,1},{6,2},{7,3},{8,12},{9,13},{10,... | collective-permute-start | bytes 786440 | tf_op jit(solution)/shard_map/ppermute | solution.py:282
  12.7 17.0 %collective-permute-start.9 = (f32[64,1024]{1,0:T(8,128)S(1)}, f32[64,1024]{1,0:T(8,128)S(1)}, u32[]{:S(2)}, u32[]{:S(2)}) collective-permute-start(f32[64,1024]{1,0:T(8,128)S(1)} %get-tuple-element.28.refs_0_), channel_id=1, source_target_pairs={{0,4},{1,5},{2,6},{3,7},{4,0},{5,1},{6,2},{7,3},{8,12},{9,13},{10,... | collective-permute-start | bytes 786440 | tf_op jit(solution)/shard_map/ppermute | solution.py:282
  13.3 17.4 %collective-permute-start.6 = (f32[64,1024]{1,0:T(8,128)S(1)}, f32[64,1024]{1,0:T(8,128)S(1)}, u32[]{:S(2)}, u32[]{:S(2)}) collective-permute-start(f32[64,1024]{1,0:T(8,128)S(1)} %get-tuple-element.29.refs_1_), channel_id=1, source_target_pairs={{0,2},{1,3},{2,0},{3,1},{4,6},{5,7},{6,4},{7,5},{8,10},{9,11},{10,... | collective-permute-start | bytes 786440 | tf_op jit(solution)/shard_map/ppermute | solution.py:282
  13.4 25.1 %collective-permute-start.3 = (f32[64,1024]{1,0:T(8,128)S(1)}, f32[64,1024]{1,0:T(8,128)}, u32[]{:S(2)}, u32[]{:S(2)}) collective-permute-start(f32[64,1024]{1,0:T(8,128)S(1)} %get-tuple-element.28.refs_0_), channel_id=1, source_target_pairs={{0,1},{1,0},{2,3},{3,2},{4,5},{5,4},{6,7},{7,6},{8,9},{9,8},{10,11... | collective-permute-start | bytes 786440 | tf_op jit(solution)/shard_map/ppermute | solution.py:282
  24.1 16.0 %collective-permute-start.4 = (f32[64,1024]{1,0:T(8,128)S(1)}, f32[64,1024]{1,0:T(8,128)}, u32[]{:S(2)}, u32[]{:S(2)}) collective-permute-start(f32[64,1024]{1,0:T(8,128)S(1)} %get-tuple-element.29.refs_1_), channel_id=1, source_target_pairs={{0,1},{1,0},{2,3},{3,2},{4,5},{5,4},{6,7},{7,6},{8,9},{9,8},{10,11... | collective-permute-start | bytes 786440 | tf_op jit(solution)/shard_map/ppermute | solution.py:282
  24.2 16.0 %collective-permute-start.13 = (f32[64,1024]{1,0:T(8,128)S(1)}, f32[64,1024]{1,0:T(8,128)}, u32[]{:S(2)}, u32[]{:S(2)}) collective-permute-start(f32[64,1024]{1,0:T(8,128)S(1)} %collective-permute-done.5.refs_4_), channel_id=1, source_target_pairs={{0,4},{1,5},{2,6},{3,7},{4,0},{5,1},{6,2},{7,3},{8,12},{9,13},{10,... | collective-permute-start | bytes 786440 | tf_op jit(solution)/shard_map/ppermute | solution.py:282
  29.8 0.9 copy-start.6
  29.8 13.1 %collective-permute-start.14 = (f32[64,1024]{1,0:T(8,128)}, f32[64,1024]{1,0:T(8,128)}, u32[]{:S(2)}, u32[]{:S(2)}) collective-permute-start(f32[64,1024]{1,0:T(8,128)} %collective-permute-done.10.refs_9_), channel_id=1, source_target_pairs={{0,2},{1,3},{2,0},{3,1},{4,6},{5,7},{6,4},{7,5},{8,10},{9,11},{10,... | collective-permute-start | bytes 786440 | tf_op jit(solution)/shard_map/ppermute | solution.py:282
  30.7 0.7 copy-start.8
  31.4 11.7 %collective-permute-start.12 = (f32[64,1024]{1,0:T(8,128)}, f32[64,1024]{1,0:T(8,128)}, u32[]{:S(2)}, u32[]{:S(2)}) collective-permute-start(f32[64,1024]{1,0:T(8,128)} %collective-permute-done.10.refs_9_), channel_id=1, source_target_pairs={{0,1},{1,0},{2,3},{3,2},{4,5},{5,4},{6,7},{7,6},{8,9},{9,8},{10,11... | collective-permute-start | bytes 786440 | tf_op jit(solution)/shard_map/ppermute | solution.py:282
  32.7 18.5 %all-to-all-start.1 = ((f32[8,128,128]{2,1,0:T(8,128)}), f32[8,128,128]{2,1,0:T(8,128)S(1)}, u32[]{:S(2)}, u32[]{:S(2)}) async-start(f32[8,128,128]{2,1,0:T(8,128)} %shard_map.95), calls=%async_computation.1 | async-start | bytes 1048576 | tf_op jit(solution)/shard_map/all_to_all | solution.py:296
  37.5 1.0 %copy-start.4 = (f32[8,128,256]{2,1,0:T(8,128)}, f32[8,128,256]{2,1,0:T(8,128)S(1)}, u32[]{:S(2)}) copy-start(f32[8,128,256]{2,1,0:T(8,128)S(1)} %get-tuple-element.24.bfeat) | copy-start | bytes 3145732
  38.5 4.6 %collective-permute-start = (f32[72,256]{1,0:T(8,128)S(1)}, f32[72,256]{1,0:T(8,128)S(1)}, u32[]{:S(2)}, u32[]{:S(2)}) collective-permute-start(f32[72,256]{1,0:T(8,128)S(1)} %get-tuple-element.25.refs_0_), channel_id=1, source_target_pairs={{0,8},{1,9},{2,10},{3,11},{4,12},{5,13},{6,14},{7,15},{8,0},{9,1},... | collective-permute-start | bytes 221192 | tf_op jit(solution)/shard_map/ppermute | solution.py:282
  40.1 13.9 %collective-permute-start.7 = (f32[64,1024]{1,0:T(8,128)S(1)}, f32[64,1024]{1,0:T(8,128)}, u32[]{:S(2)}, u32[]{:S(2)}) collective-permute-start(f32[64,1024]{1,0:T(8,128)S(1)} %collective-permute-done.5.refs_4_), channel_id=1, source_target_pairs={{0,1},{1,0},{2,3},{3,2},{4,5},{5,4},{6,7},{7,6},{8,9},{9,8},{10,11... | collective-permute-start | bytes 786440 | tf_op jit(solution)/shard_map/ppermute | solution.py:282
  40.3 9.2 %collective-permute-start.1 = (f32[72,256]{1,0:T(8,128)S(1)}, f32[72,256]{1,0:T(8,128)S(1)}, u32[]{:S(2)}, u32[]{:S(2)}) collective-permute-start(f32[72,256]{1,0:T(8,128)S(1)} %get-tuple-element.25.refs_0_), channel_id=1, source_target_pairs={{0,16},{1,17},{2,18},{3,19},{4,20},{5,21},{6,22},{7,23},{8,24},{9,... | collective-permute-start | bytes 221192 | tf_op jit(solution)/shard_map/ppermute | solution.py:282
  42.9 7.2 %collective-permute-start.2 = (f32[72,256]{1,0:T(8,128)S(1)}, f32[72,256]{1,0:T(8,128)S(1)}, u32[]{:S(2)}, u32[]{:S(2)}) collective-permute-start(f32[72,256]{1,0:T(8,128)S(1)} %get-tuple-element.25.refs_0_), channel_id=1, source_target_pairs={{0,24},{1,25},{2,26},{3,27},{4,28},{5,29},{6,30},{7,31},{8,16},{9,... | collective-permute-start | bytes 221192 | tf_op jit(solution)/shard_map/ppermute | solution.py:282
  43.1 11.4 %collective-permute-start.11 = (f32[64,1024]{1,0:T(8,128)}, f32[64,1024]{1,0:T(8,128)}, u32[]{:S(2)}, u32[]{:S(2)}) collective-permute-start(f32[64,1024]{1,0:T(8,128)} %copy-done.6), channel_id=1, source_target_pairs={{0,1},{1,0},{2,3},{3,2},{4,5},{5,4},{6,7},{7,6},{8,9},{9,8},{10,11... | collective-permute-start | bytes 786440 | tf_op jit(solution)/shard_map/ppermute | solution.py:282
  43.1 14.1 %collective-permute-start.8 = (f32[64,1024]{1,0:T(8,128)}, f32[64,1024]{1,0:T(8,128)}, u32[]{:S(2)}, u32[]{:S(2)}) collective-permute-start(f32[64,1024]{1,0:T(8,128)} %copy-done.8), channel_id=1, source_target_pairs={{0,1},{1,0},{2,3},{3,2},{4,5},{5,4},{6,7},{7,6},{8,9},{9,8},{10,11... | collective-permute-start | bytes 786440 | tf_op jit(solution)/shard_map/ppermute | solution.py:282
  49.4 0.6 copy-start.11
  50.1 9.7 %collective-permute-start.15 = (f32[64,1024]{1,0:T(8,128)}, f32[64,1024]{1,0:T(8,128)}, u32[]{:S(2)}, u32[]{:S(2)}) collective-permute-start(f32[64,1024]{1,0:T(8,128)} %collective-permute-done.13.refs_12_), channel_id=1, source_target_pairs={{0,1},{1,0},{2,3},{3,2},{4,5},{5,4},{6,7},{7,6},{8,9},{9,8},{10,11... | collective-permute-start | bytes 786440 | tf_op jit(solution)/shard_map/ppermute | solution.py:282
  50.1 0.6 copy-start.13
  50.7 9.0 %collective-permute-start.16 = (f32[64,1024]{1,0:T(8,128)}, f32[64,1024]{1,0:T(8,128)}, u32[]{:S(2)}, u32[]{:S(2)}) collective-permute-start(f32[64,1024]{1,0:T(8,128)} %collective-permute-done.14.refs_13_), channel_id=1, source_target_pairs={{0,1},{1,0},{2,3},{3,2},{4,5},{5,4},{6,7},{7,6},{8,9},{9,8},{10,11... | collective-permute-start | bytes 786440 | tf_op jit(solution)/shard_map/ppermute | solution.py:282
  51.2 0.9 copy-start.12
  51.2 0.9 copy-start.14
  52.1 7.6 %copy-start.7 = (f32[64,1024]{1,0:T(8,128)S(1)}, f32[64,1024]{1,0:T(8,128)}, u32[]{:S(2)}) copy-start(f32[64,1024]{1,0:T(8,128)} %copy-done.6) | copy-start | bytes 786436
  52.1 7.6 %copy-start.9 = (f32[64,1024]{1,0:T(8,128)S(1)}, f32[64,1024]{1,0:T(8,128)}, u32[]{:S(2)}) copy-start(f32[64,1024]{1,0:T(8,128)} %copy-done.8) | copy-start | bytes 786436
  54.0 7.8 %collective-permute-start.17 = (f32[72,256]{1,0:T(8,128)S(1)}, f32[72,256]{1,0:T(8,128)S(1)}, u32[]{:S(2)}, u32[]{:S(2)}) collective-permute-start(f32[72,256]{1,0:T(8,128)S(1)} %get-tuple-element.30.refs_0_), channel_id=1, source_target_pairs={{0,8},{1,9},{2,10},{3,11},{4,12},{5,13},{6,14},{7,15},{8,0},{9,1},... | collective-permute-start | bytes 221192 | tf_op jit(solution)/shard_map/ppermute | solution.py:282
  54.5 8.2 %collective-permute-start.18 = (f32[72,256]{1,0:T(8,128)S(1)}, f32[72,256]{1,0:T(8,128)S(1)}, u32[]{:S(2)}, u32[]{:S(2)}) collective-permute-start(f32[72,256]{1,0:T(8,128)S(1)} %get-tuple-element.30.refs_0_), channel_id=1, source_target_pairs={{0,16},{1,17},{2,18},{3,19},{4,20},{5,21},{6,22},{7,23},{8,24},{9,... | collective-permute-start | bytes 221192 | tf_op jit(solution)/shard_map/ppermute | solution.py:282
  57.2 6.3 %collective-permute-start.19 = (f32[72,256]{1,0:T(8,128)S(1)}, f32[72,256]{1,0:T(8,128)S(1)}, u32[]{:S(2)}, u32[]{:S(2)}) collective-permute-start(f32[72,256]{1,0:T(8,128)S(1)} %get-tuple-element.30.refs_0_), channel_id=1, source_target_pairs={{0,24},{1,25},{2,26},{3,27},{4,28},{5,29},{6,30},{7,31},{8,16},{9,... | collective-permute-start | bytes 221192 | tf_op jit(solution)/shard_map/ppermute | solution.py:282
  59.7 3.8 %copy-start.5 = (f32[8,128,256]{2,1,0:T(8,128)S(1)}, f32[8,128,256]{2,1,0:T(8,128)}, u32[]{:S(2)}) copy-start(f32[8,128,256]{2,1,0:T(8,128)} %copy-done.4) | copy-start | bytes 3145732
  66.0 29.3 %copy-start.2 = (bf16[1024,512]{1,0:T(8,128)(2,1)S(1)}, bf16[1024,512]{1,0:T(8,128)(2,1)}, u32[]{:S(2)}) copy-start(bf16[1024,512]{1,0:T(8,128)(2,1)} %wk.3) | copy-start | bytes 3145732
  66.1 29.3 %all-to-all-start.2 = ((f32[8,192,128]{2,1,0:T(8,128)}), f32[8,192,128]{2,1,0:T(8,128)S(1)}, u32[]{:S(2)}, u32[]{:S(2)}) async-start(f32[8,192,128]{2,1,0:T(8,128)} %get-tuple-element.31), calls=%async_computation.2 | async-start | bytes 1572864 | tf_op jit(solution)/shard_map/all_to_all | solution.py:296
  70.2 8.1 %collective-permute-start.20 = (f32[1,128,256]{2,1,0:T(8,128)S(1)}, f32[1,128,256]{2,1,0:T(8,128)S(1)}, u32[]{:S(2)}, u32[]{:S(2)}) collective-permute-start(f32[1,128,256]{2,1,0:T(8,128)S(1)} %get-tuple-element.35), channel_id=1, source_target_pairs={{0,8},{1,9},{2,10},{3,11},{4,12},{5,13},{6,14},{7,15},{8,0},{9,1},... | collective-permute-start | bytes 393224 | tf_op jit(solution)/shard_map/ppermute | solution.py:282
  71.9 12.9 %collective-permute-start.21 = (f32[1,128,256]{2,1,0:T(8,128)S(1)}, f32[1,128,256]{2,1,0:T(8,128)S(1)}, u32[]{:S(2)}, u32[]{:S(2)}) collective-permute-start(f32[1,128,256]{2,1,0:T(8,128)S(1)} %get-tuple-element.36), channel_id=1, source_target_pairs={{0,16},{1,17},{2,18},{3,19},{4,20},{5,21},{6,22},{7,23},{8,24},{9,... | collective-permute-start | bytes 393224 | tf_op jit(solution)/shard_map/ppermute | solution.py:282
  73.5 11.4 %collective-permute-start.22 = (f32[1,128,256]{2,1,0:T(8,128)S(1)}, f32[1,128,256]{2,1,0:T(8,128)S(1)}, u32[]{:S(2)}, u32[]{:S(2)}) collective-permute-start(f32[1,128,256]{2,1,0:T(8,128)S(1)} %get-tuple-element.37), channel_id=1, source_target_pairs={{0,24},{1,25},{2,26},{3,27},{4,28},{5,29},{6,30},{7,31},{8,16},{9,... | collective-permute-start | bytes 393224 | tf_op jit(solution)/shard_map/ppermute | solution.py:282
  85.0 4.3 %collective-permute-start.23 = (f32[2,32,128]{2,1,0:T(8,128)S(1)}, f32[2,32,128]{2,1,0:T(8,128)S(1)}, u32[]{:S(2)}, u32[]{:S(2)}) collective-permute-start(f32[2,32,128]{2,1,0:T(8,128)S(1)} %get-tuple-element.39), channel_id=1, source_target_pairs={{0,2},{1,3},{2,0},{3,1},{4,6},{5,7},{6,4},{7,5},{8,10},{9,11},{10,... | collective-permute-start | bytes 98312 | tf_op jit(solution)/shard_map/ppermute | solution.py:282
  87.0 3.9 %collective-permute-start.24 = (f32[2,32,128]{2,1,0:T(8,128)S(1)}, f32[2,32,128]{2,1,0:T(8,128)S(1)}, u32[]{:S(2)}, u32[]{:S(2)}) collective-permute-start(f32[2,32,128]{2,1,0:T(8,128)S(1)} %get-tuple-element.40), channel_id=1, source_target_pairs={{0,4},{1,5},{2,6},{3,7},{4,0},{5,1},{6,2},{7,3},{8,12},{9,13},{10,... | collective-permute-start | bytes 98312 | tf_op jit(solution)/shard_map/ppermute | solution.py:282
  88.5 4.8 %collective-permute-start.25 = (f32[2,32,128]{2,1,0:T(8,128)S(1)}, f32[2,32,128]{2,1,0:T(8,128)S(1)}, u32[]{:S(2)}, u32[]{:S(2)}) collective-permute-start(f32[2,32,128]{2,1,0:T(8,128)S(1)} %get-tuple-element.41), channel_id=1, source_target_pairs={{0,6},{1,7},{2,4},{3,5},{4,2},{5,3},{6,0},{7,1},{8,14},{9,15},{10,... | collective-permute-start | bytes 98312 | tf_op jit(solution)/shard_map/ppermute | solution.py:282
  93.3 1.3 %collective-permute-start.26 = (f32[4,32,128]{2,1,0:T(8,128)S(1)}, f32[4,32,128]{2,1,0:T(8,128)S(1)}, u32[]{:S(2)}, u32[]{:S(2)}) collective-permute-start(f32[4,32,128]{2,1,0:T(8,128)S(1)} %pad_maximum_fusion), channel_id=1, source_target_pairs={{0,1},{1,0},{2,3},{3,2},{4,5},{5,4},{6,7},{7,6},{8,9},{9,8},{10,11... | collective-permute-start | bytes 196616 | tf_op jit(solution)/shard_map/ppermute | solution.py:282
where the time goes:
time: 97.5 us; the launch traced here: 97 us
  waiting for transfers between devices  38.8 us (40%)
  starting transfers between devices  37.5 us (38%)
  Pallas kernels  16.5 us (17%)
  local copies, waits for them, and re-layouts  3.32 us (3%)
    ppermute x27, waiting for transfers between devices, exchange(): return lax.ppermute(value, 'seq', [(i, i ^ mask) for i in range(seq_count)])  38.8 us
    ppermute x27, starting transfers between devices, exchange(): return lax.ppermute(value, 'seq', [(i, i ^ mask) for i in range(seq_count)])  24.5 us
    pallas_call x11, Pallas kernels, call(): pl.pallas_call(body, out_shape=held, in_specs=specs, out_specs=out_specs,...  13.4 us
    all_to_all x3, starting transfers between devices, spread(): lax.all_to_all(value, 'seq', 0, 0, axis_index_groups=groups, tiled=True)  12.9 us
    unnamed x30, local copies, waits for them, and re-layouts  3.31 us
    pallas_call x1, Pallas kernels, inner_shards(): pl.pallas_call(functools.partial(project_key, dh=dh, scale=scale), out_sh...  3.12 us
  transfers between devices with their start and end apart: 30, of which 12 were waited for; matrix products, arithmetic and copies ran while one was open for 0% of the time, Pallas kernels for 9%

commit v1 on v0

--- a/solution.py
+++ b/solution.py
@@ -39,7 +39,7 @@
 
 
 CHUNK = 2
-LIMIT = 24 << 20
+LIMIT = 12 << 20
 
 
 def chunks(ref):
@@ -83,43 +83,46 @@
         packed[h, :, dh : 2 * dh] = second[:, cols].astype(F32)
 
 
-def project_key(hid, wk, val, packed, rows, weight, value, held, sems, *, dh, scale):
-    step = 2 * dh
-    count = weight.shape[0]
+def project(hid, wk, val, wq, gout, *refs, dh, scale):
+    outs, (packed, wide_a, wide_b) = refs[:-11], refs[-11:-8]
+    rows, keys, queries, value, upstream, held, spare, sems = refs[-8:]
+    count = (sems.shape[0] - 4) // 2
+    step = keys.shape[0] // count
     loads = [
         pltpu.make_async_copy(hid, rows, sems.at[0]),
         pltpu.make_async_copy(val, value, sems.at[1]),
+        pltpu.make_async_copy(gout, upstream, sems.at[2]),
     ]
-    for i in range(count):
-        cols = wk.at[:, i * step : (i + 1) * step]
-        loads.append(pltpu.make_async_copy(cols, weight.at[i], sems.at[2 + i]))
+    cuts = [slice(i * step, (i + 1) * step) for i in range(count)]
+    for weight, kept in ((wk, keys), (wq, queries)):
+        for at in cuts:
+            loads.append(pltpu.make_async_copy(weight.at[at], kept.at[at], sems.at[len(loads)]))
     for load in loads:
         load.start()
     loads[0].wait()
+    half = wide_a.shape[0]
+    wide_a[...] = rows[0:half].astype(F32)
+    wide_b[...] = rows[half:].astype(F32)
+
+    def product(weight, first):
+        total = jnp.zeros((rows.shape[0], weight.shape[1]), F32)
+        for i, at in enumerate(cuts):
+            loads[first + i].wait()
+            total = total + dot1(rows[:, at], weight[at], NN)
+        return total * scale
+
+    key = product(keys, 3)
     loads[1].wait()
-    stores = []
-    for i in range(count):
-        loads[2 + i].wait()
-        key = dot1(rows[...], weight[i], NN) * scale
-        items = value[:, i * step : (i + 1) * step].astype(F32)
-        for j in range(2):
-            held[2 * i + j, :, 0:dh] = key[:, j * dh : (j + 1) * dh]
-            held[2 * i + j, :, dh:step] = items[:, j * dh : (j + 1) * dh]
-        at = slice(2 * i, 2 * i + 2)
-        stores.append(pltpu.make_async_copy(held.at[at], packed.at[at], sems.at[2 + count + i]))
-        stores[-1].start()
-    for store in stores:
-        store.wait()
-
-
-def project_query(hid, wq, gout, packed, *, dh, scale):
-    pack_pair(packed, dot1(hid[...], wq[...], NN) * scale, gout, dh)
-
-
-def widen(hid, wide_a, wide_b):
-    half = wide_a.shape[0]
-    wide_a[...] = hid[0:half].astype(F32)
-    wide_b[...] = hid[half:].astype(F32)
+    pack_pair(held, key, value, dh)
+    inner = inner_of(len(outs))
+    for j, out in enumerate(outs):
+        out[...] = held[inner ^ j]
+    query = product(queries, 3 + count)
+    loads[2].wait()
+    pack_pair(spare, query, upstream, dh)
+    store = pltpu.make_async_copy(spare, packed, sems.at[3 + 2 * count])
+    store.start()
+    store.wait()
 
 
 def inner_of(group):
@@ -132,24 +135,30 @@
     return jnp.exp(logits - half) * table[0].shape[1] ** (-0.5)
 
 
-def key_state(feats, mine, bfeat, state, *, dh):
+def pairs_of(refs):
+    return [jnp.concatenate([a[...], b[...]], axis=0) for a, b in zip(refs[::2], refs[1::2])]
+
+
+def key_state(feats, *refs, dh):
+    blocks, state = refs[:-1], refs[-1]
     table = split(feats[inner_of(feats.shape[0])])
     total = jnp.zeros((dh, state.shape[1]), F32)
     normal = jnp.zeros((1, state.shape[1]), F32)
-    for at in chunks(mine):
-        value = rows_of(mine, at, slice(dh, 2 * dh)).astype(BF16)
-        feat = feats_of(rows_of(mine, at, slice(0, dh)), table)
-        put(bfeat, at, feat)
-        total = total + dot2(value, split(feat), TN)
+    for rows in pairs_of(blocks):
+        feat = feats_of(rows[:, :dh], table)
+        total = total + dot2(rows[:, dh:].astype(BF16), split(feat), TN)
         normal = normal + jnp.sum(feat, axis=0, keepdims=True)
     state[0:dh] = total
     state[dh:] = jnp.broadcast_to(normal, (state.shape[0] - dh, state.shape[1]))
 
 
-def query_feats(feats, mine, afeat, *, dh):
+def both_feats(feats, mine, *refs, dh):
+    blocks, (afeat, bfeat) = refs[:-2], refs[-2:]
     table = split(feats[inner_of(feats.shape[0])])
     for at in chunks(mine):
         put(afeat, at, feats_of(rows_of(mine, at, slice(0, dh)), table))
+    for i, rows in enumerate(pairs_of(blocks)):
+        put(bfeat, slice(2 * i, 2 * i + 2), feats_of(rows[:, :dh], table))
 
 
 def query_state(mine, afeat, *refs, dh):
@@ -207,39 +216,42 @@
             rows_all[pl.ds(start + side * half, half), :] = rows
 
 
-def key_grad(feats, mine, bfeat, dq, rows_all, *refs, dh, scale, count):
-    parts, back, outs = refs[:count], refs[count], refs[count + 1 : -4]
-    left, held, sent, sems = refs[-4:]
-    group = mine.shape[0]
-    copies = []
-    table = split(feats[inner_of(feats.shape[0])])
+def key_grad(feats, bfeat, dq, rows_all, *refs, dh, scale, count):
+    parts, refs = refs[:count], refs[count:]
+    group, tok, _ = bfeat.shape
+    keys, outs = refs[:group], refs[group : 2 * group]
+    sents, (left, held) = refs[2 * group : -2], refs[-2:]
+    table = split(feats[inner_of(group)])
     summed = sum(part[...] for part in parts)
     pair = split(summed[:dh])
     normal = summed[dh : dh + 1]
-    tok = mine.shape[1]
-    for at in chunks(mine):
-        value = rows_of(mine, at, slice(dh, 2 * dh)).astype(BF16)
-        grads = dot2(value, pair, NN) + normal
-        feat = rows_of(bfeat, at)
-        dv = dot3(split(feat), pair, NT)
-        dk = row_grad(rows_of(mine, at, slice(0, dh)), feat, grads, table)
-        both = jnp.concatenate([rows_of(dq, at), dk], axis=1) * scale
-        left[at.start * tok : at.stop * tok, :] = both.astype(BF16)
-        for t in range(at.start, at.stop):
-            here = slice((t - at.start) * tok, (t - at.start + 1) * tok)
-            sent[t, 0:tok, 0:dh] = dk[here]
-            sent[t, 0:tok, dh : 2 * dh] = dv[here]
-            sent[t, tok:, 0:dh] = dq[t, 0 : tok // 2]
-            sent[t, tok:, dh : 2 * dh] = dq[t, tok // 2 :]
-        copies.append(pltpu.make_async_copy(sent.at[at], back.at[at], sems.at[len(copies)]))
-        copies[-1].start()
-    outer_index = lax.axis_index("seq") // group
-    emit_blocks(outer_index, dot1(left[...], rows_all[...], TN), held, outs)
-    for copy in copies:
-        copy.wait()
-
-
-def finish_rows(wq, wk, back, grad_hidden, grad_values, *, scale):
+    inner = inner_of(group)
+    for i, rows in enumerate(pairs_of(keys)):
+        grads = dot2(rows[:, dh:].astype(BF16), pair, NN) + normal
+        feat = rows_of(bfeat, slice(2 * i, 2 * i + 2))
+        dk = row_grad(rows[:, :dh], feat, grads, table)
+        for side in range(2):
+            j = 2 * i + side
+            here = dk[side * tok : (side + 1) * tok]
+            both = jnp.concatenate([dq[inner ^ j], here], axis=1) * scale
+            start = pl.multiple_of((inner ^ j) * tok, tok)
+            left[pl.ds(start, tok), :] = both.astype(BF16)
+            outs[j][0:tok, 0:dh] = here
+    emit_blocks(lax.axis_index("seq") // group, dot1(left[...], rows_all[...], TN), held, sents)
+    for i in range(group // 2):
+        dv = dot3(split(rows_of(bfeat, slice(2 * i, 2 * i + 2))), pair, NT)
+        for side in range(2):
+            j = 2 * i + side
+            outs[j][0:tok, dh : 2 * dh] = dv[side * tok : (side + 1) * tok]
+            outs[j][tok:, 0:dh] = dq[inner ^ j, 0 : tok // 2]
+            outs[j][tok:, dh : 2 * dh] = dq[inner ^ j, tok // 2 :]
+
+
+def finish_rows(wq, wk, *refs, scale):
+    backs, (grad_hidden, grad_values, back) = refs[:-3], refs[-3:]
+    inner = inner_of(len(backs))
+    for j, item in enumerate(backs):
+        back[inner ^ j] = item[...]
     heads, rows, lanes = back.shape
     tok, dh = rows * 2 // 3, lanes // 2
     dqs, dks = [], []
@@ -250,6 +262,17 @@
     dq = (jnp.concatenate(dqs, axis=1) * scale).astype(BF16)
     dk = (jnp.concatenate(dks, axis=1) * scale).astype(BF16)
     grad_hidden[...] = dot1(dq, wq[...], NT) + dot1(dk, wk[...], NT)
+
+
+def load_weights(wq, wk, held_q, held_k, sems):
+    copies = [
+        pltpu.make_async_copy(wq, held_q, sems.at[0]),
+        pltpu.make_async_copy(wk, held_k, sems.at[1]),
+    ]
+    for copy in copies:
+        copy.start()
+    for copy in copies:
+        copy.wait()
 
 
 def turn(*refs, count):
@@ -317,30 +340,29 @@
             return [part.reshape(part.shape[1:]) for part in parts]
 
         hbm = pl.BlockSpec(memory_space=pl.ANY)
-        packed_kv = pl.pallas_call(
-            functools.partial(project_key, dh=dh, scale=scale),
-            out_shape=pltpu.HBM((group, tok, 2 * dh), F32),
-            in_specs=[hbm] * 3,
-            out_specs=hbm,
+        vmem = pl.BlockSpec(memory_space=pltpu.VMEM)
+        entry = (hidden, key_weight, values, query_weight, grad_out)
+        *packed, packed_qg, wide_a, wide_b = pl.pallas_call(
+            functools.partial(project, dh=dh, scale=scale),
+            out_shape=[pltpu.VMEM((tok, 2 * dh), F32) for _ in range(group)]
+            + [pltpu.HBM((group, tok, 2 * dh), F32)]
+            + [pltpu.VMEM((tok // 2, width), F32) for _ in range(2)],
+            in_specs=[hbm] * 5,
+            out_specs=[vmem] * group + [hbm] + [vmem] * 2,
             scratch_shapes=[
                 pltpu.VMEM((tok, width), BF16),
-                pltpu.VMEM((group // 2, width, 2 * dh), BF16),
+                pltpu.VMEM((width, group * dh), BF16),
+                pltpu.VMEM((width, group * dh), BF16),
+                pltpu.VMEM((tok, group * dh), BF16),
                 pltpu.VMEM((tok, group * dh), BF16),
                 pltpu.VMEM((group, tok, 2 * dh), F32),
-                pltpu.SemaphoreType.DMA((2 + group,)),
+                pltpu.VMEM((group, tok, 2 * dh), F32),
+                pltpu.SemaphoreType.DMA((12,)),
             ],
             compiler_params=pltpu.CompilerParams(vmem_limit_bytes=LIMIT),
-        )(*(pltpu.with_memory_space_constraint(x, pltpu.HBM) for x in (hidden, key_weight, values)))
-        mine_kv = spread(packed_kv)
-        packed_qg = call(
-            functools.partial(project_query, dh=dh, scale=scale),
-            shape(group, tok, 2 * dh),
-            entry=(hidden, query_weight, grad_out),
-        )
+        )(*(pltpu.with_memory_space_constraint(x, pltpu.HBM) for x in entry))
+        mine_kv = [packed[0]] + [exchange(item, j) for j, item in enumerate(packed) if j]
         mine_qg = spread(packed_qg)
-        wide_a, wide_b = call(
-            widen, (shape(tok // 2, width), shape(tok // 2, width)), entry=(hidden,)
-        )
 
         bits = [1 << b for b in range(group.bit_length() - 1)]
         side_a = bits[1:] + bits[:1]
@@ -354,18 +376,18 @@
             ]
 
         halves = gather_step(halves, 0)
-        bfeat, state = call(
+        state = call(
             functools.partial(key_state, dh=dh),
-            (shape(group, tok, feats), shape(padded, feats)),
-            mine_kv, entry=(random_feats,),
+            shape(padded, feats),
+            *mine_kv, entry=(random_feats,),
         )
         states = plane_parts(state)
         for k in range(1, len(bits) - 1):
             halves = gather_step(halves, k)
-        afeat = call(
-            functools.partial(query_feats, dh=dh),
-            shape(group, tok, feats),
-            mine_qg, entry=(random_feats,),
+        afeat, bfeat = call(
+            functools.partial(both_feats, dh=dh),
+            (shape(group, tok, feats), shape(group, tok, feats)),
+            mine_qg, *mine_kv, entry=(random_feats,),
         )
         state, scaled, gstate = call(
             functools.partial(query_state, dh=dh),
@@ -381,29 +403,36 @@
         halves = gather_step(halves, len(bits) - 1) if len(bits) > 1 else halves
         blocks = [side[j] for j in range(group) for side in halves]
         rows_all = call(gather_rows, shape(group * tok, width, dtype=BF16), *blocks)
+        rows = width // seq_count
         radix = radices[0]
-        slabs = tuple(shape(outer // radix, 2 * dh, width // outer) for _ in range(radix))
-        back, *sent = call(
+        results = call(
             functools.partial(key_grad, dh=dh, scale=scale, count=len(gstates)),
-            (shape(group, tok + tok // 2, 2 * dh),) + slabs,
-            mine_kv, bfeat, dq, rows_all, *gstates, entry=(random_feats,), loose=1,
+            tuple(shape(tok + tok // 2, 2 * dh) for _ in range(group))
+            + tuple(shape(outer // radix, 2 * dh, width // outer) for _ in range(radix)),
+            bfeat, dq, rows_all, *gstates, *mine_kv, entry=(random_feats,),
             scratch=[
                 pltpu.VMEM((group * tok, 2 * dh), BF16),
                 pltpu.VMEM((outer, 2 * dh, width // outer), F32),
-                pltpu.VMEM((group, tok + tok // 2, 2 * dh), F32),
-                pltpu.SemaphoreType.DMA((group,)),
             ],
         )
+        backs, sent = list(results[:group]), list(results[group:])
         parts = reduce_rows(sent)
-        back = spread(back)
+        backs = backs[:1] + [exchange(item, j) for j, item in enumerate(backs) if j]
+        held = pl.pallas_call(
+            load_weights,
+            out_shape=[pltpu.VMEM(x.shape, BF16) for x in (query_weight, key_weight)],
+            in_specs=[hbm] * 2,
+            out_specs=[pl.BlockSpec(memory_space=pltpu.VMEM)] * 2,
+            scratch_shapes=[pltpu.SemaphoreType.DMA((2,))],
+        )(*(pltpu.with_memory_space_constraint(x, pltpu.HBM) for x in (query_weight, key_weight)))
         grad_hidden, grad_values = call(
             functools.partial(finish_rows, scale=scale),
             (shape(tok, width), shape(tok, group * dh, dtype=BF16)),
-            back, entry=(query_weight, key_weight), final=True,
+            *held, *backs, final=True,
+            scratch=[pltpu.VMEM((group, tok + tok // 2, 2 * dh), F32)],
         )
         if head_count > 1:
             grad_hidden = lax.psum(grad_hidden, "head")
-        rows = width // seq_count
         mine, *others = call(
             functools.partial(turn, count=len(parts)),
             tuple(shape(2, rows, 2 * dh) for _ in range(group // 2)),

time: 97.5 us -> 105 us (1.077)
  starting transfers between devices: 37.5 us -> 45.8 us
  waiting for transfers between devices: 38.8 us -> 37.6 us
    ppermute x27 -> x41, starting transfers between devices: 24.5 us -> 42 us  [exchange(): return lax.ppermute(value, 'seq', [(i, i ^ mask) for i in range(seq_count)])]
    all_to_all x3 -> x1, starting transfers between devices: 12.9 us -> 3.85 us  [spread(): lax.all_to_all(value, 'seq', 0, 0, axis_index_groups=groups, tiled=True)]
    pallas_call x1 -> x2, Pallas kernels: 3.12 us -> 4.96 us  [the longest x1 3.4 us: inner_shards(): pl.pallas_call(functools.partial(project, dh=dh, scale=scale), out_shape=...]
    pallas_call x11 -> x9, Pallas kernels: 13.4 us -> 12 us  [call(): pl.pallas_call(body, out_shape=held, in_specs=specs, out_specs=out_specs,...]
    ppermute x27 -> x41, waiting for transfers between devices: 38.8 us -> 37.6 us  [exchange(): return lax.ppermute(value, 'seq', [(i, i ^ mask) for i in range(seq_count)])]
    unnamed x30 -> x14, local copies, waits for them, and re-layouts: 3.31 us -> 3.74 us
  transfers between devices with their start and end apart: 30 -> 42, of which waited for: 12 -> 14; matrix products, arithmetic and copies ran while one was open for 0% -> 0% of each run, Pallas kernels for 9% -> 10%
where the time goes in v1:
time: 105 us
  starting transfers between devices  45.8 us (44%)
  waiting for transfers between devices  37.6 us (36%)
  Pallas kernels  17 us (16%)
  local copies, waits for them, and re-layouts  3.75 us (4%)
    ppermute x41, starting transfers between devices, exchange(): return lax.ppermute(value, 'seq', [(i, i ^ mask) for i in range(seq_count)])  42 us
    ppermute x41, waiting for transfers between devices, exchange(): return lax.ppermute(value, 'seq', [(i, i ^ mask) for i in range(seq_count)])  37.6 us
    pallas_call x9, Pallas kernels, call(): pl.pallas_call(body, out_shape=held, in_specs=specs, out_specs=out_specs,...  12 us
    all_to_all x1, starting transfers between devices, spread(): lax.all_to_all(value, 'seq', 0, 0, axis_index_groups=groups, tiled=True)  3.85 us
    unnamed x14, local copies, waits for them, and re-layouts  3.74 us
    pallas_call x1, Pallas kernels, inner_shards(): pl.pallas_call(functools.partial(project, dh=dh, scale=scale), out_shape=...  3.4 us
  transfers between devices with their start and end apart: 42, of which 14 were waited for; matrix products, arithmetic and copies ran while one was open for 0% of the time, Pallas kernels for 10%

profile of v1, /device:TPU:0, one launch (start us, length us, event | category | flops | bytes accessed | tf_op | source)
XLA Modules:
  0.0 104.9 jit_solution(2581909471818059939)
XLA Ops:
  0.6 3.4 %shard_map.94 = (f32[128,128]{1,0:T(8,128)S(1)}, f32[128,128]{1,0:T(8,128)S(1)}, f32[128,128]{1,0:T(8,128)S(1)}, f32[128,128]{1,0:T(8,128)S(1)}, f32[128,128]{1,...) custom-call(bf16[128,1024]{1,0:T(8,128)(2,1)} %hid.1, ...), custom_call_target="tpu_custom_call" | custom-call | tf_op jit(solution)/shard_map/pallas_call | solution.py:345
  4.6 2.6 %collective-permute-start.1 = (f32[128,128]{1,0:T(8,128)S(1)}, f32[128,128]{1,0:T(8,128)S(1)}, u32[]{:S(2)}, u32[]{:S(2)}) collective-permute-start(f32[128,128]{1,0:T(8,128)S(1)} %get-tuple-element.47), channel_id=1, source_target_pairs={{0,2},{1,3},{2,0},{3,1},{4,6},{5,7},{6,4},{7,5},{8,10},{9,11},{10,... | collective-permute-start | bytes 196616 | tf_op jit(solution)/shard_map/ppermute | solution.py:305
  7.2 1.8 %collective-permute-start.3 = (f32[128,128]{1,0:T(8,128)S(1)}, f32[128,128]{1,0:T(8,128)S(1)}, u32[]{:S(2)}, u32[]{:S(2)}) collective-permute-start(f32[128,128]{1,0:T(8,128)S(1)} %get-tuple-element.49), channel_id=1, source_target_pairs={{0,4},{1,5},{2,6},{3,7},{4,0},{5,1},{6,2},{7,3},{8,12},{9,13},{10,... | collective-permute-start | bytes 196616 | tf_op jit(solution)/shard_map/ppermute | solution.py:305
  9.0 2.6 %collective-permute-start.5 = (f32[128,128]{1,0:T(8,128)S(1)}, f32[128,128]{1,0:T(8,128)S(1)}, u32[]{:S(2)}, u32[]{:S(2)}) collective-permute-start(f32[128,128]{1,0:T(8,128)S(1)} %get-tuple-element.51), channel_id=1, source_target_pairs={{0,6},{1,7},{2,4},{3,5},{4,2},{5,3},{6,0},{7,1},{8,14},{9,15},{10,... | collective-permute-start | bytes 196616 | tf_op jit(solution)/shard_map/ppermute | solution.py:305
  11.7 1.6 %collective-permute-start.12 = (f32[64,1024]{1,0:T(8,128)S(1)}, f32[64,1024]{1,0:T(8,128)S(1)}, u32[]{:S(2)}, u32[]{:S(2)}) collective-permute-start(f32[64,1024]{1,0:T(8,128)S(1)} %get-tuple-element.57.refs_0_), channel_id=1, source_target_pairs={{0,2},{1,3},{2,0},{3,1},{4,6},{5,7},{6,4},{7,5},{8,10},{9,11},{10,... | collective-permute-start | bytes 786440 | tf_op jit(solution)/shard_map/ppermute | solution.py:305
  13.3 1.5 %collective-permute-start.17 = (f32[64,1024]{1,0:T(8,128)S(1)}, f32[64,1024]{1,0:T(8,128)S(1)}, u32[]{:S(2)}, u32[]{:S(2)}) collective-permute-start(f32[64,1024]{1,0:T(8,128)S(1)} %get-tuple-element.58.refs_1_), channel_id=1, source_target_pairs={{0,4},{1,5},{2,6},{3,7},{4,0},{5,1},{6,2},{7,3},{8,12},{9,13},{10,... | collective-permute-start | bytes 786440 | tf_op jit(solution)/shard_map/ppermute | solution.py:305
  14.9 1.8 %collective-permute-done.6.refs_7_.refs_11_ = f32[128,128]{1,0:T(8,128)S(1)} collective-permute-done((f32[128,128]{1,0:T(8,128)S(1)}, f32[128,128]{1,0:T(8,128)S(1)}, u32[]{:S(2)}, u32[]{:S(2)}) %collective-permute-start.6) | collective-permute-done | bytes 65568 | tf_op jit(solution)/shard_map/ppermute | solution.py:305
  16.6 1.3 %shard_map.96.refs_0_ = f32[72,256]{1,0:T(8,128)S(1)} custom-call(f32[8,64,256]{2,1,0:T(8,128)S(1)} %copy-done, f32[128,128]{1,0:T(8,128)S(1)} %get-tuple-element.45.refs_0_.refs_4_, f32[128,128]{1,0:T(8,128)S(1)} %collective-permute-done.refs_1_.refs_5_, f32[128,128]{1,0:T(8,128)S(1)} %collective-permute-done.1.refs_2_.refs_6_, ...), custom_call_target="tpu_custom_call" | custom-call | tf_op jit(solution)/shard_map/pallas_call | solution.py:69
  18.0 1.7 %collective-permute-start.7 = (f32[72,256]{1,0:T(8,128)S(1)}, f32[72,256]{1,0:T(8,128)S(1)}, u32[]{:S(2)}, u32[]{:S(2)}) collective-permute-start(f32[72,256]{1,0:T(8,128)S(1)} %shard_map.96.refs_0_), channel_id=1, source_target_pairs={{0,8},{1,9},{2,10},{3,11},{4,12},{5,13},{6,14},{7,15},{8,0},{9,1},... | collective-permute-start | bytes 221192 | tf_op jit(solution)/shard_map/ppermute | solution.py:305
  20.1 1.9 %collective-permute-start.16 = (f32[64,1024]{1,0:T(8,128)S(1)}, f32[64,1024]{1,0:T(8,128)S(1)}, u32[]{:S(2)}, u32[]{:S(2)}) collective-permute-start(f32[64,1024]{1,0:T(8,128)S(1)} %get-tuple-element.57.refs_0_), channel_id=1, source_target_pairs={{0,4},{1,5},{2,6},{3,7},{4,0},{5,1},{6,2},{7,3},{8,12},{9,13},{10,... | collective-permute-start | bytes 786440 | tf_op jit(solution)/shard_map/ppermute | solution.py:305
  22.0 0.7 collective-permute-done.7.refs_1_
  22.6 2.6 %collective-permute-start.8 = (f32[72,256]{1,0:T(8,128)S(1)}, f32[72,256]{1,0:T(8,128)S(1)}, u32[]{:S(2)}, u32[]{:S(2)}) collective-permute-start(f32[72,256]{1,0:T(8,128)S(1)} %shard_map.96.refs_0_), channel_id=1, source_target_pairs={{0,16},{1,17},{2,18},{3,19},{4,20},{5,21},{6,22},{7,23},{8,24},{9,... | collective-permute-start | bytes 221192 | tf_op jit(solution)/shard_map/ppermute | solution.py:305
  25.2 3.9 %collective-permute-done.8.refs_2_ = f32[72,256]{1,0:T(8,128)S(1)} collective-permute-done((f32[72,256]{1,0:T(8,128)S(1)}, f32[72,256]{1,0:T(8,128)S(1)}, u32[]{:S(2)}, u32[]{:S(2)}) %collective-permute-start.8) | collective-permute-done | bytes 73760 | tf_op jit(solution)/shard_map/ppermute | solution.py:305
  29.1 0.6 copy-done.3
  29.7 3.3 %collective-permute-start.9 = (f32[72,256]{1,0:T(8,128)S(1)}, f32[72,256]{1,0:T(8,128)S(1)}, u32[]{:S(2)}, u32[]{:S(2)}) collective-permute-start(f32[72,256]{1,0:T(8,128)S(1)} %shard_map.96.refs_0_), channel_id=1, source_target_pairs={{0,24},{1,25},{2,26},{3,27},{4,28},{5,29},{6,30},{7,31},{8,16},{9,... | collective-permute-start | bytes 221192 | tf_op jit(solution)/shard_map/ppermute | solution.py:305
  33.0 2.9 %collective-permute-done.9.refs_3_ = f32[72,256]{1,0:T(8,128)S(1)} collective-permute-done((f32[72,256]{1,0:T(8,128)S(1)}, f32[72,256]{1,0:T(8,128)S(1)}, u32[]{:S(2)}, u32[]{:S(2)}) %collective-permute-start.9) | collective-permute-done | bytes 73760 | tf_op jit(solution)/shard_map/ppermute | solution.py:305
  35.9 0.6 copy-done.5
  37.0 3.8 %all-to-all-start = ((f32[8,128,128]{2,1,0:T(8,128)}), f32[8,128,128]{2,1,0:T(8,128)S(1)}, u32[]{:S(2)}, u32[]{:S(2)}) async-start(f32[8,128,128]{2,1,0:T(8,128)} %get-tuple-element.44), calls=%async_computation | async-start | bytes 1048576 | tf_op jit(solution)/shard_map/all_to_all | solution.py:319
  40.9 2.0 %collective-permute-start.21 = (f32[64,1024]{1,0:T(8,128)S(1)}, f32[64,1024]{1,0:T(8,128)}, u32[]{:S(2)}, u32[]{:S(2)}) collective-permute-start(f32[64,1024]{1,0:T(8,128)S(1)} %collective-permute-done.17.refs_9_), channel_id=1, source_target_pairs={{0,2},{1,3},{2,0},{3,1},{4,6},{5,7},{6,4},{7,5},{8,10},{9,11},{10,... | collective-permute-start | bytes 786440 | tf_op jit(solution)/shard_map/ppermute | solution.py:305
  43.5 3.2 %collective-permute-done.20.refs_12_ = f32[64,1024]{1,0:T(8,128)} collective-permute-done((f32[64,1024]{1,0:T(8,128)S(1)}, f32[64,1024]{1,0:T(8,128)}, u32[]{:S(2)}, u32[]{:S(2)}) %collective-permute-start.20) | collective-permute-done | bytes 262176 | tf_op jit(solution)/shard_map/ppermute | solution.py:305
  46.7 8.7 %collective-permute-done.21.refs_13_ = f32[64,1024]{1,0:T(8,128)} collective-permute-done((f32[64,1024]{1,0:T(8,128)S(1)}, f32[64,1024]{1,0:T(8,128)}, u32[]{:S(2)}, u32[]{:S(2)}) %collective-permute-start.21) | collective-permute-done | bytes 262176 | tf_op jit(solution)/shard_map/ppermute | solution.py:305
  55.4 0.7 copy-done.1
  56.6 1.0 shard_map.95
  57.7 0.9 copy-done.4
  58.6 0.9 copy-done.6
  59.4 1.9 %shard_map.97 = (f32[72,256]{1,0:T(8,128)S(1)}, f32[8,128,72]{2,1,0:T(8,128)S(1)}, f32[72,256]{1,0:T(8,128)S(1)}) custom-call(f32[8,128,128]{2,1,0:T(8,128)S(1)} %all-to-all-done.mine, f32[8,128,256]{2,1,0:T(8,128)S(1)} %get-tuple-element.54.afeat, f32[72,256]{1,0:T(8,128)S(1)} %shard_map.96.refs_0_, f32[72,256]{1,0:T(8,128)S(1)} %collective-permute-done.7.refs_1_, ...), custom_call_target="tpu_custom_call" | custom-call | tf_op jit(solution)/shard_map/pallas_call | solution.py:69
  61.4 3.8 %collective-permute-start.25 = (f32[72,256]{1,0:T(8,128)S(1)}, f32[72,256]{1,0:T(8,128)S(1)}, u32[]{:S(2)}, u32[]{:S(2)}) collective-permute-start(f32[72,256]{1,0:T(8,128)S(1)} %get-tuple-element.59.refs_0_), channel_id=1, source_target_pairs={{0,16},{1,17},{2,18},{3,19},{4,20},{5,21},{6,22},{7,23},{8,24},{9,... | collective-permute-start | bytes 221192 | tf_op jit(solution)/shard_map/ppermute | solution.py:305
  65.2 0.6 collective-permute-start.26
  65.8 1.2 %shard_map.98.dq = f32[8,128,64]{2,1,0:T(8,128)S(1)} custom-call(f32[8,64,256]{2,1,0:T(8,128)S(1)} %copy-done, f32[8,128,128]{2,1,0:T(8,128)S(1)} %all-to-all-done.mine, f32[8,128,256]{2,1,0:T(8,128)S(1)} %get-tuple-element.54.afeat, f32[72,256]{1,0:T(8,128)S(1)} %get-tuple-element.55.state, f32[8,128,72]{2,1,0:T(8,128)S(1)} %get-tuple-element.56.scaled), custom_call_target="tpu_custom_call" | custom-call | tf_op jit(solution)/shard_map/pallas_call | solution.py:69
  67.1 1.7 %shard_map.99.rows_all = bf16[1024,1024]{1,0:T(8,128)(2,1)S(1)} custom-call(f32[64,1024]{1,0:T(8,128)S(1)} %get-tuple-element.57.refs_0_, f32[64,1024]{1,0:T(8,128)S(1)} %get-tuple-element.58.refs_1_, f32[64,1024]{1,0:T(8,128)S(1)} %collective-permute-done.10.refs_2_, f32[64,1024]{1,0:T(8,128)} %collective-permute-done.11.refs_3_, ...), custom_call_target="tpu_custom_call" | custom-call | tf_op jit(solution)/shard_map/pallas_call | solution.py:69
  68.8 1.6 %collective-permute-done.25.refs_2_ = f32[72,256]{1,0:T(8,128)S(1)} collective-permute-done((f32[72,256]{1,0:T(8,128)S(1)}, f32[72,256]{1,0:T(8,128)S(1)}, u32[]{:S(2)}, u32[]{:S(2)}) %collective-permute-start.25) | collective-permute-done | bytes 73760 | tf_op jit(solution)/shard_map/ppermute | solution.py:305
  70.4 1.1 %collective-permute-done.26.refs_3_ = f32[72,256]{1,0:T(8,128)S(1)} collective-permute-done((f32[72,256]{1,0:T(8,128)S(1)}, f32[72,256]{1,0:T(8,128)S(1)}, u32[]{:S(2)}, u32[]{:S(2)}) %collective-permute-start.26) | collective-permute-done | bytes 73760 | tf_op jit(solution)/shard_map/ppermute | solution.py:305
  71.5 2.3 %shard_map.100 = (f32[192,128]{1,0:T(8,128)S(1)}, f32[192,128]{1,0:T(8,128)S(1)}, f32[192,128]{1,0:T(8,128)S(1)}, f32[192,128]{1,0:T(8,128)S(1)}, f32[192,128]{1...) custom-call(f32[8,64,256]{2,1,0:T(8,128)S(1)} %copy-done, ...), custom_call_target="tpu_custom_call" | custom-call | tf_op jit(solution)/shard_map/pallas_call | solution.py:69
  73.8 1.3 %collective-permute-start.34 = (f32[1,128,256]{2,1,0:T(8,128)S(1)}, f32[1,128,256]{2,1,0:T(8,128)S(1)}, u32[]{:S(2)}, u32[]{:S(2)}) collective-permute-start(f32[1,128,256]{2,1,0:T(8,128)S(1)} %get-tuple-element.71), channel_id=1, source_target_pairs={{0,8},{1,9},{2,10},{3,11},{4,12},{5,13},{6,14},{7,15},{8,0},{9,1},... | collective-permute-start | bytes 393224 | tf_op jit(solution)/shard_map/ppermute | solution.py:305
  75.0 1.7 %collective-permute-start.35 = (f32[1,128,256]{2,1,0:T(8,128)S(1)}, f32[1,128,256]{2,1,0:T(8,128)S(1)}, u32[]{:S(2)}, u32[]{:S(2)}) collective-permute-start(f32[1,128,256]{2,1,0:T(8,128)S(1)} %get-tuple-element.72), channel_id=1, source_target_pairs={{0,16},{1,17},{2,18},{3,19},{4,20},{5,21},{6,22},{7,23},{8,24},{9,... | collective-permute-start | bytes 393224 | tf_op jit(solution)/shard_map/ppermute | solution.py:305
  76.7 1.5 %collective-permute-start.36 = (f32[1,128,256]{2,1,0:T(8,128)S(1)}, f32[1,128,256]{2,1,0:T(8,128)S(1)}, u32[]{:S(2)}, u32[]{:S(2)}) collective-permute-start(f32[1,128,256]{2,1,0:T(8,128)S(1)} %get-tuple-element.73), channel_id=1, source_target_pairs={{0,24},{1,25},{2,26},{3,27},{4,28},{5,29},{6,30},{7,31},{8,16},{9,... | collective-permute-start | bytes 393224 | tf_op jit(solution)/shard_map/ppermute | solution.py:305
  78.7 1.1 %collective-permute-done.34 = f32[1,128,256]{2,1,0:T(8,128)S(1)} collective-permute-done((f32[1,128,256]{2,1,0:T(8,128)S(1)}, f32[1,128,256]{2,1,0:T(8,128)S(1)}, u32[]{:S(2)}, u32[]{:S(2)}) %collective-permute-start.34) | collective-permute-done | bytes 131104 | tf_op jit(solution)/shard_map/ppermute | solution.py:305
  79.8 6.9 %collective-permute-done.35 = f32[1,128,256]{2,1,0:T(8,128)S(1)} collective-permute-done((f32[1,128,256]{2,1,0:T(8,128)S(1)}, f32[1,128,256]{2,1,0:T(8,128)S(1)}, u32[]{:S(2)}, u32[]{:S(2)}) %collective-permute-start.35) | collective-permute-done | bytes 131104 | tf_op jit(solution)/shard_map/ppermute | solution.py:305
  87.4 1.6 %collective-permute-start.38 = (f32[2,32,128]{2,1,0:T(8,128)S(1)}, f32[2,32,128]{2,1,0:T(8,128)S(1)}, u32[]{:S(2)}, u32[]{:S(2)}) collective-permute-start(f32[2,32,128]{2,1,0:T(8,128)S(1)} %get-tuple-element.76), channel_id=1, source_target_pairs={{0,4},{1,5},{2,6},{3,7},{4,0},{5,1},{6,2},{7,3},{8,12},{9,13},{10,... | collective-permute-start | bytes 98312 | tf_op jit(solution)/shard_map/ppermute | solution.py:305
  89.0 1.5 %collective-permute-start.39 = (f32[2,32,128]{2,1,0:T(8,128)S(1)}, f32[2,32,128]{2,1,0:T(8,128)S(1)}, u32[]{:S(2)}, u32[]{:S(2)}) collective-permute-start(f32[2,32,128]{2,1,0:T(8,128)S(1)} %get-tuple-element.77), channel_id=1, source_target_pairs={{0,6},{1,7},{2,4},{3,5},{4,2},{5,3},{6,0},{7,1},{8,14},{9,15},{10,... | collective-permute-start | bytes 98312 | tf_op jit(solution)/shard_map/ppermute | solution.py:305
  91.3 1.6 %collective-permute-start.30 = (f32[192,128]{1,0:T(8,128)S(1)}, f32[192,128]{1,0:T(8,128)S(1)}, u32[]{:S(2)}, u32[]{:S(2)}) collective-permute-start(f32[192,128]{1,0:T(8,128)S(1)} %get-tuple-element.64), channel_id=1, source_target_pairs={{0,4},{1,5},{2,6},{3,7},{4,0},{5,1},{6,2},{7,3},{8,12},{9,13},{10,... | collective-permute-start | bytes 294920 | tf_op jit(solution)/shard_map/ppermute | solution.py:305
  92.9 0.9 collective-permute-done.39.refs_3_
  93.8 1.5 %collective-permute-start.32 = (f32[192,128]{1,0:T(8,128)S(1)}, f32[192,128]{1,0:T(8,128)S(1)}, u32[]{:S(2)}, u32[]{:S(2)}) collective-permute-start(f32[192,128]{1,0:T(8,128)S(1)} %get-tuple-element.66), channel_id=1, source_target_pairs={{0,6},{1,7},{2,4},{3,5},{4,2},{5,3},{6,0},{7,1},{8,14},{9,15},{10,... | collective-permute-start | bytes 294920 | tf_op jit(solution)/shard_map/ppermute | solution.py:305
  95.4 1.3 %collective-permute-start.33 = (f32[192,128]{1,0:T(8,128)S(1)}, f32[192,128]{1,0:T(8,128)S(1)}, u32[]{:S(2)}, u32[]{:S(2)}) collective-permute-start(f32[192,128]{1,0:T(8,128)S(1)} %get-tuple-element.67), channel_id=1, source_target_pairs={{0,7},{1,6},{2,5},{3,4},{4,3},{5,2},{6,1},{7,0},{8,15},{9,14},{10,... | collective-permute-start | bytes 294920 | tf_op jit(solution)/shard_map/ppermute | solution.py:305
  97.0 1.6 %shard_map.93 = (bf16[1024,512]{1,0:T(8,128)(2,1)S(1)}, bf16[1024,512]{1,0:T(8,128)(2,1)S(1)}) custom-call(bf16[1024,512]{1,0:T(8,128)(2,1)} %wq.3, bf16[1024,512]{1,0:T(8,128)(2,1)} %wk.3), custom_call_target="tpu_custom_call" | custom-call | tf_op jit(solution)/shard_map/pallas_call | solution.py:421
  98.6 3.9 %collective-permute-done.31.refs_5_ = f32[192,128]{1,0:T(8,128)S(1)} collective-permute-done((f32[192,128]{1,0:T(8,128)S(1)}, f32[192,128]{1,0:T(8,128)S(1)}, u32[]{:S(2)}, u32[]{:S(2)}) %collective-permute-start.31) | collective-permute-done | bytes 98336 | tf_op jit(solution)/shard_map/ppermute | solution.py:305
  102.5 1.7 %shard_map.101 = (f32[128,1024]{1,0:T(8,128)}, bf16[128,512]{1,0:T(8,128)(2,1)}) custom-call(bf16[1024,512]{1,0:T(8,128)(2,1)S(1)} %get-tuple-element.42.wq, bf16[1024,512]{1,0:T(8,128)(2,1)S(1)} %get-tuple-element.43.wk, f32[192,128]{1,0:T(8,128)S(1)} %get-tuple-element.60.refs_0_, f32[192,128]{1,0:T(8,128)S(1)} %collective-permute-done.27.refs_1_, ...), custom_call_target="tpu_custom_call" | custom-call | tf_op jit(solution)/shard_map/pallas_call | solution.py:69
  104.2 0.8 shard_map.103
  (66 shorter events, 5.4 us)
Async XLA Ops:
  0.6 16.0 %copy-start = (f32[8,64,256]{2,1,0:T(8,128)S(1)}, f32[8,64,256]{2,1,0:T(8,128)}, u32[]{:S(2)}) copy-start(f32[8,64,256]{2,1,0:T(8,128)} %feats.7) | copy-start | bytes 1572868
  4.0 4.9 %collective-permute-start = (f32[128,128]{1,0:T(8,128)S(1)}, f32[128,128]{1,0:T(8,128)S(1)}, u32[]{:S(2)}, u32[]{:S(2)}) collective-permute-start(f32[128,128]{1,0:T(8,128)S(1)} %get-tuple-element.46), channel_id=1, source_target_pairs={{0,1},{1,0},{2,3},{3,2},{4,5},{5,4},{6,7},{7,6},{8,9},{9,8},{10,11... | collective-permute-start | bytes 196616 | tf_op jit(solution)/shard_map/ppermute | solution.py:305
  4.6 7.0 %collective-permute-start.1 = (f32[128,128]{1,0:T(8,128)S(1)}, f32[128,128]{1,0:T(8,128)S(1)}, u32[]{:S(2)}, u32[]{:S(2)}) collective-permute-start(f32[128,128]{1,0:T(8,128)S(1)} %get-tuple-element.47), channel_id=1, source_target_pairs={{0,2},{1,3},{2,0},{3,1},{4,6},{5,7},{6,4},{7,5},{8,10},{9,11},{10,... | collective-permute-start | bytes 196616 | tf_op jit(solution)/shard_map/ppermute | solution.py:305
  7.2 4.6 %collective-permute-start.2 = (f32[128,128]{1,0:T(8,128)S(1)}, f32[128,128]{1,0:T(8,128)S(1)}, u32[]{:S(2)}, u32[]{:S(2)}) collective-permute-start(f32[128,128]{1,0:T(8,128)S(1)} %get-tuple-element.48), channel_id=1, source_target_pairs={{0,3},{1,2},{2,1},{3,0},{4,7},{5,6},{6,5},{7,4},{8,11},{9,10},{10,... | collective-permute-start | bytes 196616 | tf_op jit(solution)/shard_map/ppermute | solution.py:305
  7.2 6.2 %collective-permute-start.3 = (f32[128,128]{1,0:T(8,128)S(1)}, f32[128,128]{1,0:T(8,128)S(1)}, u32[]{:S(2)}, u32[]{:S(2)}) collective-permute-start(f32[128,128]{1,0:T(8,128)S(1)} %get-tuple-element.49), channel_id=1, source_target_pairs={{0,4},{1,5},{2,6},{3,7},{4,0},{5,1},{6,2},{7,3},{8,12},{9,13},{10,... | collective-permute-start | bytes 196616 | tf_op jit(solution)/shard_map/ppermute | solution.py:305
  9.0 5.9 %collective-permute-start.4 = (f32[128,128]{1,0:T(8,128)S(1)}, f32[128,128]{1,0:T(8,128)S(1)}, u32[]{:S(2)}, u32[]{:S(2)}) collective-permute-start(f32[128,128]{1,0:T(8,128)S(1)} %get-tuple-element.50), channel_id=1, source_target_pairs={{0,5},{1,4},{2,7},{3,6},{4,1},{5,0},{6,3},{7,2},{8,13},{9,12},{10,... | collective-permute-start | bytes 196616 | tf_op jit(solution)/shard_map/ppermute | solution.py:305
  9.0 5.9 %collective-permute-start.5 = (f32[128,128]{1,0:T(8,128)S(1)}, f32[128,128]{1,0:T(8,128)S(1)}, u32[]{:S(2)}, u32[]{:S(2)}) collective-permute-start(f32[128,128]{1,0:T(8,128)S(1)} %get-tuple-element.51), channel_id=1, source_target_pairs={{0,6},{1,7},{2,4},{3,5},{4,2},{5,3},{6,0},{7,1},{8,14},{9,15},{10,... | collective-permute-start | bytes 196616 | tf_op jit(solution)/shard_map/ppermute | solution.py:305
  11.6 5.0 %collective-permute-start.6 = (f32[128,128]{1,0:T(8,128)S(1)}, f32[128,128]{1,0:T(8,128)S(1)}, u32[]{:S(2)}, u32[]{:S(2)}) collective-permute-start(f32[128,128]{1,0:T(8,128)S(1)} %get-tuple-element.52), channel_id=1, source_target_pairs={{0,7},{1,6},{2,5},{3,4},{4,3},{5,2},{6,1},{7,0},{8,15},{9,14},{10,... | collective-permute-start | bytes 196616 | tf_op jit(solution)/shard_map/ppermute | solution.py:305
  11.7 24.8 %collective-permute-start.12 = (f32[64,1024]{1,0:T(8,128)S(1)}, f32[64,1024]{1,0:T(8,128)S(1)}, u32[]{:S(2)}, u32[]{:S(2)}) collective-permute-start(f32[64,1024]{1,0:T(8,128)S(1)} %get-tuple-element.57.refs_0_), channel_id=1, source_target_pairs={{0,2},{1,3},{2,0},{3,1},{4,6},{5,7},{6,4},{7,5},{8,10},{9,11},{10,... | collective-permute-start | bytes 786440 | tf_op jit(solution)/shard_map/ppermute | solution.py:305
  13.3 23.7 %collective-permute-start.17 = (f32[64,1024]{1,0:T(8,128)S(1)}, f32[64,1024]{1,0:T(8,128)S(1)}, u32[]{:S(2)}, u32[]{:S(2)}) collective-permute-start(f32[64,1024]{1,0:T(8,128)S(1)} %get-tuple-element.58.refs_1_), channel_id=1, source_target_pairs={{0,4},{1,5},{2,6},{3,7},{4,0},{5,1},{6,2},{7,3},{8,12},{9,13},{10,... | collective-permute-start | bytes 786440 | tf_op jit(solution)/shard_map/ppermute | solution.py:305
  18.0 4.7 %collective-permute-start.7 = (f32[72,256]{1,0:T(8,128)S(1)}, f32[72,256]{1,0:T(8,128)S(1)}, u32[]{:S(2)}, u32[]{:S(2)}) collective-permute-start(f32[72,256]{1,0:T(8,128)S(1)} %shard_map.96.refs_0_), channel_id=1, source_target_pairs={{0,8},{1,9},{2,10},{3,11},{4,12},{5,13},{6,14},{7,15},{8,0},{9,1},... | collective-permute-start | bytes 221192 | tf_op jit(solution)/shard_map/ppermute | solution.py:305
  19.6 21.2 %collective-permute-start.13 = (f32[64,1024]{1,0:T(8,128)S(1)}, f32[64,1024]{1,0:T(8,128)S(1)}, u32[]{:S(2)}, u32[]{:S(2)}) collective-permute-start(f32[64,1024]{1,0:T(8,128)S(1)} %get-tuple-element.58.refs_1_), channel_id=1, source_target_pairs={{0,2},{1,3},{2,0},{3,1},{4,6},{5,7},{6,4},{7,5},{8,10},{9,11},{10,... | collective-permute-start | bytes 786440 | tf_op jit(solution)/shard_map/ppermute | solution.py:305
  20.1 22.8 %collective-permute-start.16 = (f32[64,1024]{1,0:T(8,128)S(1)}, f32[64,1024]{1,0:T(8,128)S(1)}, u32[]{:S(2)}, u32[]{:S(2)}) collective-permute-start(f32[64,1024]{1,0:T(8,128)S(1)} %get-tuple-element.57.refs_0_), channel_id=1, source_target_pairs={{0,4},{1,5},{2,6},{3,7},{4,0},{5,1},{6,2},{7,3},{8,12},{9,13},{10,... | collective-permute-start | bytes 786440 | tf_op jit(solution)/shard_map/ppermute | solution.py:305
  22.6 6.5 %collective-permute-start.8 = (f32[72,256]{1,0:T(8,128)S(1)}, f32[72,256]{1,0:T(8,128)S(1)}, u32[]{:S(2)}, u32[]{:S(2)}) collective-permute-start(f32[72,256]{1,0:T(8,128)S(1)} %shard_map.96.refs_0_), channel_id=1, source_target_pairs={{0,16},{1,17},{2,18},{3,19},{4,20},{5,21},{6,22},{7,23},{8,24},{9,... | collective-permute-start | bytes 221192 | tf_op jit(solution)/shard_map/ppermute | solution.py:305
  29.1 0.6 copy-start.3
  29.7 6.2 %collective-permute-start.9 = (f32[72,256]{1,0:T(8,128)S(1)}, f32[72,256]{1,0:T(8,128)S(1)}, u32[]{:S(2)}, u32[]{:S(2)}) collective-permute-start(f32[72,256]{1,0:T(8,128)S(1)} %shard_map.96.refs_0_), channel_id=1, source_target_pairs={{0,24},{1,25},{2,26},{3,27},{4,28},{5,29},{6,30},{7,31},{8,16},{9,... | collective-permute-start | bytes 221192 | tf_op jit(solution)/shard_map/ppermute | solution.py:305
  36.5 6.4 %collective-permute-start.10 = (f32[64,1024]{1,0:T(8,128)S(1)}, f32[64,1024]{1,0:T(8,128)S(1)}, u32[]{:S(2)}, u32[]{:S(2)}) collective-permute-start(f32[64,1024]{1,0:T(8,128)S(1)} %get-tuple-element.57.refs_0_), channel_id=1, source_target_pairs={{0,1},{1,0},{2,3},{3,2},{4,5},{5,4},{6,7},{7,6},{8,9},{9,8},{10,11... | collective-permute-start | bytes 786440 | tf_op jit(solution)/shard_map/ppermute | solution.py:305
  36.5 6.9 %collective-permute-start.11 = (f32[64,1024]{1,0:T(8,128)S(1)}, f32[64,1024]{1,0:T(8,128)}, u32[]{:S(2)}, u32[]{:S(2)}) collective-permute-start(f32[64,1024]{1,0:T(8,128)S(1)} %get-tuple-element.58.refs_1_), channel_id=1, source_target_pairs={{0,1},{1,0},{2,3},{3,2},{4,5},{5,4},{6,7},{7,6},{8,9},{9,8},{10,11... | collective-permute-start | bytes 786440 | tf_op jit(solution)/shard_map/ppermute | solution.py:305
  37.0 9.7 %collective-permute-start.20 = (f32[64,1024]{1,0:T(8,128)S(1)}, f32[64,1024]{1,0:T(8,128)}, u32[]{:S(2)}, u32[]{:S(2)}) collective-permute-start(f32[64,1024]{1,0:T(8,128)S(1)} %collective-permute-done.12.refs_4_), channel_id=1, source_target_pairs={{0,4},{1,5},{2,6},{3,7},{4,0},{5,1},{6,2},{7,3},{8,12},{9,13},{10,... | collective-permute-start | bytes 786440 | tf_op jit(solution)/shard_map/ppermute | solution.py:305
  37.0 19.6 %all-to-all-start = ((f32[8,128,128]{2,1,0:T(8,128)}), f32[8,128,128]{2,1,0:T(8,128)S(1)}, u32[]{:S(2)}, u32[]{:S(2)}) async-start(f32[8,128,128]{2,1,0:T(8,128)} %get-tuple-element.44), calls=%async_computation | async-start | bytes 1048576 | tf_op jit(solution)/shard_map/all_to_all | solution.py:319
  40.9 14.5 %collective-permute-start.21 = (f32[64,1024]{1,0:T(8,128)S(1)}, f32[64,1024]{1,0:T(8,128)}, u32[]{:S(2)}, u32[]{:S(2)}) collective-permute-start(f32[64,1024]{1,0:T(8,128)S(1)} %collective-permute-done.17.refs_9_), channel_id=1, source_target_pairs={{0,2},{1,3},{2,0},{3,1},{4,6},{5,7},{6,4},{7,5},{8,10},{9,11},{10,... | collective-permute-start | bytes 786440 | tf_op jit(solution)/shard_map/ppermute | solution.py:305
  42.9 12.5 %collective-permute-start.14 = (f32[64,1024]{1,0:T(8,128)S(1)}, f32[64,1024]{1,0:T(8,128)S(1)}, u32[]{:S(2)}, u32[]{:S(2)}) collective-permute-start(f32[64,1024]{1,0:T(8,128)S(1)} %collective-permute-done.12.refs_4_), channel_id=1, source_target_pairs={{0,1},{1,0},{2,3},{3,2},{4,5},{5,4},{6,7},{7,6},{8,9},{9,8},{10,11... | collective-permute-start | bytes 786440 | tf_op jit(solution)/shard_map/ppermute | solution.py:305
  42.9 18.5 %collective-permute-start.19 = (f32[64,1024]{1,0:T(8,128)S(1)}, f32[64,1024]{1,0:T(8,128)}, u32[]{:S(2)}, u32[]{:S(2)}) collective-permute-start(f32[64,1024]{1,0:T(8,128)S(1)} %collective-permute-done.17.refs_9_), channel_id=1, source_target_pairs={{0,1},{1,0},{2,3},{3,2},{4,5},{5,4},{6,7},{7,6},{8,9},{9,8},{10,11... | collective-permute-start | bytes 786440 | tf_op jit(solution)/shard_map/ppermute | solution.py:305
  43.4 18.0 %collective-permute-start.15 = (f32[64,1024]{1,0:T(8,128)S(1)}, f32[64,1024]{1,0:T(8,128)}, u32[]{:S(2)}, u32[]{:S(2)}) collective-permute-start(f32[64,1024]{1,0:T(8,128)S(1)} %collective-permute-done.13.refs_5_), channel_id=1, source_target_pairs={{0,1},{1,0},{2,3},{3,2},{4,5},{5,4},{6,7},{7,6},{8,9},{9,8},{10,11... | collective-permute-start | bytes 786440 | tf_op jit(solution)/shard_map/ppermute | solution.py:305
  46.7 18.5 %collective-permute-start.18 = (f32[64,1024]{1,0:T(8,128)S(1)}, f32[64,1024]{1,0:T(8,128)}, u32[]{:S(2)}, u32[]{:S(2)}) collective-permute-start(f32[64,1024]{1,0:T(8,128)S(1)} %collective-permute-done.16.refs_8_), channel_id=1, source_target_pairs={{0,1},{1,0},{2,3},{3,2},{4,5},{5,4},{6,7},{7,6},{8,9},{9,8},{10,11... | collective-permute-start | bytes 786440 | tf_op jit(solution)/shard_map/ppermute | solution.py:305
  55.4 11.6 %collective-permute-start.22 = (f32[64,1024]{1,0:T(8,128)}, f32[64,1024]{1,0:T(8,128)}, u32[]{:S(2)}, u32[]{:S(2)}) collective-permute-start(f32[64,1024]{1,0:T(8,128)} %collective-permute-done.20.refs_12_), channel_id=1, source_target_pairs={{0,1},{1,0},{2,3},{3,2},{4,5},{5,4},{6,7},{7,6},{8,9},{9,8},{10,11... | collective-permute-start | bytes 786440 | tf_op jit(solution)/shard_map/ppermute | solution.py:305
  55.4 0.7 copy-start.1
  56.1 10.9 %collective-permute-start.23 = (f32[64,1024]{1,0:T(8,128)}, f32[64,1024]{1,0:T(8,128)}, u32[]{:S(2)}, u32[]{:S(2)}) collective-permute-start(f32[64,1024]{1,0:T(8,128)} %collective-permute-done.21.refs_13_), channel_id=1, source_target_pairs={{0,1},{1,0},{2,3},{3,2},{4,5},{5,4},{6,7},{7,6},{8,9},{9,8},{10,11... | collective-permute-start | bytes 786440 | tf_op jit(solution)/shard_map/ppermute | solution.py:305
  57.7 0.9 copy-start.4
  58.6 0.9 copy-start.6
  59.4 7.6 %copy-start.2 = (f32[64,1024]{1,0:T(8,128)S(1)}, f32[64,1024]{1,0:T(8,128)}, u32[]{:S(2)}) copy-start(f32[64,1024]{1,0:T(8,128)} %copy-done.1) | copy-start | bytes 786436
  61.4 7.4 %collective-permute-start.24 = (f32[72,256]{1,0:T(8,128)S(1)}, f32[72,256]{1,0:T(8,128)S(1)}, u32[]{:S(2)}, u32[]{:S(2)}) collective-permute-start(f32[72,256]{1,0:T(8,128)S(1)} %get-tuple-element.59.refs_0_), channel_id=1, source_target_pairs={{0,8},{1,9},{2,10},{3,11},{4,12},{5,13},{6,14},{7,15},{8,0},{9,1},... | collective-permute-start | bytes 221192 | tf_op jit(solution)/shard_map/ppermute | solution.py:305
  61.4 8.9 %collective-permute-start.25 = (f32[72,256]{1,0:T(8,128)S(1)}, f32[72,256]{1,0:T(8,128)S(1)}, u32[]{:S(2)}, u32[]{:S(2)}) collective-permute-start(f32[72,256]{1,0:T(8,128)S(1)} %get-tuple-element.59.refs_0_), channel_id=1, source_target_pairs={{0,16},{1,17},{2,18},{3,19},{4,20},{5,21},{6,22},{7,23},{8,24},{9,... | collective-permute-start | bytes 221192 | tf_op jit(solution)/shard_map/ppermute | solution.py:305
  65.2 6.3 %collective-permute-start.26 = (f32[72,256]{1,0:T(8,128)S(1)}, f32[72,256]{1,0:T(8,128)S(1)}, u32[]{:S(2)}, u32[]{:S(2)}) collective-permute-start(f32[72,256]{1,0:T(8,128)S(1)} %get-tuple-element.59.refs_0_), channel_id=1, source_target_pairs={{0,24},{1,25},{2,26},{3,27},{4,28},{5,29},{6,30},{7,31},{8,16},{9,... | collective-permute-start | bytes 221192 | tf_op jit(solution)/shard_map/ppermute | solution.py:305
  73.8 6.1 %collective-permute-start.34 = (f32[1,128,256]{2,1,0:T(8,128)S(1)}, f32[1,128,256]{2,1,0:T(8,128)S(1)}, u32[]{:S(2)}, u32[]{:S(2)}) collective-permute-start(f32[1,128,256]{2,1,0:T(8,128)S(1)} %get-tuple-element.71), channel_id=1, source_target_pairs={{0,8},{1,9},{2,10},{3,11},{4,12},{5,13},{6,14},{7,15},{8,0},{9,1},... | collective-permute-start | bytes 393224 | tf_op jit(solution)/shard_map/ppermute | solution.py:305
  75.0 11.7 %collective-permute-start.35 = (f32[1,128,256]{2,1,0:T(8,128)S(1)}, f32[1,128,256]{2,1,0:T(8,128)S(1)}, u32[]{:S(2)}, u32[]{:S(2)}) collective-permute-start(f32[1,128,256]{2,1,0:T(8,128)S(1)} %get-tuple-element.72), channel_id=1, source_target_pairs={{0,16},{1,17},{2,18},{3,19},{4,20},{5,21},{6,22},{7,23},{8,24},{9,... | collective-permute-start | bytes 393224 | tf_op jit(solution)/shard_map/ppermute | solution.py:305
  76.7 10.1 %collective-permute-start.36 = (f32[1,128,256]{2,1,0:T(8,128)S(1)}, f32[1,128,256]{2,1,0:T(8,128)S(1)}, u32[]{:S(2)}, u32[]{:S(2)}) collective-permute-start(f32[1,128,256]{2,1,0:T(8,128)S(1)} %get-tuple-element.73), channel_id=1, source_target_pairs={{0,24},{1,25},{2,26},{3,27},{4,28},{5,29},{6,30},{7,31},{8,16},{9,... | collective-permute-start | bytes 393224 | tf_op jit(solution)/shard_map/ppermute | solution.py:305
  78.2 15.6 %collective-permute-start.27 = (f32[192,128]{1,0:T(8,128)S(1)}, f32[192,128]{1,0:T(8,128)S(1)}, u32[]{:S(2)}, u32[]{:S(2)}) collective-permute-start(f32[192,128]{1,0:T(8,128)S(1)} %get-tuple-element.61), channel_id=1, source_target_pairs={{0,1},{1,0},{2,3},{3,2},{4,5},{5,4},{6,7},{7,6},{8,9},{9,8},{10,11... | collective-permute-start | bytes 294920 | tf_op jit(solution)/shard_map/ppermute | solution.py:305
  78.2 17.1 %collective-permute-start.28 = (f32[192,128]{1,0:T(8,128)S(1)}, f32[192,128]{1,0:T(8,128)S(1)}, u32[]{:S(2)}, u32[]{:S(2)}) collective-permute-start(f32[192,128]{1,0:T(8,128)S(1)} %get-tuple-element.62), channel_id=1, source_target_pairs={{0,2},{1,3},{2,0},{3,1},{4,6},{5,7},{6,4},{7,5},{8,10},{9,11},{10,... | collective-permute-start | bytes 294920 | tf_op jit(solution)/shard_map/ppermute | solution.py:305
  86.9 4.0 %collective-permute-start.37 = (f32[2,32,128]{2,1,0:T(8,128)S(1)}, f32[2,32,128]{2,1,0:T(8,128)S(1)}, u32[]{:S(2)}, u32[]{:S(2)}) collective-permute-start(f32[2,32,128]{2,1,0:T(8,128)S(1)} %get-tuple-element.75), channel_id=1, source_target_pairs={{0,2},{1,3},{2,0},{3,1},{4,6},{5,7},{6,4},{7,5},{8,10},{9,11},{10,... | collective-permute-start | bytes 98312 | tf_op jit(solution)/shard_map/ppermute | solution.py:305
  87.4 3.9 %collective-permute-start.38 = (f32[2,32,128]{2,1,0:T(8,128)S(1)}, f32[2,32,128]{2,1,0:T(8,128)S(1)}, u32[]{:S(2)}, u32[]{:S(2)}) collective-permute-start(f32[2,32,128]{2,1,0:T(8,128)S(1)} %get-tuple-element.76), channel_id=1, source_target_pairs={{0,4},{1,5},{2,6},{3,7},{4,0},{5,1},{6,2},{7,3},{8,12},{9,13},{10,... | collective-permute-start | bytes 98312 | tf_op jit(solution)/shard_map/ppermute | solution.py:305
  89.0 4.8 %collective-permute-start.39 = (f32[2,32,128]{2,1,0:T(8,128)S(1)}, f32[2,32,128]{2,1,0:T(8,128)S(1)}, u32[]{:S(2)}, u32[]{:S(2)}) collective-permute-start(f32[2,32,128]{2,1,0:T(8,128)S(1)} %get-tuple-element.77), channel_id=1, source_target_pairs={{0,6},{1,7},{2,4},{3,5},{4,2},{5,3},{6,0},{7,1},{8,14},{9,15},{10,... | collective-permute-start | bytes 98312 | tf_op jit(solution)/shard_map/ppermute | solution.py:305
  90.9 5.8 %collective-permute-start.29 = (f32[192,128]{1,0:T(8,128)S(1)}, f32[192,128]{1,0:T(8,128)S(1)}, u32[]{:S(2)}, u32[]{:S(2)}) collective-permute-start(f32[192,128]{1,0:T(8,128)S(1)} %get-tuple-element.63), channel_id=1, source_target_pairs={{0,3},{1,2},{2,1},{3,0},{4,7},{5,6},{6,5},{7,4},{8,11},{9,10},{10,... | collective-permute-start | bytes 294920 | tf_op jit(solution)/shard_map/ppermute | solution.py:305
  91.3 7.2 %collective-permute-start.30 = (f32[192,128]{1,0:T(8,128)S(1)}, f32[192,128]{1,0:T(8,128)S(1)}, u32[]{:S(2)}, u32[]{:S(2)}) collective-permute-start(f32[192,128]{1,0:T(8,128)S(1)} %get-tuple-element.64), channel_id=1, source_target_pairs={{0,4},{1,5},{2,6},{3,7},{4,0},{5,1},{6,2},{7,3},{8,12},{9,13},{10,... | collective-permute-start | bytes 294920 | tf_op jit(solution)/shard_map/ppermute | solution.py:305
  93.8 8.7 %collective-permute-start.31 = (f32[192,128]{1,0:T(8,128)S(1)}, f32[192,128]{1,0:T(8,128)S(1)}, u32[]{:S(2)}, u32[]{:S(2)}) collective-permute-start(f32[192,128]{1,0:T(8,128)S(1)} %get-tuple-element.65), channel_id=1, source_target_pairs={{0,5},{1,4},{2,7},{3,6},{4,1},{5,0},{6,3},{7,2},{8,13},{9,12},{10,... | collective-permute-start | bytes 294920 | tf_op jit(solution)/shard_map/ppermute | solution.py:305
  93.8 8.7 %collective-permute-start.32 = (f32[192,128]{1,0:T(8,128)S(1)}, f32[192,128]{1,0:T(8,128)S(1)}, u32[]{:S(2)}, u32[]{:S(2)}) collective-permute-start(f32[192,128]{1,0:T(8,128)S(1)} %get-tuple-element.66), channel_id=1, source_target_pairs={{0,6},{1,7},{2,4},{3,5},{4,2},{5,3},{6,0},{7,1},{8,14},{9,15},{10,... | collective-permute-start | bytes 294920 | tf_op jit(solution)/shard_map/ppermute | solution.py:305
  95.4 7.1 %collective-permute-start.33 = (f32[192,128]{1,0:T(8,128)S(1)}, f32[192,128]{1,0:T(8,128)S(1)}, u32[]{:S(2)}, u32[]{:S(2)}) collective-permute-start(f32[192,128]{1,0:T(8,128)S(1)} %get-tuple-element.67), channel_id=1, source_target_pairs={{0,7},{1,6},{2,5},{3,4},{4,3},{5,2},{6,1},{7,0},{8,15},{9,14},{10,... | collective-permute-start | bytes 294920 | tf_op jit(solution)/shard_map/ppermute | solution.py:305
  96.6 7.5 %collective-permute-start.40 = (f32[4,32,128]{2,1,0:T(8,128)S(1)}, f32[4,32,128]{2,1,0:T(8,128)S(1)}, u32[]{:S(2)}, u32[]{:S(2)}) collective-permute-start(f32[4,32,128]{2,1,0:T(8,128)S(1)} %pad_maximum_fusion), channel_id=1, source_target_pairs={{0,1},{1,0},{2,3},{3,2},{4,5},{5,4},{6,7},{7,6},{8,9},{9,8},{10,11... | collective-permute-start | bytes 196616 | tf_op jit(solution)/shard_map/ppermute | solution.py:305
  (1 other events, 0.6 us)

commit v2 on v1

--- a/solution.py
+++ b/solution.py
@@ -38,13 +38,7 @@
     return dot1(left, rh, dims) + dot1(left, rl, dims)
 
 
-CHUNK = 2
 LIMIT = 12 << 20
-
-
-def chunks(ref):
-    step = min(CHUNK, ref.shape[0])
-    return [slice(t, t + step) for t in range(0, ref.shape[0], step)]
 
 
 def rows_of(ref, at, lanes=slice(None)):
@@ -76,17 +70,17 @@
     )(*args)
 
 
-def pack_pair(packed, first, second, dh):
+def pack_pair(packed, first, second, dh, at):
     for h in range(packed.shape[0]):
         cols = slice(h * dh, (h + 1) * dh)
-        packed[h, :, 0:dh] = first[:, cols]
-        packed[h, :, dh : 2 * dh] = second[:, cols].astype(F32)
+        packed[h, :, at : at + dh] = first[:, cols]
+        packed[h, :, at + dh : at + 2 * dh] = second[:, cols].astype(F32)
 
 
 def project(hid, wk, val, wq, gout, *refs, dh, scale):
-    outs, (packed, wide_a, wide_b) = refs[:-11], refs[-11:-8]
-    rows, keys, queries, value, upstream, held, spare, sems = refs[-8:]
-    count = (sems.shape[0] - 4) // 2
+    outs, (wide_a, wide_b) = refs[:-9], refs[-9:-7]
+    rows, keys, queries, value, upstream, held, sems = refs[-7:]
+    count = (sems.shape[0] - 3) // 2
     step = keys.shape[0] // count
     loads = [
         pltpu.make_async_copy(hid, rows, sems.at[0]),
@@ -113,16 +107,13 @@
 
     key = product(keys, 3)
     loads[1].wait()
-    pack_pair(held, key, value, dh)
+    pack_pair(held, key, value, dh, 0)
+    query = product(queries, 3 + count)
+    loads[2].wait()
+    pack_pair(held, query, upstream, dh, 2 * dh)
     inner = inner_of(len(outs))
     for j, out in enumerate(outs):
         out[...] = held[inner ^ j]
-    query = product(queries, 3 + count)
-    loads[2].wait()
-    pack_pair(spare, query, upstream, dh)
-    store = pltpu.make_async_copy(spare, packed, sems.at[3 + 2 * count])
-    store.start()
-    store.wait()
 
 
 def inner_of(group):
@@ -146,29 +137,31 @@
     normal = jnp.zeros((1, state.shape[1]), F32)
     for rows in pairs_of(blocks):
         feat = feats_of(rows[:, :dh], table)
-        total = total + dot2(rows[:, dh:].astype(BF16), split(feat), TN)
+        total = total + dot2(rows[:, dh : 2 * dh].astype(BF16), split(feat), TN)
         normal = normal + jnp.sum(feat, axis=0, keepdims=True)
     state[0:dh] = total
     state[dh:] = jnp.broadcast_to(normal, (state.shape[0] - dh, state.shape[1]))
 
 
-def both_feats(feats, mine, *refs, dh):
+def both_feats(feats, *refs, dh):
     blocks, (afeat, bfeat) = refs[:-2], refs[-2:]
     table = split(feats[inner_of(feats.shape[0])])
-    for at in chunks(mine):
-        put(afeat, at, feats_of(rows_of(mine, at, slice(0, dh)), table))
     for i, rows in enumerate(pairs_of(blocks)):
-        put(bfeat, slice(2 * i, 2 * i + 2), feats_of(rows[:, :dh], table))
-
-
-def query_state(mine, afeat, *refs, dh):
-    parts, (state, scaled, gstate) = refs[:-3], refs[-3:]
+        at = slice(2 * i, 2 * i + 2)
+        put(afeat, at, feats_of(rows[:, 2 * dh : 3 * dh], table))
+        put(bfeat, at, feats_of(rows[:, :dh], table))
+
+
+def query_state(afeat, *refs, dh):
+    group = afeat.shape[0]
+    blocks, parts, (state, scaled, gstate) = refs[:group], refs[group:-3], refs[-3:]
     summed = sum(part[...] for part in parts)
     state[...] = summed
     pair = split(summed)
     total = jnp.zeros(gstate.shape, F32)
-    for at in chunks(mine):
-        upstream = rows_of(mine, at, slice(dh, 2 * dh))
+    for i, block in enumerate(pairs_of(blocks)):
+        at = slice(2 * i, 2 * i + 2)
+        upstream = block[:, 3 * dh :]
         feat = split(rows_of(afeat, at))
         both = dot3(feat, pair, NT)
         inv = 1.0 / both[:, dh : dh + 1]
@@ -187,12 +180,14 @@
     return back - rows * jnp.sum(weighted, axis=1, keepdims=True)
 
 
-def query_grad(feats, mine, afeat, state, scaled, out, *, dh):
+def query_grad(feats, afeat, state, scaled, *refs, dh):
+    blocks, out = refs[:-1], refs[-1]
     table = split(feats[inner_of(feats.shape[0])])
     pair = split(state[...])
-    for at in chunks(mine):
+    for i, rows in enumerate(pairs_of(blocks)):
+        at = slice(2 * i, 2 * i + 2)
         grads = dot3(split(rows_of(scaled, at)), pair, NN)
-        put(out, at, row_grad(rows_of(mine, at, slice(0, dh)), rows_of(afeat, at), grads, table))
+        put(out, at, row_grad(rows[:, 2 * dh : 3 * dh], rows_of(afeat, at), grads, table))
 
 
 def emit_blocks(outer_index, total, held, outs):
@@ -219,32 +214,36 @@
 def key_grad(feats, bfeat, dq, rows_all, *refs, dh, scale, count):
     parts, refs = refs[:count], refs[count:]
     group, tok, _ = bfeat.shape
-    keys, outs = refs[:group], refs[group : 2 * group]
-    sents, (left, held) = refs[2 * group : -2], refs[-2:]
+    keys, out, sents, (left, held) = refs[:group], refs[group], refs[group + 1 : -2], refs[-2:]
     table = split(feats[inner_of(group)])
     summed = sum(part[...] for part in parts)
     pair = split(summed[:dh])
     normal = summed[dh : dh + 1]
     inner = inner_of(group)
     for i, rows in enumerate(pairs_of(keys)):
-        grads = dot2(rows[:, dh:].astype(BF16), pair, NN) + normal
-        feat = rows_of(bfeat, slice(2 * i, 2 * i + 2))
-        dk = row_grad(rows[:, :dh], feat, grads, table)
+        at = slice(2 * i, 2 * i + 2)
+        grads = dot2(rows[:, dh : 2 * dh].astype(BF16), pair, NN) + normal
+        dk = row_grad(rows[:, :dh], rows_of(bfeat, at), grads, table)
+        put(out, at, dk)
+        both = (jnp.concatenate([rows_of(dq, at), dk], axis=1) * scale).astype(BF16)
         for side in range(2):
-            j = 2 * i + side
-            here = dk[side * tok : (side + 1) * tok]
-            both = jnp.concatenate([dq[inner ^ j], here], axis=1) * scale
-            start = pl.multiple_of((inner ^ j) * tok, tok)
-            left[pl.ds(start, tok), :] = both.astype(BF16)
-            outs[j][0:tok, 0:dh] = here
+            start = pl.multiple_of((inner ^ (2 * i + side)) * tok, tok)
+            left[pl.ds(start, tok), :] = both[side * tok : (side + 1) * tok]
     emit_blocks(lax.axis_index("seq") // group, dot1(left[...], rows_all[...], TN), held, sents)
+
+
+def back_rows(bfeat, dq, dk, *refs, dh, count):
+    parts, outs = refs[:count], refs[count:]
+    group, tok, _ = bfeat.shape
+    pair = split(sum(part[0:dh] for part in parts))
     for i in range(group // 2):
         dv = dot3(split(rows_of(bfeat, slice(2 * i, 2 * i + 2))), pair, NT)
         for side in range(2):
             j = 2 * i + side
+            outs[j][0:tok, 0:dh] = dk[j]
             outs[j][0:tok, dh : 2 * dh] = dv[side * tok : (side + 1) * tok]
-            outs[j][tok:, 0:dh] = dq[inner ^ j, 0 : tok // 2]
-            outs[j][tok:, dh : 2 * dh] = dq[inner ^ j, tok // 2 :]
+            outs[j][tok:, 0:dh] = dq[j, 0 : tok // 2]
+            outs[j][tok:, dh : 2 * dh] = dq[j, tok // 2 :]
 
 
 def finish_rows(wq, wk, *refs, scale):
@@ -312,13 +311,7 @@
         assert group & (group - 1) == 0 and width % seq_count == 0
         scale = dh ** (-0.25)
         padded = dh + 8
-        groups = [[o * group + i for i in range(group)] for o in range(outer)]
         radices = [2] * ((outer.bit_length() - 1) % 2) + [4] * ((outer.bit_length() - 1) // 2)
-
-        def spread(value):
-            return lax.all_to_all(
-                value, "seq", 0, 0, axis_index_groups=groups, tiled=True
-            )
 
         def plane_parts(value):
             parts, stride = [value], group
@@ -342,27 +335,24 @@
         hbm = pl.BlockSpec(memory_space=pl.ANY)
         vmem = pl.BlockSpec(memory_space=pltpu.VMEM)
         entry = (hidden, key_weight, values, query_weight, grad_out)
-        *packed, packed_qg, wide_a, wide_b = pl.pallas_call(
+        *packed, wide_a, wide_b = pl.pallas_call(
             functools.partial(project, dh=dh, scale=scale),
-            out_shape=[pltpu.VMEM((tok, 2 * dh), F32) for _ in range(group)]
-            + [pltpu.HBM((group, tok, 2 * dh), F32)]
+            out_shape=[pltpu.VMEM((tok, 4 * dh), F32) for _ in range(group)]
             + [pltpu.VMEM((tok // 2, width), F32) for _ in range(2)],
             in_specs=[hbm] * 5,
-            out_specs=[vmem] * group + [hbm] + [vmem] * 2,
+            out_specs=[vmem] * (group + 2),
             scratch_shapes=[
                 pltpu.VMEM((tok, width), BF16),
                 pltpu.VMEM((width, group * dh), BF16),
                 pltpu.VMEM((width, group * dh), BF16),
                 pltpu.VMEM((tok, group * dh), BF16),
                 pltpu.VMEM((tok, group * dh), BF16),
-                pltpu.VMEM((group, tok, 2 * dh), F32),
-                pltpu.VMEM((group, tok, 2 * dh), F32),
-                pltpu.SemaphoreType.DMA((12,)),
+                pltpu.VMEM((group, tok, 4 * dh), F32),
+                pltpu.SemaphoreType.DMA((11,)),
             ],
             compiler_params=pltpu.CompilerParams(vmem_limit_bytes=LIMIT),
         )(*(pltpu.with_memory_space_constraint(x, pltpu.HBM) for x in entry))
-        mine_kv = [packed[0]] + [exchange(item, j) for j, item in enumerate(packed) if j]
-        mine_qg = spread(packed_qg)
+        mine = [packed[0]] + [exchange(item, j) for j, item in enumerate(packed) if j]
 
         bits = [1 << b for b in range(group.bit_length() - 1)]
         side_a = bits[1:] + bits[:1]
@@ -379,7 +369,7 @@
         state = call(
             functools.partial(key_state, dh=dh),
             shape(padded, feats),
-            *mine_kv, entry=(random_feats,),
+            *mine, entry=(random_feats,),
         )
         states = plane_parts(state)
         for k in range(1, len(bits) - 1):
@@ -387,37 +377,41 @@
         afeat, bfeat = call(
             functools.partial(both_feats, dh=dh),
             (shape(group, tok, feats), shape(group, tok, feats)),
-            mine_qg, *mine_kv, entry=(random_feats,),
+            *mine, entry=(random_feats,),
         )
         state, scaled, gstate = call(
             functools.partial(query_state, dh=dh),
             (shape(padded, feats), shape(group, tok, padded), shape(padded, feats)),
-            mine_qg, afeat, *states,
+            afeat, *mine, *states,
         )
         gstates = plane_parts(gstate)
         dq = call(
             functools.partial(query_grad, dh=dh),
             shape(group, tok, dh),
-            mine_qg, afeat, state, scaled, entry=(random_feats,),
+            afeat, state, scaled, *mine, entry=(random_feats,),
         )
         halves = gather_step(halves, len(bits) - 1) if len(bits) > 1 else halves
         blocks = [side[j] for j in range(group) for side in halves]
         rows_all = call(gather_rows, shape(group * tok, width, dtype=BF16), *blocks)
         rows = width // seq_count
         radix = radices[0]
-        results = call(
+        dk, *sent = call(
             functools.partial(key_grad, dh=dh, scale=scale, count=len(gstates)),
-            tuple(shape(tok + tok // 2, 2 * dh) for _ in range(group))
+            (shape(group, tok, dh),)
             + tuple(shape(outer // radix, 2 * dh, width // outer) for _ in range(radix)),
-            bfeat, dq, rows_all, *gstates, *mine_kv, entry=(random_feats,),
+            bfeat, dq, rows_all, *gstates, *mine, entry=(random_feats,),
             scratch=[
                 pltpu.VMEM((group * tok, 2 * dh), BF16),
                 pltpu.VMEM((outer, 2 * dh, width // outer), F32),
             ],
         )
-        backs, sent = list(results[:group]), list(results[group:])
         parts = reduce_rows(sent)
-        backs = backs[:1] + [exchange(item, j) for j, item in enumerate(backs) if j]
+        backs = call(
+            functools.partial(back_rows, dh=dh, count=len(gstates)),
+            tuple(shape(tok + tok // 2, 2 * dh) for _ in range(group)),
+            bfeat, dq, dk, *gstates,
+        )
+        backs = [backs[0]] + [exchange(item, j) for j, item in enumerate(backs) if j]
         held = pl.pallas_call(
             load_weights,
             out_shape=[pltpu.VMEM(x.shape, BF16) for x in (query_weight, key_weight)],

time: 105 us -> 97.8 us (0.931)
  local copies, waits for them, and re-layouts: 3.75 us -> 0.01 us
  Pallas kernels: 17 us -> 14.9 us
    all_to_all x1 -> x0, starting transfers between devices: 3.85 us -> none  [spread(): lax.all_to_all(value, 'seq', 0, 0, axis_index_groups=groups, tiled=True)]
    unnamed x14 -> x2, local copies, waits for them, and re-layouts: 3.74 us -> 0.01 us
    ppermute x41, starting transfers between devices: 42 us -> 45.2 us  [exchange(): return lax.ppermute(value, 'seq', [(i, i ^ mask) for i in range(seq_count)])]
    pallas_call x9 -> x10, Pallas kernels: 12 us -> 10.7 us  [call(): pl.pallas_call(body, out_shape=held, in_specs=specs, out_specs=out_specs,...]
  transfers between devices with their start and end apart: 42 -> 41, of which waited for: 14 -> 14; matrix products, arithmetic and copies ran while one was open for 0% -> 0% of each run, Pallas kernels for 10% -> 10%
where the time goes in v2:
time: 97.8 us; the launch traced here: 97.7 us
  starting transfers between devices  45.2 us (46%)
  waiting for transfers between devices  36.7 us (38%)
  Pallas kernels  14.9 us (15%)
    ppermute x41, starting transfers between devices, exchange(): return lax.ppermute(value, 'seq', [(i, i ^ mask) for i in range(seq_count)])  45.2 us
    ppermute x41, waiting for transfers between devices, exchange(): return lax.ppermute(value, 'seq', [(i, i ^ mask) for i in range(seq_count)])  36.7 us
    pallas_call x10, Pallas kernels, call(): pl.pallas_call(body, out_shape=held, in_specs=specs, out_specs=out_specs,...  10.7 us
    pallas_call x1, Pallas kernels, inner_shards(): pl.pallas_call(functools.partial(project, dh=dh, scale=scale), out_shape=...  2.63 us
  transfers between devices with their start and end apart: 41, of which 14 were waited for; matrix products, arithmetic and copies ran while one was open for 0% of the time, Pallas kernels for 10%

profile of v2, /device:TPU:0, one launch (start us, length us, event | category | flops | bytes accessed | tf_op | source)
XLA Modules:
  0.0 97.7 jit_solution(1381400761093491414)
XLA Ops:
  0.6 2.6 %shard_map.94 = (f32[128,256]{1,0:T(8,128)S(1)}, f32[128,256]{1,0:T(8,128)S(1)}, f32[128,256]{1,0:T(8,128)S(1)}, f32[128,256]{1,0:T(8,128)S(1)}, f32[128,256]{1,...) custom-call(bf16[128,1024]{1,0:T(8,128)(2,1)} %hid.1, ...), custom_call_target="tpu_custom_call" | custom-call | tf_op jit(solution)/shard_map/pallas_call | solution.py:338
  3.3 0.6 collective-permute-start
  3.8 2.6 %collective-permute-start.1 = (f32[128,256]{1,0:T(8,128)S(1)}, f32[128,256]{1,0:T(8,128)S(1)}, u32[]{:S(2)}, u32[]{:S(2)}) collective-permute-start(f32[128,256]{1,0:T(8,128)S(1)} %get-tuple-element.46), channel_id=1, source_target_pairs={{0,2},{1,3},{2,0},{3,1},{4,6},{5,7},{6,4},{7,5},{8,10},{9,11},{10,... | collective-permute-start | bytes 393224 | tf_op jit(solution)/shard_map/ppermute | solution.py:304
  6.4 1.8 %collective-permute-start.3 = (f32[128,256]{1,0:T(8,128)S(1)}, f32[128,256]{1,0:T(8,128)S(1)}, u32[]{:S(2)}, u32[]{:S(2)}) collective-permute-start(f32[128,256]{1,0:T(8,128)S(1)} %get-tuple-element.48), channel_id=1, source_target_pairs={{0,4},{1,5},{2,6},{3,7},{4,0},{5,1},{6,2},{7,3},{8,12},{9,13},{10,... | collective-permute-start | bytes 393224 | tf_op jit(solution)/shard_map/ppermute | solution.py:304
  8.2 2.6 %collective-permute-start.5 = (f32[128,256]{1,0:T(8,128)S(1)}, f32[128,256]{1,0:T(8,128)S(1)}, u32[]{:S(2)}, u32[]{:S(2)}) collective-permute-start(f32[128,256]{1,0:T(8,128)S(1)} %get-tuple-element.50), channel_id=1, source_target_pairs={{0,6},{1,7},{2,4},{3,5},{4,2},{5,3},{6,0},{7,1},{8,14},{9,15},{10,... | collective-permute-start | bytes 393224 | tf_op jit(solution)/shard_map/ppermute | solution.py:304
  10.9 1.5 %collective-permute-start.6 = (f32[128,256]{1,0:T(8,128)S(1)}, f32[128,256]{1,0:T(8,128)S(1)}, u32[]{:S(2)}, u32[]{:S(2)}) collective-permute-start(f32[128,256]{1,0:T(8,128)S(1)} %get-tuple-element.51), channel_id=1, source_target_pairs={{0,7},{1,6},{2,5},{3,4},{4,3},{5,2},{6,1},{7,0},{8,15},{9,14},{10,... | collective-permute-start | bytes 393224 | tf_op jit(solution)/shard_map/ppermute | solution.py:304
  12.4 0.7 collective-permute-done.2.refs_3_.refs_7_
  13.1 1.4 %collective-permute-start.12 = (f32[64,1024]{1,0:T(8,128)S(1)}, f32[64,1024]{1,0:T(8,128)S(1)}, u32[]{:S(2)}, u32[]{:S(2)}) collective-permute-start(f32[64,1024]{1,0:T(8,128)S(1)} %get-tuple-element.56.refs_0_), channel_id=1, source_target_pairs={{0,2},{1,3},{2,0},{3,1},{4,6},{5,7},{6,4},{7,5},{8,10},{9,11},{10,... | collective-permute-start | bytes 786440 | tf_op jit(solution)/shard_map/ppermute | solution.py:304
  14.5 1.5 %collective-permute-start.17 = (f32[64,1024]{1,0:T(8,128)S(1)}, f32[64,1024]{1,0:T(8,128)S(1)}, u32[]{:S(2)}, u32[]{:S(2)}) collective-permute-start(f32[64,1024]{1,0:T(8,128)S(1)} %get-tuple-element.57.refs_1_), channel_id=1, source_target_pairs={{0,4},{1,5},{2,6},{3,7},{4,0},{5,1},{6,2},{7,3},{8,12},{9,13},{10,... | collective-permute-start | bytes 786440 | tf_op jit(solution)/shard_map/ppermute | solution.py:304
  16.0 4.5 %collective-permute-done.4.refs_5_.refs_9_ = f32[128,256]{1,0:T(8,128)S(1)} collective-permute-done((f32[128,256]{1,0:T(8,128)S(1)}, f32[128,256]{1,0:T(8,128)S(1)}, u32[]{:S(2)}, u32[]{:S(2)}) %collective-permute-start.4) | collective-permute-done | bytes 131104 | tf_op jit(solution)/shard_map/ppermute | solution.py:304
  20.5 1.3 %shard_map.96.refs_8_ = f32[72,256]{1,0:T(8,128)S(1)} custom-call(f32[8,64,256]{2,1,0:T(8,128)S(1)} %copy-done, f32[128,256]{1,0:T(8,128)S(1)} %get-tuple-element.44.refs_0_.refs_4_, f32[128,256]{1,0:T(8,128)S(1)} %collective-permute-done.refs_1_.refs_5_, f32[128,256]{1,0:T(8,128)S(1)} %collective-permute-done.1.refs_2_.refs_6_, ...), custom_call_target="tpu_custom_call" | custom-call | tf_op jit(solution)/shard_map/pallas_call | solution.py:63
  21.9 1.6 %collective-permute-start.7 = (f32[72,256]{1,0:T(8,128)S(1)}, f32[72,256]{1,0:T(8,128)S(1)}, u32[]{:S(2)}, u32[]{:S(2)}) collective-permute-start(f32[72,256]{1,0:T(8,128)S(1)} %shard_map.96.refs_8_), channel_id=1, source_target_pairs={{0,8},{1,9},{2,10},{3,11},{4,12},{5,13},{6,14},{7,15},{8,0},{9,1},... | collective-permute-start | bytes 221192 | tf_op jit(solution)/shard_map/ppermute | solution.py:304
  23.5 1.5 %collective-permute-start.13 = (f32[64,1024]{1,0:T(8,128)S(1)}, f32[64,1024]{1,0:T(8,128)S(1)}, u32[]{:S(2)}, u32[]{:S(2)}) collective-permute-start(f32[64,1024]{1,0:T(8,128)S(1)} %get-tuple-element.57.refs_1_), channel_id=1, source_target_pairs={{0,2},{1,3},{2,0},{3,1},{4,6},{5,7},{6,4},{7,5},{8,10},{9,11},{10,... | collective-permute-start | bytes 786440 | tf_op jit(solution)/shard_map/ppermute | solution.py:304
  25.0 1.3 %collective-permute-start.16 = (f32[64,1024]{1,0:T(8,128)S(1)}, f32[64,1024]{1,0:T(8,128)S(1)}, u32[]{:S(2)}, u32[]{:S(2)}) collective-permute-start(f32[64,1024]{1,0:T(8,128)S(1)} %get-tuple-element.56.refs_0_), channel_id=1, source_target_pairs={{0,4},{1,5},{2,6},{3,7},{4,0},{5,1},{6,2},{7,3},{8,12},{9,13},{10,... | collective-permute-start | bytes 786440 | tf_op jit(solution)/shard_map/ppermute | solution.py:304
  26.3 0.8 collective-permute-done.7.refs_9_
  27.0 2.5 %collective-permute-start.8 = (f32[72,256]{1,0:T(8,128)S(1)}, f32[72,256]{1,0:T(8,128)S(1)}, u32[]{:S(2)}, u32[]{:S(2)}) collective-permute-start(f32[72,256]{1,0:T(8,128)S(1)} %shard_map.96.refs_8_), channel_id=1, source_target_pairs={{0,16},{1,17},{2,18},{3,19},{4,20},{5,21},{6,22},{7,23},{8,24},{9,... | collective-permute-start | bytes 221192 | tf_op jit(solution)/shard_map/ppermute | solution.py:304
  29.6 4.3 %collective-permute-done.8.refs_10_ = f32[72,256]{1,0:T(8,128)S(1)} collective-permute-done((f32[72,256]{1,0:T(8,128)S(1)}, f32[72,256]{1,0:T(8,128)S(1)}, u32[]{:S(2)}, u32[]{:S(2)}) %collective-permute-start.8) | collective-permute-done | bytes 73760 | tf_op jit(solution)/shard_map/ppermute | solution.py:304
  33.8 3.4 %collective-permute-start.9 = (f32[72,256]{1,0:T(8,128)S(1)}, f32[72,256]{1,0:T(8,128)S(1)}, u32[]{:S(2)}, u32[]{:S(2)}) collective-permute-start(f32[72,256]{1,0:T(8,128)S(1)} %shard_map.96.refs_8_), channel_id=1, source_target_pairs={{0,24},{1,25},{2,26},{3,27},{4,28},{5,29},{6,30},{7,31},{8,16},{9,... | collective-permute-start | bytes 221192 | tf_op jit(solution)/shard_map/ppermute | solution.py:304
  37.2 2.8 %collective-permute-done.9.refs_11_ = f32[72,256]{1,0:T(8,128)S(1)} collective-permute-done((f32[72,256]{1,0:T(8,128)S(1)}, f32[72,256]{1,0:T(8,128)S(1)}, u32[]{:S(2)}, u32[]{:S(2)}) %collective-permute-start.9) | collective-permute-done | bytes 73760 | tf_op jit(solution)/shard_map/ppermute | solution.py:304
  40.5 1.3 %collective-permute-start.20 = (f32[64,1024]{1,0:T(8,128)S(1)}, f32[64,1024]{1,0:T(8,128)S(1)}, u32[]{:S(2)}, u32[]{:S(2)}) collective-permute-start(f32[64,1024]{1,0:T(8,128)S(1)} %collective-permute-done.12.refs_4_), channel_id=1, source_target_pairs={{0,4},{1,5},{2,6},{3,7},{4,0},{5,1},{6,2},{7,3},{8,12},{9,13},{10,... | collective-permute-start | bytes 786440 | tf_op jit(solution)/shard_map/ppermute | solution.py:304
  41.8 1.5 %collective-permute-start.21 = (f32[64,1024]{1,0:T(8,128)S(1)}, f32[64,1024]{1,0:T(8,128)S(1)}, u32[]{:S(2)}, u32[]{:S(2)}) collective-permute-start(f32[64,1024]{1,0:T(8,128)S(1)} %collective-permute-done.17.refs_9_), channel_id=1, source_target_pairs={{0,2},{1,3},{2,0},{3,1},{4,6},{5,7},{6,4},{7,5},{8,10},{9,11},{10,... | collective-permute-start | bytes 786440 | tf_op jit(solution)/shard_map/ppermute | solution.py:304
  43.9 4.9 %collective-permute-done.20.refs_12_ = f32[64,1024]{1,0:T(8,128)S(1)} collective-permute-done((f32[64,1024]{1,0:T(8,128)S(1)}, f32[64,1024]{1,0:T(8,128)S(1)}, u32[]{:S(2)}, u32[]{:S(2)}) %collective-permute-start.20) | collective-permute-done | bytes 262176 | tf_op jit(solution)/shard_map/ppermute | solution.py:304
  48.8 1.0 collective-permute-done.21.refs_13_
  50.3 1.0 %shard_map.95 = (f32[8,128,256]{2,1,0:T(8,128)S(1)}, f32[8,128,256]{2,1,0:T(8,128)S(1)}) custom-call(f32[8,64,256]{2,1,0:T(8,128)S(1)} %copy-done, f32[128,256]{1,0:T(8,128)S(1)} %get-tuple-element.44.refs_0_.refs_4_, f32[128,256]{1,0:T(8,128)S(1)} %collective-permute-done.refs_1_.refs_5_, f32[128,256]{1,0:T(8,128)S(1)} %collective-permute-done.1.refs_2_.refs_6_, ...), custom_call_target="tpu_custom_call" | custom-call | tf_op jit(solution)/shard_map/pallas_call | solution.py:63
  51.3 1.9 %shard_map.97 = (f32[72,256]{1,0:T(8,128)S(1)}, f32[8,128,72]{2,1,0:T(8,128)S(1)}, f32[72,256]{1,0:T(8,128)S(1)}) custom-call(f32[8,128,256]{2,1,0:T(8,128)S(1)} %get-tuple-element.53.afeat, f32[128,256]{1,0:T(8,128)S(1)} %get-tuple-element.44.refs_0_.refs_4_, f32[128,256]{1,0:T(8,128)S(1)} %collective-permute-done.refs_1_.refs_5_, ...), custom_call_target="tpu_custom_call" | custom-call | tf_op jit(solution)/shard_map/pallas_call | solution.py:63
  53.3 4.0 %collective-permute-start.25 = (f32[72,256]{1,0:T(8,128)S(1)}, f32[72,256]{1,0:T(8,128)S(1)}, u32[]{:S(2)}, u32[]{:S(2)}) collective-permute-start(f32[72,256]{1,0:T(8,128)S(1)} %get-tuple-element.58.refs_0_), channel_id=1, source_target_pairs={{0,16},{1,17},{2,18},{3,19},{4,20},{5,21},{6,22},{7,23},{8,24},{9,... | collective-permute-start | bytes 221192 | tf_op jit(solution)/shard_map/ppermute | solution.py:304
  57.7 1.2 %shard_map.98.dq = f32[8,128,64]{2,1,0:T(8,128)S(1)} custom-call(f32[8,64,256]{2,1,0:T(8,128)S(1)} %copy-done, f32[8,128,256]{2,1,0:T(8,128)S(1)} %get-tuple-element.53.afeat, f32[72,256]{1,0:T(8,128)S(1)} %get-tuple-element.54.state, f32[8,128,72]{2,1,0:T(8,128)S(1)} %get-tuple-element.55.scaled, f32[128,256]{1,0:T(8,128)S(1)} %get-tuple-element.44.refs_0_.refs_4_, ...), custom_call_target="tpu_custom_call" | custom-call | tf_op jit(solution)/shard_map/pallas_call | solution.py:63
  59.2 3.4 %collective-permute-done.25.refs_2_ = f32[72,256]{1,0:T(8,128)S(1)} collective-permute-done((f32[72,256]{1,0:T(8,128)S(1)}, f32[72,256]{1,0:T(8,128)S(1)}, u32[]{:S(2)}, u32[]{:S(2)}) %collective-permute-start.25) | collective-permute-done | bytes 73760 | tf_op jit(solution)/shard_map/ppermute | solution.py:304
  62.5 1.1 %collective-permute-done.26.refs_3_ = f32[72,256]{1,0:T(8,128)S(1)} collective-permute-done((f32[72,256]{1,0:T(8,128)S(1)}, f32[72,256]{1,0:T(8,128)S(1)}, u32[]{:S(2)}, u32[]{:S(2)}) %collective-permute-start.26) | collective-permute-done | bytes 73760 | tf_op jit(solution)/shard_map/ppermute | solution.py:304
  63.6 1.8 %shard_map.100 = (f32[8,128,64]{2,1,0:T(8,128)S(1)}, f32[1,128,256]{2,1,0:T(8,128)S(1)}, f32[1,128,256]{2,1,0:T(8,128)S(1)}, f32[1,128,256]{2,1,0:T(8,128)S(1)}, f32[1,128,256]{2,1,0:T(8,128)S(1)}) custom-call(f32[8,64,256]{2,1,0:T(8,128)S(1)} %copy-done, f32[8,128,256]{2,1,0:T(8,128)S(1)} %get-tuple-element.52.bfeat, f32[8,128,64]{2,1,0:T(8,128)S(1)} %shard_map.98.dq, ...), custom_call_target="tpu_custom_call" | custom-call | tf_op jit(solution)/shard_map/pallas_call | solution.py:63
  65.5 1.3 %collective-permute-start.34 = (f32[1,128,256]{2,1,0:T(8,128)S(1)}, f32[1,128,256]{2,1,0:T(8,128)S(1)}, u32[]{:S(2)}, u32[]{:S(2)}) collective-permute-start(f32[1,128,256]{2,1,0:T(8,128)S(1)} %get-tuple-element.71), channel_id=1, source_target_pairs={{0,8},{1,9},{2,10},{3,11},{4,12},{5,13},{6,14},{7,15},{8,0},{9,1},... | collective-permute-start | bytes 393224 | tf_op jit(solution)/shard_map/ppermute | solution.py:304
  66.7 1.7 %collective-permute-start.35 = (f32[1,128,256]{2,1,0:T(8,128)S(1)}, f32[1,128,256]{2,1,0:T(8,128)S(1)}, u32[]{:S(2)}, u32[]{:S(2)}) collective-permute-start(f32[1,128,256]{2,1,0:T(8,128)S(1)} %get-tuple-element.72), channel_id=1, source_target_pairs={{0,16},{1,17},{2,18},{3,19},{4,20},{5,21},{6,22},{7,23},{8,24},{9,... | collective-permute-start | bytes 393224 | tf_op jit(solution)/shard_map/ppermute | solution.py:304
  68.4 1.5 %collective-permute-start.36 = (f32[1,128,256]{2,1,0:T(8,128)S(1)}, f32[1,128,256]{2,1,0:T(8,128)S(1)}, u32[]{:S(2)}, u32[]{:S(2)}) collective-permute-start(f32[1,128,256]{2,1,0:T(8,128)S(1)} %get-tuple-element.73), channel_id=1, source_target_pairs={{0,24},{1,25},{2,26},{3,27},{4,28},{5,29},{6,30},{7,31},{8,16},{9,... | collective-permute-start | bytes 393224 | tf_op jit(solution)/shard_map/ppermute | solution.py:304
  69.9 0.6 shard_map.101
  70.6 1.6 %collective-permute-start.28 = (f32[192,128]{1,0:T(8,128)S(1)}, f32[192,128]{1,0:T(8,128)S(1)}, u32[]{:S(2)}, u32[]{:S(2)}) collective-permute-start(f32[192,128]{1,0:T(8,128)S(1)} %get-tuple-element.62), channel_id=1, source_target_pairs={{0,2},{1,3},{2,0},{3,1},{4,6},{5,7},{6,4},{7,5},{8,10},{9,11},{10,... | collective-permute-start | bytes 294920 | tf_op jit(solution)/shard_map/ppermute | solution.py:304
  72.2 6.5 %collective-permute-done.35 = f32[1,128,256]{2,1,0:T(8,128)S(1)} collective-permute-done((f32[1,128,256]{2,1,0:T(8,128)S(1)}, f32[1,128,256]{2,1,0:T(8,128)S(1)}, u32[]{:S(2)}, u32[]{:S(2)}) %collective-permute-start.35) | collective-permute-done | bytes 131104 | tf_op jit(solution)/shard_map/ppermute | solution.py:304
  78.8 1.4 %collective-permute-start.37 = (f32[2,32,128]{2,1,0:T(8,128)S(1)}, f32[2,32,128]{2,1,0:T(8,128)S(1)}, u32[]{:S(2)}, u32[]{:S(2)}) collective-permute-start(f32[2,32,128]{2,1,0:T(8,128)S(1)} %get-tuple-element.75), channel_id=1, source_target_pairs={{0,2},{1,3},{2,0},{3,1},{4,6},{5,7},{6,4},{7,5},{8,10},{9,11},{10,... | collective-permute-start | bytes 98312 | tf_op jit(solution)/shard_map/ppermute | solution.py:304
  80.2 1.1 %collective-permute-start.38 = (f32[2,32,128]{2,1,0:T(8,128)S(1)}, f32[2,32,128]{2,1,0:T(8,128)S(1)}, u32[]{:S(2)}, u32[]{:S(2)}) collective-permute-start(f32[2,32,128]{2,1,0:T(8,128)S(1)} %get-tuple-element.76), channel_id=1, source_target_pairs={{0,4},{1,5},{2,6},{3,7},{4,0},{5,1},{6,2},{7,3},{8,12},{9,13},{10,... | collective-permute-start | bytes 98312 | tf_op jit(solution)/shard_map/ppermute | solution.py:304
  81.3 1.1 %collective-permute-start.39 = (f32[2,32,128]{2,1,0:T(8,128)S(1)}, f32[2,32,128]{2,1,0:T(8,128)S(1)}, u32[]{:S(2)}, u32[]{:S(2)}) collective-permute-start(f32[2,32,128]{2,1,0:T(8,128)S(1)} %get-tuple-element.77), channel_id=1, source_target_pairs={{0,6},{1,7},{2,4},{3,5},{4,2},{5,3},{6,0},{7,1},{8,14},{9,15},{10,... | collective-permute-start | bytes 98312 | tf_op jit(solution)/shard_map/ppermute | solution.py:304
  82.8 1.3 %collective-permute-done.38.refs_2_ = f32[2,32,128]{2,1,0:T(8,128)S(1)} collective-permute-done((f32[2,32,128]{2,1,0:T(8,128)S(1)}, f32[2,32,128]{2,1,0:T(8,128)S(1)}, u32[]{:S(2)}, u32[]{:S(2)}) %collective-permute-start.38) | collective-permute-done | bytes 32800 | tf_op jit(solution)/shard_map/ppermute | solution.py:304
  84.1 1.1 %collective-permute-start.30 = (f32[192,128]{1,0:T(8,128)S(1)}, f32[192,128]{1,0:T(8,128)S(1)}, u32[]{:S(2)}, u32[]{:S(2)}) collective-permute-start(f32[192,128]{1,0:T(8,128)S(1)} %get-tuple-element.64), channel_id=1, source_target_pairs={{0,4},{1,5},{2,6},{3,7},{4,0},{5,1},{6,2},{7,3},{8,12},{9,13},{10,... | collective-permute-start | bytes 294920 | tf_op jit(solution)/shard_map/ppermute | solution.py:304
  85.2 0.9 collective-permute-done.39.refs_3_
  86.1 1.2 %collective-permute-start.32 = (f32[192,128]{1,0:T(8,128)S(1)}, f32[192,128]{1,0:T(8,128)S(1)}, u32[]{:S(2)}, u32[]{:S(2)}) collective-permute-start(f32[192,128]{1,0:T(8,128)S(1)} %get-tuple-element.66), channel_id=1, source_target_pairs={{0,6},{1,7},{2,4},{3,5},{4,2},{5,3},{6,0},{7,1},{8,14},{9,15},{10,... | collective-permute-start | bytes 294920 | tf_op jit(solution)/shard_map/ppermute | solution.py:304
  87.3 2.1 %collective-permute-start.33 = (f32[192,128]{1,0:T(8,128)S(1)}, f32[192,128]{1,0:T(8,128)S(1)}, u32[]{:S(2)}, u32[]{:S(2)}) collective-permute-start(f32[192,128]{1,0:T(8,128)S(1)} %get-tuple-element.67), channel_id=1, source_target_pairs={{0,7},{1,6},{2,5},{3,4},{4,3},{5,2},{6,1},{7,0},{8,15},{9,14},{10,... | collective-permute-start | bytes 294920 | tf_op jit(solution)/shard_map/ppermute | solution.py:304
  89.5 1.6 %shard_map.93 = (bf16[1024,512]{1,0:T(8,128)(2,1)S(1)}, bf16[1024,512]{1,0:T(8,128)(2,1)S(1)}) custom-call(bf16[1024,512]{1,0:T(8,128)(2,1)} %wq.3, bf16[1024,512]{1,0:T(8,128)(2,1)} %wk.3), custom_call_target="tpu_custom_call" | custom-call | tf_op jit(solution)/shard_map/pallas_call | solution.py:415
  91.1 4.2 %collective-permute-done.31.refs_5_ = f32[192,128]{1,0:T(8,128)S(1)} collective-permute-done((f32[192,128]{1,0:T(8,128)S(1)}, f32[192,128]{1,0:T(8,128)S(1)}, u32[]{:S(2)}, u32[]{:S(2)}) %collective-permute-start.31) | collective-permute-done | bytes 98336 | tf_op jit(solution)/shard_map/ppermute | solution.py:304
  95.2 1.7 %shard_map.102 = (f32[128,1024]{1,0:T(8,128)}, bf16[128,512]{1,0:T(8,128)(2,1)}) custom-call(bf16[1024,512]{1,0:T(8,128)(2,1)S(1)} %get-tuple-element.42.wq, bf16[1024,512]{1,0:T(8,128)(2,1)S(1)} %get-tuple-element.43.wk, f32[192,128]{1,0:T(8,128)S(1)} %get-tuple-element.60.refs_0_, f32[192,128]{1,0:T(8,128)S(1)} %collective-permute-done.27.refs_1_, ...), custom_call_target="tpu_custom_call" | custom-call | tf_op jit(solution)/shard_map/pallas_call | solution.py:63
  96.9 0.8 shard_map.104
  (53 shorter events, 3.0 us)
Async XLA Ops:
  0.6 19.9 %copy-start = (f32[8,64,256]{2,1,0:T(8,128)S(1)}, f32[8,64,256]{2,1,0:T(8,128)}, u32[]{:S(2)}) copy-start(f32[8,64,256]{2,1,0:T(8,128)} %feats.7) | copy-start | bytes 1572868
  3.3 4.9 %collective-permute-start = (f32[128,256]{1,0:T(8,128)S(1)}, f32[128,256]{1,0:T(8,128)S(1)}, u32[]{:S(2)}, u32[]{:S(2)}) collective-permute-start(f32[128,256]{1,0:T(8,128)S(1)} %get-tuple-element.45), channel_id=1, source_target_pairs={{0,1},{1,0},{2,3},{3,2},{4,5},{5,4},{6,7},{7,6},{8,9},{9,8},{10,11... | collective-permute-start | bytes 393224 | tf_op jit(solution)/shard_map/ppermute | solution.py:304
  3.8 7.0 %collective-permute-start.1 = (f32[128,256]{1,0:T(8,128)S(1)}, f32[128,256]{1,0:T(8,128)S(1)}, u32[]{:S(2)}, u32[]{:S(2)}) collective-permute-start(f32[128,256]{1,0:T(8,128)S(1)} %get-tuple-element.46), channel_id=1, source_target_pairs={{0,2},{1,3},{2,0},{3,1},{4,6},{5,7},{6,4},{7,5},{8,10},{9,11},{10,... | collective-permute-start | bytes 393224 | tf_op jit(solution)/shard_map/ppermute | solution.py:304
  6.4 6.7 %collective-permute-start.2 = (f32[128,256]{1,0:T(8,128)S(1)}, f32[128,256]{1,0:T(8,128)S(1)}, u32[]{:S(2)}, u32[]{:S(2)}) collective-permute-start(f32[128,256]{1,0:T(8,128)S(1)} %get-tuple-element.47), channel_id=1, source_target_pairs={{0,3},{1,2},{2,1},{3,0},{4,7},{5,6},{6,5},{7,4},{8,11},{9,10},{10,... | collective-permute-start | bytes 393224 | tf_op jit(solution)/shard_map/ppermute | solution.py:304
  6.4 8.1 %collective-permute-start.3 = (f32[128,256]{1,0:T(8,128)S(1)}, f32[128,256]{1,0:T(8,128)S(1)}, u32[]{:S(2)}, u32[]{:S(2)}) collective-permute-start(f32[128,256]{1,0:T(8,128)S(1)} %get-tuple-element.48), channel_id=1, source_target_pairs={{0,4},{1,5},{2,6},{3,7},{4,0},{5,1},{6,2},{7,3},{8,12},{9,13},{10,... | collective-permute-start | bytes 393224 | tf_op jit(solution)/shard_map/ppermute | solution.py:304
  8.2 12.3 %collective-permute-start.4 = (f32[128,256]{1,0:T(8,128)S(1)}, f32[128,256]{1,0:T(8,128)S(1)}, u32[]{:S(2)}, u32[]{:S(2)}) collective-permute-start(f32[128,256]{1,0:T(8,128)S(1)} %get-tuple-element.49), channel_id=1, source_target_pairs={{0,5},{1,4},{2,7},{3,6},{4,1},{5,0},{6,3},{7,2},{8,13},{9,12},{10,... | collective-permute-start | bytes 393224 | tf_op jit(solution)/shard_map/ppermute | solution.py:304
  8.2 12.3 %collective-permute-start.5 = (f32[128,256]{1,0:T(8,128)S(1)}, f32[128,256]{1,0:T(8,128)S(1)}, u32[]{:S(2)}, u32[]{:S(2)}) collective-permute-start(f32[128,256]{1,0:T(8,128)S(1)} %get-tuple-element.50), channel_id=1, source_target_pairs={{0,6},{1,7},{2,4},{3,5},{4,2},{5,3},{6,0},{7,1},{8,14},{9,15},{10,... | collective-permute-start | bytes 393224 | tf_op jit(solution)/shard_map/ppermute | solution.py:304
  10.9 9.7 %collective-permute-start.6 = (f32[128,256]{1,0:T(8,128)S(1)}, f32[128,256]{1,0:T(8,128)S(1)}, u32[]{:S(2)}, u32[]{:S(2)}) collective-permute-start(f32[128,256]{1,0:T(8,128)S(1)} %get-tuple-element.51), channel_id=1, source_target_pairs={{0,7},{1,6},{2,5},{3,4},{4,3},{5,2},{6,1},{7,0},{8,15},{9,14},{10,... | collective-permute-start | bytes 393224 | tf_op jit(solution)/shard_map/ppermute | solution.py:304
  13.1 26.9 %collective-permute-start.12 = (f32[64,1024]{1,0:T(8,128)S(1)}, f32[64,1024]{1,0:T(8,128)S(1)}, u32[]{:S(2)}, u32[]{:S(2)}) collective-permute-start(f32[64,1024]{1,0:T(8,128)S(1)} %get-tuple-element.56.refs_0_), channel_id=1, source_target_pairs={{0,2},{1,3},{2,0},{3,1},{4,6},{5,7},{6,4},{7,5},{8,10},{9,11},{10,... | collective-permute-start | bytes 786440 | tf_op jit(solution)/shard_map/ppermute | solution.py:304
  14.5 26.0 %collective-permute-start.17 = (f32[64,1024]{1,0:T(8,128)S(1)}, f32[64,1024]{1,0:T(8,128)S(1)}, u32[]{:S(2)}, u32[]{:S(2)}) collective-permute-start(f32[64,1024]{1,0:T(8,128)S(1)} %get-tuple-element.57.refs_1_), channel_id=1, source_target_pairs={{0,4},{1,5},{2,6},{3,7},{4,0},{5,1},{6,2},{7,3},{8,12},{9,13},{10,... | collective-permute-start | bytes 786440 | tf_op jit(solution)/shard_map/ppermute | solution.py:304
  21.9 5.1 %collective-permute-start.7 = (f32[72,256]{1,0:T(8,128)S(1)}, f32[72,256]{1,0:T(8,128)S(1)}, u32[]{:S(2)}, u32[]{:S(2)}) collective-permute-start(f32[72,256]{1,0:T(8,128)S(1)} %shard_map.96.refs_8_), channel_id=1, source_target_pairs={{0,8},{1,9},{2,10},{3,11},{4,12},{5,13},{6,14},{7,15},{8,0},{9,1},... | collective-permute-start | bytes 221192 | tf_op jit(solution)/shard_map/ppermute | solution.py:304
  23.5 18.3 %collective-permute-start.13 = (f32[64,1024]{1,0:T(8,128)S(1)}, f32[64,1024]{1,0:T(8,128)S(1)}, u32[]{:S(2)}, u32[]{:S(2)}) collective-permute-start(f32[64,1024]{1,0:T(8,128)S(1)} %get-tuple-element.57.refs_1_), channel_id=1, source_target_pairs={{0,2},{1,3},{2,0},{3,1},{4,6},{5,7},{6,4},{7,5},{8,10},{9,11},{10,... | collective-permute-start | bytes 786440 | tf_op jit(solution)/shard_map/ppermute | solution.py:304
  25.0 18.3 %collective-permute-start.16 = (f32[64,1024]{1,0:T(8,128)S(1)}, f32[64,1024]{1,0:T(8,128)S(1)}, u32[]{:S(2)}, u32[]{:S(2)}) collective-permute-start(f32[64,1024]{1,0:T(8,128)S(1)} %get-tuple-element.56.refs_0_), channel_id=1, source_target_pairs={{0,4},{1,5},{2,6},{3,7},{4,0},{5,1},{6,2},{7,3},{8,12},{9,13},{10,... | collective-permute-start | bytes 786440 | tf_op jit(solution)/shard_map/ppermute | solution.py:304
  27.0 6.8 %collective-permute-start.8 = (f32[72,256]{1,0:T(8,128)S(1)}, f32[72,256]{1,0:T(8,128)S(1)}, u32[]{:S(2)}, u32[]{:S(2)}) collective-permute-start(f32[72,256]{1,0:T(8,128)S(1)} %shard_map.96.refs_8_), channel_id=1, source_target_pairs={{0,16},{1,17},{2,18},{3,19},{4,20},{5,21},{6,22},{7,23},{8,24},{9,... | collective-permute-start | bytes 221192 | tf_op jit(solution)/shard_map/ppermute | solution.py:304
  33.8 6.2 %collective-permute-start.9 = (f32[72,256]{1,0:T(8,128)S(1)}, f32[72,256]{1,0:T(8,128)S(1)}, u32[]{:S(2)}, u32[]{:S(2)}) collective-permute-start(f32[72,256]{1,0:T(8,128)S(1)} %shard_map.96.refs_8_), channel_id=1, source_target_pairs={{0,24},{1,25},{2,26},{3,27},{4,28},{5,29},{6,30},{7,31},{8,16},{9,... | collective-permute-start | bytes 221192 | tf_op jit(solution)/shard_map/ppermute | solution.py:304
  40.0 3.3 %collective-permute-start.10 = (f32[64,1024]{1,0:T(8,128)S(1)}, f32[64,1024]{1,0:T(8,128)S(1)}, u32[]{:S(2)}, u32[]{:S(2)}) collective-permute-start(f32[64,1024]{1,0:T(8,128)S(1)} %get-tuple-element.56.refs_0_), channel_id=1, source_target_pairs={{0,1},{1,0},{2,3},{3,2},{4,5},{5,4},{6,7},{7,6},{8,9},{9,8},{10,11... | collective-permute-start | bytes 786440 | tf_op jit(solution)/shard_map/ppermute | solution.py:304
  40.0 3.8 %collective-permute-start.11 = (f32[64,1024]{1,0:T(8,128)S(1)}, f32[64,1024]{1,0:T(8,128)S(1)}, u32[]{:S(2)}, u32[]{:S(2)}) collective-permute-start(f32[64,1024]{1,0:T(8,128)S(1)} %get-tuple-element.57.refs_1_), channel_id=1, source_target_pairs={{0,1},{1,0},{2,3},{3,2},{4,5},{5,4},{6,7},{7,6},{8,9},{9,8},{10,11... | collective-permute-start | bytes 786440 | tf_op jit(solution)/shard_map/ppermute | solution.py:304
  40.5 8.3 %collective-permute-start.20 = (f32[64,1024]{1,0:T(8,128)S(1)}, f32[64,1024]{1,0:T(8,128)S(1)}, u32[]{:S(2)}, u32[]{:S(2)}) collective-permute-start(f32[64,1024]{1,0:T(8,128)S(1)} %collective-permute-done.12.refs_4_), channel_id=1, source_target_pairs={{0,4},{1,5},{2,6},{3,7},{4,0},{5,1},{6,2},{7,3},{8,12},{9,13},{10,... | collective-permute-start | bytes 786440 | tf_op jit(solution)/shard_map/ppermute | solution.py:304
  41.8 8.0 %collective-permute-start.21 = (f32[64,1024]{1,0:T(8,128)S(1)}, f32[64,1024]{1,0:T(8,128)S(1)}, u32[]{:S(2)}, u32[]{:S(2)}) collective-permute-start(f32[64,1024]{1,0:T(8,128)S(1)} %collective-permute-done.17.refs_9_), channel_id=1, source_target_pairs={{0,2},{1,3},{2,0},{3,1},{4,6},{5,7},{6,4},{7,5},{8,10},{9,11},{10,... | collective-permute-start | bytes 786440 | tf_op jit(solution)/shard_map/ppermute | solution.py:304
  43.3 6.5 %collective-permute-start.14 = (f32[64,1024]{1,0:T(8,128)S(1)}, f32[64,1024]{1,0:T(8,128)S(1)}, u32[]{:S(2)}, u32[]{:S(2)}) collective-permute-start(f32[64,1024]{1,0:T(8,128)S(1)} %collective-permute-done.12.refs_4_), channel_id=1, source_target_pairs={{0,1},{1,0},{2,3},{3,2},{4,5},{5,4},{6,7},{7,6},{8,9},{9,8},{10,11... | collective-permute-start | bytes 786440 | tf_op jit(solution)/shard_map/ppermute | solution.py:304
  43.3 9.9 %collective-permute-start.19 = (f32[64,1024]{1,0:T(8,128)S(1)}, f32[64,1024]{1,0:T(8,128)S(1)}, u32[]{:S(2)}, u32[]{:S(2)}) collective-permute-start(f32[64,1024]{1,0:T(8,128)S(1)} %collective-permute-done.17.refs_9_), channel_id=1, source_target_pairs={{0,1},{1,0},{2,3},{3,2},{4,5},{5,4},{6,7},{7,6},{8,9},{9,8},{10,11... | collective-permute-start | bytes 786440 | tf_op jit(solution)/shard_map/ppermute | solution.py:304
  43.8 9.5 %collective-permute-start.15 = (f32[64,1024]{1,0:T(8,128)S(1)}, f32[64,1024]{1,0:T(8,128)S(1)}, u32[]{:S(2)}, u32[]{:S(2)}) collective-permute-start(f32[64,1024]{1,0:T(8,128)S(1)} %collective-permute-done.13.refs_5_), channel_id=1, source_target_pairs={{0,1},{1,0},{2,3},{3,2},{4,5},{5,4},{6,7},{7,6},{8,9},{9,8},{10,11... | collective-permute-start | bytes 786440 | tf_op jit(solution)/shard_map/ppermute | solution.py:304
  48.8 8.6 %collective-permute-start.18 = (f32[64,1024]{1,0:T(8,128)S(1)}, f32[64,1024]{1,0:T(8,128)S(1)}, u32[]{:S(2)}, u32[]{:S(2)}) collective-permute-start(f32[64,1024]{1,0:T(8,128)S(1)} %collective-permute-done.16.refs_8_), channel_id=1, source_target_pairs={{0,1},{1,0},{2,3},{3,2},{4,5},{5,4},{6,7},{7,6},{8,9},{9,8},{10,11... | collective-permute-start | bytes 786440 | tf_op jit(solution)/shard_map/ppermute | solution.py:304
  49.8 9.1 %collective-permute-start.22 = (f32[64,1024]{1,0:T(8,128)S(1)}, f32[64,1024]{1,0:T(8,128)S(1)}, u32[]{:S(2)}, u32[]{:S(2)}) collective-permute-start(f32[64,1024]{1,0:T(8,128)S(1)} %collective-permute-done.20.refs_12_), channel_id=1, source_target_pairs={{0,1},{1,0},{2,3},{3,2},{4,5},{5,4},{6,7},{7,6},{8,9},{9,8},{10,11... | collective-permute-start | bytes 786440 | tf_op jit(solution)/shard_map/ppermute | solution.py:304
  49.8 9.1 %collective-permute-start.23 = (f32[64,1024]{1,0:T(8,128)S(1)}, f32[64,1024]{1,0:T(8,128)S(1)}, u32[]{:S(2)}, u32[]{:S(2)}) collective-permute-start(f32[64,1024]{1,0:T(8,128)S(1)} %collective-permute-done.21.refs_13_), channel_id=1, source_target_pairs={{0,1},{1,0},{2,3},{3,2},{4,5},{5,4},{6,7},{7,6},{8,9},{9,8},{10,11... | collective-permute-start | bytes 786440 | tf_op jit(solution)/shard_map/ppermute | solution.py:304
  53.2 5.9 %collective-permute-start.24 = (f32[72,256]{1,0:T(8,128)S(1)}, f32[72,256]{1,0:T(8,128)S(1)}, u32[]{:S(2)}, u32[]{:S(2)}) collective-permute-start(f32[72,256]{1,0:T(8,128)S(1)} %get-tuple-element.58.refs_0_), channel_id=1, source_target_pairs={{0,8},{1,9},{2,10},{3,11},{4,12},{5,13},{6,14},{7,15},{8,0},{9,1},... | collective-permute-start | bytes 221192 | tf_op jit(solution)/shard_map/ppermute | solution.py:304
  53.3 9.2 %collective-permute-start.25 = (f32[72,256]{1,0:T(8,128)S(1)}, f32[72,256]{1,0:T(8,128)S(1)}, u32[]{:S(2)}, u32[]{:S(2)}) collective-permute-start(f32[72,256]{1,0:T(8,128)S(1)} %get-tuple-element.58.refs_0_), channel_id=1, source_target_pairs={{0,16},{1,17},{2,18},{3,19},{4,20},{5,21},{6,22},{7,23},{8,24},{9,... | collective-permute-start | bytes 221192 | tf_op jit(solution)/shard_map/ppermute | solution.py:304
  57.4 6.3 %collective-permute-start.26 = (f32[72,256]{1,0:T(8,128)S(1)}, f32[72,256]{1,0:T(8,128)S(1)}, u32[]{:S(2)}, u32[]{:S(2)}) collective-permute-start(f32[72,256]{1,0:T(8,128)S(1)} %get-tuple-element.58.refs_0_), channel_id=1, source_target_pairs={{0,24},{1,25},{2,26},{3,27},{4,28},{5,29},{6,30},{7,31},{8,16},{9,... | collective-permute-start | bytes 221192 | tf_op jit(solution)/shard_map/ppermute | solution.py:304
  65.5 6.8 %collective-permute-start.34 = (f32[1,128,256]{2,1,0:T(8,128)S(1)}, f32[1,128,256]{2,1,0:T(8,128)S(1)}, u32[]{:S(2)}, u32[]{:S(2)}) collective-permute-start(f32[1,128,256]{2,1,0:T(8,128)S(1)} %get-tuple-element.71), channel_id=1, source_target_pairs={{0,8},{1,9},{2,10},{3,11},{4,12},{5,13},{6,14},{7,15},{8,0},{9,1},... | collective-permute-start | bytes 393224 | tf_op jit(solution)/shard_map/ppermute | solution.py:304
  66.7 11.9 %collective-permute-start.35 = (f32[1,128,256]{2,1,0:T(8,128)S(1)}, f32[1,128,256]{2,1,0:T(8,128)S(1)}, u32[]{:S(2)}, u32[]{:S(2)}) collective-permute-start(f32[1,128,256]{2,1,0:T(8,128)S(1)} %get-tuple-element.72), channel_id=1, source_target_pairs={{0,16},{1,17},{2,18},{3,19},{4,20},{5,21},{6,22},{7,23},{8,24},{9,... | collective-permute-start | bytes 393224 | tf_op jit(solution)/shard_map/ppermute | solution.py:304
  68.4 10.3 %collective-permute-start.36 = (f32[1,128,256]{2,1,0:T(8,128)S(1)}, f32[1,128,256]{2,1,0:T(8,128)S(1)}, u32[]{:S(2)}, u32[]{:S(2)}) collective-permute-start(f32[1,128,256]{2,1,0:T(8,128)S(1)} %get-tuple-element.73), channel_id=1, source_target_pairs={{0,24},{1,25},{2,26},{3,27},{4,28},{5,29},{6,30},{7,31},{8,16},{9,... | collective-permute-start | bytes 393224 | tf_op jit(solution)/shard_map/ppermute | solution.py:304
  70.6 15.5 %collective-permute-start.27 = (f32[192,128]{1,0:T(8,128)S(1)}, f32[192,128]{1,0:T(8,128)S(1)}, u32[]{:S(2)}, u32[]{:S(2)}) collective-permute-start(f32[192,128]{1,0:T(8,128)S(1)} %get-tuple-element.61), channel_id=1, source_target_pairs={{0,1},{1,0},{2,3},{3,2},{4,5},{5,4},{6,7},{7,6},{8,9},{9,8},{10,11... | collective-permute-start | bytes 294920 | tf_op jit(solution)/shard_map/ppermute | solution.py:304
  70.6 16.6 %collective-permute-start.28 = (f32[192,128]{1,0:T(8,128)S(1)}, f32[192,128]{1,0:T(8,128)S(1)}, u32[]{:S(2)}, u32[]{:S(2)}) collective-permute-start(f32[192,128]{1,0:T(8,128)S(1)} %get-tuple-element.62), channel_id=1, source_target_pairs={{0,2},{1,3},{2,0},{3,1},{4,6},{5,7},{6,4},{7,5},{8,10},{9,11},{10,... | collective-permute-start | bytes 294920 | tf_op jit(solution)/shard_map/ppermute | solution.py:304
  78.8 4.0 %collective-permute-start.37 = (f32[2,32,128]{2,1,0:T(8,128)S(1)}, f32[2,32,128]{2,1,0:T(8,128)S(1)}, u32[]{:S(2)}, u32[]{:S(2)}) collective-permute-start(f32[2,32,128]{2,1,0:T(8,128)S(1)} %get-tuple-element.75), channel_id=1, source_target_pairs={{0,2},{1,3},{2,0},{3,1},{4,6},{5,7},{6,4},{7,5},{8,10},{9,11},{10,... | collective-permute-start | bytes 98312 | tf_op jit(solution)/shard_map/ppermute | solution.py:304
  80.2 3.9 %collective-permute-start.38 = (f32[2,32,128]{2,1,0:T(8,128)S(1)}, f32[2,32,128]{2,1,0:T(8,128)S(1)}, u32[]{:S(2)}, u32[]{:S(2)}) collective-permute-start(f32[2,32,128]{2,1,0:T(8,128)S(1)} %get-tuple-element.76), channel_id=1, source_target_pairs={{0,4},{1,5},{2,6},{3,7},{4,0},{5,1},{6,2},{7,3},{8,12},{9,13},{10,... | collective-permute-start | bytes 98312 | tf_op jit(solution)/shard_map/ppermute | solution.py:304
  81.3 4.8 %collective-permute-start.39 = (f32[2,32,128]{2,1,0:T(8,128)S(1)}, f32[2,32,128]{2,1,0:T(8,128)S(1)}, u32[]{:S(2)}, u32[]{:S(2)}) collective-permute-start(f32[2,32,128]{2,1,0:T(8,128)S(1)} %get-tuple-element.77), channel_id=1, source_target_pairs={{0,6},{1,7},{2,4},{3,5},{4,2},{5,3},{6,0},{7,1},{8,14},{9,15},{10,... | collective-permute-start | bytes 98312 | tf_op jit(solution)/shard_map/ppermute | solution.py:304
  82.8 6.6 %collective-permute-start.29 = (f32[192,128]{1,0:T(8,128)S(1)}, f32[192,128]{1,0:T(8,128)S(1)}, u32[]{:S(2)}, u32[]{:S(2)}) collective-permute-start(f32[192,128]{1,0:T(8,128)S(1)} %get-tuple-element.63), channel_id=1, source_target_pairs={{0,3},{1,2},{2,1},{3,0},{4,7},{5,6},{6,5},{7,4},{8,11},{9,10},{10,... | collective-permute-start | bytes 294920 | tf_op jit(solution)/shard_map/ppermute | solution.py:304
  84.1 7.0 %collective-permute-start.30 = (f32[192,128]{1,0:T(8,128)S(1)}, f32[192,128]{1,0:T(8,128)S(1)}, u32[]{:S(2)}, u32[]{:S(2)}) collective-permute-start(f32[192,128]{1,0:T(8,128)S(1)} %get-tuple-element.64), channel_id=1, source_target_pairs={{0,4},{1,5},{2,6},{3,7},{4,0},{5,1},{6,2},{7,3},{8,12},{9,13},{10,... | collective-permute-start | bytes 294920 | tf_op jit(solution)/shard_map/ppermute | solution.py:304
  86.1 9.1 %collective-permute-start.31 = (f32[192,128]{1,0:T(8,128)S(1)}, f32[192,128]{1,0:T(8,128)S(1)}, u32[]{:S(2)}, u32[]{:S(2)}) collective-permute-start(f32[192,128]{1,0:T(8,128)S(1)} %get-tuple-element.65), channel_id=1, source_target_pairs={{0,5},{1,4},{2,7},{3,6},{4,1},{5,0},{6,3},{7,2},{8,13},{9,12},{10,... | collective-permute-start | bytes 294920 | tf_op jit(solution)/shard_map/ppermute | solution.py:304
  86.1 9.1 %collective-permute-start.32 = (f32[192,128]{1,0:T(8,128)S(1)}, f32[192,128]{1,0:T(8,128)S(1)}, u32[]{:S(2)}, u32[]{:S(2)}) collective-permute-start(f32[192,128]{1,0:T(8,128)S(1)} %get-tuple-element.66), channel_id=1, source_target_pairs={{0,6},{1,7},{2,4},{3,5},{4,2},{5,3},{6,0},{7,1},{8,14},{9,15},{10,... | collective-permute-start | bytes 294920 | tf_op jit(solution)/shard_map/ppermute | solution.py:304
  87.3 8.0 %collective-permute-start.33 = (f32[192,128]{1,0:T(8,128)S(1)}, f32[192,128]{1,0:T(8,128)S(1)}, u32[]{:S(2)}, u32[]{:S(2)}) collective-permute-start(f32[192,128]{1,0:T(8,128)S(1)} %get-tuple-element.67), channel_id=1, source_target_pairs={{0,7},{1,6},{2,5},{3,4},{4,3},{5,2},{6,1},{7,0},{8,15},{9,14},{10,... | collective-permute-start | bytes 294920 | tf_op jit(solution)/shard_map/ppermute | solution.py:304
  89.4 7.5 %collective-permute-start.40 = (f32[4,32,128]{2,1,0:T(8,128)S(1)}, f32[4,32,128]{2,1,0:T(8,128)S(1)}, u32[]{:S(2)}, u32[]{:S(2)}) collective-permute-start(f32[4,32,128]{2,1,0:T(8,128)S(1)} %pad_maximum_fusion), channel_id=1, source_target_pairs={{0,1},{1,0},{2,3},{3,2},{4,5},{5,4},{6,7},{7,6},{8,9},{9,8},{10,11... | collective-permute-start | bytes 196616 | tf_op jit(solution)/shard_map/ppermute | solution.py:304

commit v3 on v2

--- a/solution.py
+++ b/solution.py
@@ -261,17 +261,6 @@
     dq = (jnp.concatenate(dqs, axis=1) * scale).astype(BF16)
     dk = (jnp.concatenate(dks, axis=1) * scale).astype(BF16)
     grad_hidden[...] = dot1(dq, wq[...], NT) + dot1(dk, wk[...], NT)
-
-
-def load_weights(wq, wk, held_q, held_k, sems):
-    copies = [
-        pltpu.make_async_copy(wq, held_q, sems.at[0]),
-        pltpu.make_async_copy(wk, held_k, sems.at[1]),
-    ]
-    for copy in copies:
-        copy.start()
-    for copy in copies:
-        copy.wait()
 
 
 def turn(*refs, count):
@@ -412,17 +401,10 @@
             bfeat, dq, dk, *gstates,
         )
         backs = [backs[0]] + [exchange(item, j) for j, item in enumerate(backs) if j]
-        held = pl.pallas_call(
-            load_weights,
-            out_shape=[pltpu.VMEM(x.shape, BF16) for x in (query_weight, key_weight)],
-            in_specs=[hbm] * 2,
-            out_specs=[pl.BlockSpec(memory_space=pltpu.VMEM)] * 2,
-            scratch_shapes=[pltpu.SemaphoreType.DMA((2,))],
-        )(*(pltpu.with_memory_space_constraint(x, pltpu.HBM) for x in (query_weight, key_weight)))
         grad_hidden, grad_values = call(
             functools.partial(finish_rows, scale=scale),
             (shape(tok, width), shape(tok, group * dh, dtype=BF16)),
-            *held, *backs, final=True,
+            *backs, entry=(query_weight, key_weight), final=True,
             scratch=[pltpu.VMEM((group, tok + tok // 2, 2 * dh), F32)],
         )
         if head_count > 1:

time: 97.8 us -> 97.9 us (level)
  Pallas kernels: 14.9 us -> 13.3 us
  waiting for transfers between devices: 36.7 us -> 38.3 us
    ppermute x41, waiting for transfers between devices: 36.7 us -> 38.3 us  [exchange(): return lax.ppermute(value, 'seq', [(i, i ^ mask) for i in range(seq_count)])]
    pallas_call x1 -> x0, Pallas kernels: 1.56 us -> none  [inner_shards(): pl.pallas_call(load_weights, out_shape=[pltpu.VMEM(x.shape, BF16) for x i...]
  transfers between devices with their start and end apart: 41 -> 41, of which waited for: 14 -> 14; matrix products, arithmetic and copies ran while one was open for 0% -> 0% of each run, Pallas kernels for 10% -> 8%
where the time goes in v3:
time: 97.9 us; the launch traced here: 97.7 us
  starting transfers between devices  45.2 us (46%)
  waiting for transfers between devices  38.3 us (39%)
  Pallas kernels  13.3 us (14%)
    ppermute x41, starting transfers between devices, exchange(): return lax.ppermute(value, 'seq', [(i, i ^ mask) for i in range(seq_count)])  45.2 us
    ppermute x41, waiting for transfers between devices, exchange(): return lax.ppermute(value, 'seq', [(i, i ^ mask) for i in range(seq_count)])  38.3 us
    pallas_call x10, Pallas kernels, call(): pl.pallas_call(body, out_shape=held, in_specs=specs, out_specs=out_specs,...  10.7 us
    pallas_call x1, Pallas kernels, inner_shards(): pl.pallas_call(functools.partial(project, dh=dh, scale=scale), out_shape=...  2.63 us
  transfers between devices with their start and end apart: 41, of which 14 were waited for; matrix products, arithmetic and copies ran while one was open for 0% of the time, Pallas kernels for 8%

profile of v3, /device:TPU:0, one launch (start us, length us, event | category | flops | bytes accessed | tf_op | source)
XLA Modules:
  0.0 97.7 jit_solution(3177264132844785769)
XLA Ops:
  0.6 2.6 %shard_map.93 = (f32[128,256]{1,0:T(8,128)S(1)}, f32[128,256]{1,0:T(8,128)S(1)}, f32[128,256]{1,0:T(8,128)S(1)}, f32[128,256]{1,0:T(8,128)S(1)}, f32[128,256]{1,...) custom-call(bf16[128,1024]{1,0:T(8,128)(2,1)} %hid.1, ...), custom_call_target="tpu_custom_call" | custom-call | tf_op jit(solution)/shard_map/pallas_call | solution.py:327
  3.3 0.6 collective-permute-start
  3.8 2.6 %collective-permute-start.1 = (f32[128,256]{1,0:T(8,128)S(1)}, f32[128,256]{1,0:T(8,128)S(1)}, u32[]{:S(2)}, u32[]{:S(2)}) collective-permute-start(f32[128,256]{1,0:T(8,128)S(1)} %get-tuple-element.42), channel_id=1, source_target_pairs={{0,2},{1,3},{2,0},{3,1},{4,6},{5,7},{6,4},{7,5},{8,10},{9,11},{10,... | collective-permute-start | bytes 393224 | tf_op jit(solution)/shard_map/ppermute | solution.py:293
  6.4 1.8 %collective-permute-start.3 = (f32[128,256]{1,0:T(8,128)S(1)}, f32[128,256]{1,0:T(8,128)S(1)}, u32[]{:S(2)}, u32[]{:S(2)}) collective-permute-start(f32[128,256]{1,0:T(8,128)S(1)} %get-tuple-element.44), channel_id=1, source_target_pairs={{0,4},{1,5},{2,6},{3,7},{4,0},{5,1},{6,2},{7,3},{8,12},{9,13},{10,... | collective-permute-start | bytes 393224 | tf_op jit(solution)/shard_map/ppermute | solution.py:293
  8.2 2.6 %collective-permute-start.5 = (f32[128,256]{1,0:T(8,128)S(1)}, f32[128,256]{1,0:T(8,128)S(1)}, u32[]{:S(2)}, u32[]{:S(2)}) collective-permute-start(f32[128,256]{1,0:T(8,128)S(1)} %get-tuple-element.46), channel_id=1, source_target_pairs={{0,6},{1,7},{2,4},{3,5},{4,2},{5,3},{6,0},{7,1},{8,14},{9,15},{10,... | collective-permute-start | bytes 393224 | tf_op jit(solution)/shard_map/ppermute | solution.py:293
  10.9 1.5 %collective-permute-start.6 = (f32[128,256]{1,0:T(8,128)S(1)}, f32[128,256]{1,0:T(8,128)S(1)}, u32[]{:S(2)}, u32[]{:S(2)}) collective-permute-start(f32[128,256]{1,0:T(8,128)S(1)} %get-tuple-element.47), channel_id=1, source_target_pairs={{0,7},{1,6},{2,5},{3,4},{4,3},{5,2},{6,1},{7,0},{8,15},{9,14},{10,... | collective-permute-start | bytes 393224 | tf_op jit(solution)/shard_map/ppermute | solution.py:293
  12.4 0.7 collective-permute-done.2.refs_3_.refs_7_
  13.1 1.4 %collective-permute-start.12 = (f32[64,1024]{1,0:T(8,128)S(1)}, f32[64,1024]{1,0:T(8,128)S(1)}, u32[]{:S(2)}, u32[]{:S(2)}) collective-permute-start(f32[64,1024]{1,0:T(8,128)S(1)} %get-tuple-element.52.refs_0_), channel_id=1, source_target_pairs={{0,2},{1,3},{2,0},{3,1},{4,6},{5,7},{6,4},{7,5},{8,10},{9,11},{10,... | collective-permute-start | bytes 786440 | tf_op jit(solution)/shard_map/ppermute | solution.py:293
  14.5 1.5 %collective-permute-start.17 = (f32[64,1024]{1,0:T(8,128)S(1)}, f32[64,1024]{1,0:T(8,128)S(1)}, u32[]{:S(2)}, u32[]{:S(2)}) collective-permute-start(f32[64,1024]{1,0:T(8,128)S(1)} %get-tuple-element.53.refs_1_), channel_id=1, source_target_pairs={{0,4},{1,5},{2,6},{3,7},{4,0},{5,1},{6,2},{7,3},{8,12},{9,13},{10,... | collective-permute-start | bytes 786440 | tf_op jit(solution)/shard_map/ppermute | solution.py:293
  16.0 4.5 %collective-permute-done.4.refs_5_.refs_9_ = f32[128,256]{1,0:T(8,128)S(1)} collective-permute-done((f32[128,256]{1,0:T(8,128)S(1)}, f32[128,256]{1,0:T(8,128)S(1)}, u32[]{:S(2)}, u32[]{:S(2)}) %collective-permute-start.4) | collective-permute-done | bytes 131104 | tf_op jit(solution)/shard_map/ppermute | solution.py:293
  20.5 1.3 %shard_map.95.refs_8_ = f32[72,256]{1,0:T(8,128)S(1)} custom-call(f32[8,64,256]{2,1,0:T(8,128)S(1)} %copy-done, f32[128,256]{1,0:T(8,128)S(1)} %get-tuple-element.40.refs_0_.refs_4_, f32[128,256]{1,0:T(8,128)S(1)} %collective-permute-done.refs_1_.refs_5_, f32[128,256]{1,0:T(8,128)S(1)} %collective-permute-done.1.refs_2_.refs_6_, ...), custom_call_target="tpu_custom_call" | custom-call | tf_op jit(solution)/shard_map/pallas_call | solution.py:63
  21.9 1.6 %collective-permute-start.7 = (f32[72,256]{1,0:T(8,128)S(1)}, f32[72,256]{1,0:T(8,128)S(1)}, u32[]{:S(2)}, u32[]{:S(2)}) collective-permute-start(f32[72,256]{1,0:T(8,128)S(1)} %shard_map.95.refs_8_), channel_id=1, source_target_pairs={{0,8},{1,9},{2,10},{3,11},{4,12},{5,13},{6,14},{7,15},{8,0},{9,1},... | collective-permute-start | bytes 221192 | tf_op jit(solution)/shard_map/ppermute | solution.py:293
  23.5 1.5 %collective-permute-start.13 = (f32[64,1024]{1,0:T(8,128)S(1)}, f32[64,1024]{1,0:T(8,128)S(1)}, u32[]{:S(2)}, u32[]{:S(2)}) collective-permute-start(f32[64,1024]{1,0:T(8,128)S(1)} %get-tuple-element.53.refs_1_), channel_id=1, source_target_pairs={{0,2},{1,3},{2,0},{3,1},{4,6},{5,7},{6,4},{7,5},{8,10},{9,11},{10,... | collective-permute-start | bytes 786440 | tf_op jit(solution)/shard_map/ppermute | solution.py:293
  25.0 1.3 %collective-permute-start.16 = (f32[64,1024]{1,0:T(8,128)S(1)}, f32[64,1024]{1,0:T(8,128)S(1)}, u32[]{:S(2)}, u32[]{:S(2)}) collective-permute-start(f32[64,1024]{1,0:T(8,128)S(1)} %get-tuple-element.52.refs_0_), channel_id=1, source_target_pairs={{0,4},{1,5},{2,6},{3,7},{4,0},{5,1},{6,2},{7,3},{8,12},{9,13},{10,... | collective-permute-start | bytes 786440 | tf_op jit(solution)/shard_map/ppermute | solution.py:293
  26.3 0.8 collective-permute-done.7.refs_9_
  27.0 2.5 %collective-permute-start.8 = (f32[72,256]{1,0:T(8,128)S(1)}, f32[72,256]{1,0:T(8,128)S(1)}, u32[]{:S(2)}, u32[]{:S(2)}) collective-permute-start(f32[72,256]{1,0:T(8,128)S(1)} %shard_map.95.refs_8_), channel_id=1, source_target_pairs={{0,16},{1,17},{2,18},{3,19},{4,20},{5,21},{6,22},{7,23},{8,24},{9,... | collective-permute-start | bytes 221192 | tf_op jit(solution)/shard_map/ppermute | solution.py:293
  29.6 4.3 %collective-permute-done.8.refs_10_ = f32[72,256]{1,0:T(8,128)S(1)} collective-permute-done((f32[72,256]{1,0:T(8,128)S(1)}, f32[72,256]{1,0:T(8,128)S(1)}, u32[]{:S(2)}, u32[]{:S(2)}) %collective-permute-start.8) | collective-permute-done | bytes 73760 | tf_op jit(solution)/shard_map/ppermute | solution.py:293
  33.8 3.4 %collective-permute-start.9 = (f32[72,256]{1,0:T(8,128)S(1)}, f32[72,256]{1,0:T(8,128)S(1)}, u32[]{:S(2)}, u32[]{:S(2)}) collective-permute-start(f32[72,256]{1,0:T(8,128)S(1)} %shard_map.95.refs_8_), channel_id=1, source_target_pairs={{0,24},{1,25},{2,26},{3,27},{4,28},{5,29},{6,30},{7,31},{8,16},{9,... | collective-permute-start | bytes 221192 | tf_op jit(solution)/shard_map/ppermute | solution.py:293
  37.2 2.8 %collective-permute-done.9.refs_11_ = f32[72,256]{1,0:T(8,128)S(1)} collective-permute-done((f32[72,256]{1,0:T(8,128)S(1)}, f32[72,256]{1,0:T(8,128)S(1)}, u32[]{:S(2)}, u32[]{:S(2)}) %collective-permute-start.9) | collective-permute-done | bytes 73760 | tf_op jit(solution)/shard_map/ppermute | solution.py:293
  40.0 0.5 collective-permute-start.11
  40.5 1.3 %collective-permute-start.20 = (f32[64,1024]{1,0:T(8,128)S(1)}, f32[64,1024]{1,0:T(8,128)S(1)}, u32[]{:S(2)}, u32[]{:S(2)}) collective-permute-start(f32[64,1024]{1,0:T(8,128)S(1)} %collective-permute-done.12.refs_4_), channel_id=1, source_target_pairs={{0,4},{1,5},{2,6},{3,7},{4,0},{5,1},{6,2},{7,3},{8,12},{9,13},{10,... | collective-permute-start | bytes 786440 | tf_op jit(solution)/shard_map/ppermute | solution.py:293
  41.8 1.5 %collective-permute-start.21 = (f32[64,1024]{1,0:T(8,128)S(1)}, f32[64,1024]{1,0:T(8,128)S(1)}, u32[]{:S(2)}, u32[]{:S(2)}) collective-permute-start(f32[64,1024]{1,0:T(8,128)S(1)} %collective-permute-done.17.refs_9_), channel_id=1, source_target_pairs={{0,2},{1,3},{2,0},{3,1},{4,6},{5,7},{6,4},{7,5},{8,10},{9,11},{10,... | collective-permute-start | bytes 786440 | tf_op jit(solution)/shard_map/ppermute | solution.py:293
  43.9 4.9 %collective-permute-done.20.refs_12_ = f32[64,1024]{1,0:T(8,128)S(1)} collective-permute-done((f32[64,1024]{1,0:T(8,128)S(1)}, f32[64,1024]{1,0:T(8,128)S(1)}, u32[]{:S(2)}, u32[]{:S(2)}) %collective-permute-start.20) | collective-permute-done | bytes 262176 | tf_op jit(solution)/shard_map/ppermute | solution.py:293
  48.8 1.0 collective-permute-done.21.refs_13_
  50.3 1.0 %shard_map.94 = (f32[8,128,256]{2,1,0:T(8,128)S(1)}, f32[8,128,256]{2,1,0:T(8,128)S(1)}) custom-call(f32[8,64,256]{2,1,0:T(8,128)S(1)} %copy-done, f32[128,256]{1,0:T(8,128)S(1)} %get-tuple-element.40.refs_0_.refs_4_, f32[128,256]{1,0:T(8,128)S(1)} %collective-permute-done.refs_1_.refs_5_, f32[128,256]{1,0:T(8,128)S(1)} %collective-permute-done.1.refs_2_.refs_6_, ...), custom_call_target="tpu_custom_call" | custom-call | tf_op jit(solution)/shard_map/pallas_call | solution.py:63
  51.3 1.9 %shard_map.96 = (f32[72,256]{1,0:T(8,128)S(1)}, f32[8,128,72]{2,1,0:T(8,128)S(1)}, f32[72,256]{1,0:T(8,128)S(1)}) custom-call(f32[8,128,256]{2,1,0:T(8,128)S(1)} %get-tuple-element.49.afeat, f32[128,256]{1,0:T(8,128)S(1)} %get-tuple-element.40.refs_0_.refs_4_, f32[128,256]{1,0:T(8,128)S(1)} %collective-permute-done.refs_1_.refs_5_, ...), custom_call_target="tpu_custom_call" | custom-call | tf_op jit(solution)/shard_map/pallas_call | solution.py:63
  53.3 4.0 %collective-permute-start.25 = (f32[72,256]{1,0:T(8,128)S(1)}, f32[72,256]{1,0:T(8,128)S(1)}, u32[]{:S(2)}, u32[]{:S(2)}) collective-permute-start(f32[72,256]{1,0:T(8,128)S(1)} %get-tuple-element.54.refs_0_), channel_id=1, source_target_pairs={{0,16},{1,17},{2,18},{3,19},{4,20},{5,21},{6,22},{7,23},{8,24},{9,... | collective-permute-start | bytes 221192 | tf_op jit(solution)/shard_map/ppermute | solution.py:293
  57.7 1.2 %shard_map.97.dq = f32[8,128,64]{2,1,0:T(8,128)S(1)} custom-call(f32[8,64,256]{2,1,0:T(8,128)S(1)} %copy-done, f32[8,128,256]{2,1,0:T(8,128)S(1)} %get-tuple-element.49.afeat, f32[72,256]{1,0:T(8,128)S(1)} %get-tuple-element.50.state, f32[8,128,72]{2,1,0:T(8,128)S(1)} %get-tuple-element.51.scaled, f32[128,256]{1,0:T(8,128)S(1)} %get-tuple-element.40.refs_0_.refs_4_, ...), custom_call_target="tpu_custom_call" | custom-call | tf_op jit(solution)/shard_map/pallas_call | solution.py:63
  59.2 3.4 %collective-permute-done.25.refs_2_ = f32[72,256]{1,0:T(8,128)S(1)} collective-permute-done((f32[72,256]{1,0:T(8,128)S(1)}, f32[72,256]{1,0:T(8,128)S(1)}, u32[]{:S(2)}, u32[]{:S(2)}) %collective-permute-start.25) | collective-permute-done | bytes 73760 | tf_op jit(solution)/shard_map/ppermute | solution.py:293
  62.5 1.1 %collective-permute-done.26.refs_3_ = f32[72,256]{1,0:T(8,128)S(1)} collective-permute-done((f32[72,256]{1,0:T(8,128)S(1)}, f32[72,256]{1,0:T(8,128)S(1)}, u32[]{:S(2)}, u32[]{:S(2)}) %collective-permute-start.26) | collective-permute-done | bytes 73760 | tf_op jit(solution)/shard_map/ppermute | solution.py:293
  63.6 1.8 %shard_map.99 = (f32[8,128,64]{2,1,0:T(8,128)S(1)}, f32[1,128,256]{2,1,0:T(8,128)S(1)}, f32[1,128,256]{2,1,0:T(8,128)S(1)}, f32[1,128,256]{2,1,0:T(8,128)S(1)}, f32[1,128,256]{2,1,0:T(8,128)S(1)}) custom-call(f32[8,64,256]{2,1,0:T(8,128)S(1)} %copy-done, f32[8,128,256]{2,1,0:T(8,128)S(1)} %get-tuple-element.48.bfeat, f32[8,128,64]{2,1,0:T(8,128)S(1)} %shard_map.97.dq, ...), custom_call_target="tpu_custom_call" | custom-call | tf_op jit(solution)/shard_map/pallas_call | solution.py:63
  65.5 1.3 %collective-permute-start.34 = (f32[1,128,256]{2,1,0:T(8,128)S(1)}, f32[1,128,256]{2,1,0:T(8,128)S(1)}, u32[]{:S(2)}, u32[]{:S(2)}) collective-permute-start(f32[1,128,256]{2,1,0:T(8,128)S(1)} %get-tuple-element.67), channel_id=1, source_target_pairs={{0,8},{1,9},{2,10},{3,11},{4,12},{5,13},{6,14},{7,15},{8,0},{9,1},... | collective-permute-start | bytes 393224 | tf_op jit(solution)/shard_map/ppermute | solution.py:293
  66.8 1.7 %collective-permute-start.35 = (f32[1,128,256]{2,1,0:T(8,128)S(1)}, f32[1,128,256]{2,1,0:T(8,128)S(1)}, u32[]{:S(2)}, u32[]{:S(2)}) collective-permute-start(f32[1,128,256]{2,1,0:T(8,128)S(1)} %get-tuple-element.68), channel_id=1, source_target_pairs={{0,16},{1,17},{2,18},{3,19},{4,20},{5,21},{6,22},{7,23},{8,24},{9,... | collective-permute-start | bytes 393224 | tf_op jit(solution)/shard_map/ppermute | solution.py:293
  68.4 1.5 %collective-permute-start.36 = (f32[1,128,256]{2,1,0:T(8,128)S(1)}, f32[1,128,256]{2,1,0:T(8,128)S(1)}, u32[]{:S(2)}, u32[]{:S(2)}) collective-permute-start(f32[1,128,256]{2,1,0:T(8,128)S(1)} %get-tuple-element.69), channel_id=1, source_target_pairs={{0,24},{1,25},{2,26},{3,27},{4,28},{5,29},{6,30},{7,31},{8,16},{9,... | collective-permute-start | bytes 393224 | tf_op jit(solution)/shard_map/ppermute | solution.py:293
  69.9 0.6 shard_map.100
  70.7 1.6 %collective-permute-start.28 = (f32[192,128]{1,0:T(8,128)S(1)}, f32[192,128]{1,0:T(8,128)S(1)}, u32[]{:S(2)}, u32[]{:S(2)}) collective-permute-start(f32[192,128]{1,0:T(8,128)S(1)} %get-tuple-element.58), channel_id=1, source_target_pairs={{0,2},{1,3},{2,0},{3,1},{4,6},{5,7},{6,4},{7,5},{8,10},{9,11},{10,... | collective-permute-start | bytes 294920 | tf_op jit(solution)/shard_map/ppermute | solution.py:293
  72.2 6.5 %collective-permute-done.35 = f32[1,128,256]{2,1,0:T(8,128)S(1)} collective-permute-done((f32[1,128,256]{2,1,0:T(8,128)S(1)}, f32[1,128,256]{2,1,0:T(8,128)S(1)}, u32[]{:S(2)}, u32[]{:S(2)}) %collective-permute-start.35) | collective-permute-done | bytes 131104 | tf_op jit(solution)/shard_map/ppermute | solution.py:293
  78.8 1.4 %collective-permute-start.37 = (f32[2,32,128]{2,1,0:T(8,128)S(1)}, f32[2,32,128]{2,1,0:T(8,128)S(1)}, u32[]{:S(2)}, u32[]{:S(2)}) collective-permute-start(f32[2,32,128]{2,1,0:T(8,128)S(1)} %get-tuple-element.71), channel_id=1, source_target_pairs={{0,2},{1,3},{2,0},{3,1},{4,6},{5,7},{6,4},{7,5},{8,10},{9,11},{10,... | collective-permute-start | bytes 98312 | tf_op jit(solution)/shard_map/ppermute | solution.py:293
  80.2 1.1 %collective-permute-start.38 = (f32[2,32,128]{2,1,0:T(8,128)S(1)}, f32[2,32,128]{2,1,0:T(8,128)S(1)}, u32[]{:S(2)}, u32[]{:S(2)}) collective-permute-start(f32[2,32,128]{2,1,0:T(8,128)S(1)} %get-tuple-element.72), channel_id=1, source_target_pairs={{0,4},{1,5},{2,6},{3,7},{4,0},{5,1},{6,2},{7,3},{8,12},{9,13},{10,... | collective-permute-start | bytes 98312 | tf_op jit(solution)/shard_map/ppermute | solution.py:293
  81.3 1.1 %collective-permute-start.39 = (f32[2,32,128]{2,1,0:T(8,128)S(1)}, f32[2,32,128]{2,1,0:T(8,128)S(1)}, u32[]{:S(2)}, u32[]{:S(2)}) collective-permute-start(f32[2,32,128]{2,1,0:T(8,128)S(1)} %get-tuple-element.73), channel_id=1, source_target_pairs={{0,6},{1,7},{2,4},{3,5},{4,2},{5,3},{6,0},{7,1},{8,14},{9,15},{10,... | collective-permute-start | bytes 98312 | tf_op jit(solution)/shard_map/ppermute | solution.py:293
  82.8 1.3 %collective-permute-done.38.refs_2_ = f32[2,32,128]{2,1,0:T(8,128)S(1)} collective-permute-done((f32[2,32,128]{2,1,0:T(8,128)S(1)}, f32[2,32,128]{2,1,0:T(8,128)S(1)}, u32[]{:S(2)}, u32[]{:S(2)}) %collective-permute-start.38) | collective-permute-done | bytes 32800 | tf_op jit(solution)/shard_map/ppermute | solution.py:293
  84.1 1.1 %collective-permute-start.30 = (f32[192,128]{1,0:T(8,128)S(1)}, f32[192,128]{1,0:T(8,128)S(1)}, u32[]{:S(2)}, u32[]{:S(2)}) collective-permute-start(f32[192,128]{1,0:T(8,128)S(1)} %get-tuple-element.60), channel_id=1, source_target_pairs={{0,4},{1,5},{2,6},{3,7},{4,0},{5,1},{6,2},{7,3},{8,12},{9,13},{10,... | collective-permute-start | bytes 294920 | tf_op jit(solution)/shard_map/ppermute | solution.py:293
  85.2 0.9 collective-permute-done.39.refs_3_
  86.1 1.2 %collective-permute-start.32 = (f32[192,128]{1,0:T(8,128)S(1)}, f32[192,128]{1,0:T(8,128)S(1)}, u32[]{:S(2)}, u32[]{:S(2)}) collective-permute-start(f32[192,128]{1,0:T(8,128)S(1)} %get-tuple-element.62), channel_id=1, source_target_pairs={{0,6},{1,7},{2,4},{3,5},{4,2},{5,3},{6,0},{7,1},{8,14},{9,15},{10,... | collective-permute-start | bytes 294920 | tf_op jit(solution)/shard_map/ppermute | solution.py:293
  87.3 2.1 %collective-permute-start.33 = (f32[192,128]{1,0:T(8,128)S(1)}, f32[192,128]{1,0:T(8,128)S(1)}, u32[]{:S(2)}, u32[]{:S(2)}) collective-permute-start(f32[192,128]{1,0:T(8,128)S(1)} %get-tuple-element.63), channel_id=1, source_target_pairs={{0,7},{1,6},{2,5},{3,4},{4,3},{5,2},{6,1},{7,0},{8,15},{9,14},{10,... | collective-permute-start | bytes 294920 | tf_op jit(solution)/shard_map/ppermute | solution.py:293
  89.5 5.7 %collective-permute-done.31.refs_5_ = f32[192,128]{1,0:T(8,128)S(1)} collective-permute-done((f32[192,128]{1,0:T(8,128)S(1)}, f32[192,128]{1,0:T(8,128)S(1)}, u32[]{:S(2)}, u32[]{:S(2)}) %collective-permute-start.31) | collective-permute-done | bytes 98336 | tf_op jit(solution)/shard_map/ppermute | solution.py:293
  95.3 1.7 %shard_map.101 = (f32[128,1024]{1,0:T(8,128)}, bf16[128,512]{1,0:T(8,128)(2,1)}) custom-call(bf16[1024,512]{1,0:T(8,128)(2,1)S(1)} %copy-done.1, bf16[1024,512]{1,0:T(8,128)(2,1)S(1)} %copy-done.2, f32[192,128]{1,0:T(8,128)S(1)} %get-tuple-element.56.refs_0_, f32[192,128]{1,0:T(8,128)S(1)} %collective-permute-done.27.refs_1_, ...), custom_call_target="tpu_custom_call" | custom-call | tf_op jit(solution)/shard_map/pallas_call | solution.py:63
  97.0 0.8 shard_map.103
  (56 shorter events, 2.5 us)
Async XLA Ops:
  0.6 19.9 %copy-start = (f32[8,64,256]{2,1,0:T(8,128)S(1)}, f32[8,64,256]{2,1,0:T(8,128)}, u32[]{:S(2)}) copy-start(f32[8,64,256]{2,1,0:T(8,128)} %feats.7) | copy-start | bytes 1572868
  3.3 4.9 %collective-permute-start = (f32[128,256]{1,0:T(8,128)S(1)}, f32[128,256]{1,0:T(8,128)S(1)}, u32[]{:S(2)}, u32[]{:S(2)}) collective-permute-start(f32[128,256]{1,0:T(8,128)S(1)} %get-tuple-element.41), channel_id=1, source_target_pairs={{0,1},{1,0},{2,3},{3,2},{4,5},{5,4},{6,7},{7,6},{8,9},{9,8},{10,11... | collective-permute-start | bytes 393224 | tf_op jit(solution)/shard_map/ppermute | solution.py:293
  3.8 7.0 %collective-permute-start.1 = (f32[128,256]{1,0:T(8,128)S(1)}, f32[128,256]{1,0:T(8,128)S(1)}, u32[]{:S(2)}, u32[]{:S(2)}) collective-permute-start(f32[128,256]{1,0:T(8,128)S(1)} %get-tuple-element.42), channel_id=1, source_target_pairs={{0,2},{1,3},{2,0},{3,1},{4,6},{5,7},{6,4},{7,5},{8,10},{9,11},{10,... | collective-permute-start | bytes 393224 | tf_op jit(solution)/shard_map/ppermute | solution.py:293
  6.4 6.7 %collective-permute-start.2 = (f32[128,256]{1,0:T(8,128)S(1)}, f32[128,256]{1,0:T(8,128)S(1)}, u32[]{:S(2)}, u32[]{:S(2)}) collective-permute-start(f32[128,256]{1,0:T(8,128)S(1)} %get-tuple-element.43), channel_id=1, source_target_pairs={{0,3},{1,2},{2,1},{3,0},{4,7},{5,6},{6,5},{7,4},{8,11},{9,10},{10,... | collective-permute-start | bytes 393224 | tf_op jit(solution)/shard_map/ppermute | solution.py:293
  6.4 8.1 %collective-permute-start.3 = (f32[128,256]{1,0:T(8,128)S(1)}, f32[128,256]{1,0:T(8,128)S(1)}, u32[]{:S(2)}, u32[]{:S(2)}) collective-permute-start(f32[128,256]{1,0:T(8,128)S(1)} %get-tuple-element.44), channel_id=1, source_target_pairs={{0,4},{1,5},{2,6},{3,7},{4,0},{5,1},{6,2},{7,3},{8,12},{9,13},{10,... | collective-permute-start | bytes 393224 | tf_op jit(solution)/shard_map/ppermute | solution.py:293
  8.2 12.3 %collective-permute-start.4 = (f32[128,256]{1,0:T(8,128)S(1)}, f32[128,256]{1,0:T(8,128)S(1)}, u32[]{:S(2)}, u32[]{:S(2)}) collective-permute-start(f32[128,256]{1,0:T(8,128)S(1)} %get-tuple-element.45), channel_id=1, source_target_pairs={{0,5},{1,4},{2,7},{3,6},{4,1},{5,0},{6,3},{7,2},{8,13},{9,12},{10,... | collective-permute-start | bytes 393224 | tf_op jit(solution)/shard_map/ppermute | solution.py:293
  8.2 12.3 %collective-permute-start.5 = (f32[128,256]{1,0:T(8,128)S(1)}, f32[128,256]{1,0:T(8,128)S(1)}, u32[]{:S(2)}, u32[]{:S(2)}) collective-permute-start(f32[128,256]{1,0:T(8,128)S(1)} %get-tuple-element.46), channel_id=1, source_target_pairs={{0,6},{1,7},{2,4},{3,5},{4,2},{5,3},{6,0},{7,1},{8,14},{9,15},{10,... | collective-permute-start | bytes 393224 | tf_op jit(solution)/shard_map/ppermute | solution.py:293
  10.9 9.7 %collective-permute-start.6 = (f32[128,256]{1,0:T(8,128)S(1)}, f32[128,256]{1,0:T(8,128)S(1)}, u32[]{:S(2)}, u32[]{:S(2)}) collective-permute-start(f32[128,256]{1,0:T(8,128)S(1)} %get-tuple-element.47), channel_id=1, source_target_pairs={{0,7},{1,6},{2,5},{3,4},{4,3},{5,2},{6,1},{7,0},{8,15},{9,14},{10,... | collective-permute-start | bytes 393224 | tf_op jit(solution)/shard_map/ppermute | solution.py:293
  13.1 26.9 %collective-permute-start.12 = (f32[64,1024]{1,0:T(8,128)S(1)}, f32[64,1024]{1,0:T(8,128)S(1)}, u32[]{:S(2)}, u32[]{:S(2)}) collective-permute-start(f32[64,1024]{1,0:T(8,128)S(1)} %get-tuple-element.52.refs_0_), channel_id=1, source_target_pairs={{0,2},{1,3},{2,0},{3,1},{4,6},{5,7},{6,4},{7,5},{8,10},{9,11},{10,... | collective-permute-start | bytes 786440 | tf_op jit(solution)/shard_map/ppermute | solution.py:293
  14.5 26.0 %collective-permute-start.17 = (f32[64,1024]{1,0:T(8,128)S(1)}, f32[64,1024]{1,0:T(8,128)S(1)}, u32[]{:S(2)}, u32[]{:S(2)}) collective-permute-start(f32[64,1024]{1,0:T(8,128)S(1)} %get-tuple-element.53.refs_1_), channel_id=1, source_target_pairs={{0,4},{1,5},{2,6},{3,7},{4,0},{5,1},{6,2},{7,3},{8,12},{9,13},{10,... | collective-permute-start | bytes 786440 | tf_op jit(solution)/shard_map/ppermute | solution.py:293
  21.9 5.1 %collective-permute-start.7 = (f32[72,256]{1,0:T(8,128)S(1)}, f32[72,256]{1,0:T(8,128)S(1)}, u32[]{:S(2)}, u32[]{:S(2)}) collective-permute-start(f32[72,256]{1,0:T(8,128)S(1)} %shard_map.95.refs_8_), channel_id=1, source_target_pairs={{0,8},{1,9},{2,10},{3,11},{4,12},{5,13},{6,14},{7,15},{8,0},{9,1},... | collective-permute-start | bytes 221192 | tf_op jit(solution)/shard_map/ppermute | solution.py:293
  23.5 18.3 %collective-permute-start.13 = (f32[64,1024]{1,0:T(8,128)S(1)}, f32[64,1024]{1,0:T(8,128)S(1)}, u32[]{:S(2)}, u32[]{:S(2)}) collective-permute-start(f32[64,1024]{1,0:T(8,128)S(1)} %get-tuple-element.53.refs_1_), channel_id=1, source_target_pairs={{0,2},{1,3},{2,0},{3,1},{4,6},{5,7},{6,4},{7,5},{8,10},{9,11},{10,... | collective-permute-start | bytes 786440 | tf_op jit(solution)/shard_map/ppermute | solution.py:293
  25.0 18.3 %collective-permute-start.16 = (f32[64,1024]{1,0:T(8,128)S(1)}, f32[64,1024]{1,0:T(8,128)S(1)}, u32[]{:S(2)}, u32[]{:S(2)}) collective-permute-start(f32[64,1024]{1,0:T(8,128)S(1)} %get-tuple-element.52.refs_0_), channel_id=1, source_target_pairs={{0,4},{1,5},{2,6},{3,7},{4,0},{5,1},{6,2},{7,3},{8,12},{9,13},{10,... | collective-permute-start | bytes 786440 | tf_op jit(solution)/shard_map/ppermute | solution.py:293
  27.0 6.8 %collective-permute-start.8 = (f32[72,256]{1,0:T(8,128)S(1)}, f32[72,256]{1,0:T(8,128)S(1)}, u32[]{:S(2)}, u32[]{:S(2)}) collective-permute-start(f32[72,256]{1,0:T(8,128)S(1)} %shard_map.95.refs_8_), channel_id=1, source_target_pairs={{0,16},{1,17},{2,18},{3,19},{4,20},{5,21},{6,22},{7,23},{8,24},{9,... | collective-permute-start | bytes 221192 | tf_op jit(solution)/shard_map/ppermute | solution.py:293
  33.8 6.2 %collective-permute-start.9 = (f32[72,256]{1,0:T(8,128)S(1)}, f32[72,256]{1,0:T(8,128)S(1)}, u32[]{:S(2)}, u32[]{:S(2)}) collective-permute-start(f32[72,256]{1,0:T(8,128)S(1)} %shard_map.95.refs_8_), channel_id=1, source_target_pairs={{0,24},{1,25},{2,26},{3,27},{4,28},{5,29},{6,30},{7,31},{8,16},{9,... | collective-permute-start | bytes 221192 | tf_op jit(solution)/shard_map/ppermute | solution.py:293
  40.0 3.3 %collective-permute-start.10 = (f32[64,1024]{1,0:T(8,128)S(1)}, f32[64,1024]{1,0:T(8,128)S(1)}, u32[]{:S(2)}, u32[]{:S(2)}) collective-permute-start(f32[64,1024]{1,0:T(8,128)S(1)} %get-tuple-element.52.refs_0_), channel_id=1, source_target_pairs={{0,1},{1,0},{2,3},{3,2},{4,5},{5,4},{6,7},{7,6},{8,9},{9,8},{10,11... | collective-permute-start | bytes 786440 | tf_op jit(solution)/shard_map/ppermute | solution.py:293
  40.0 3.8 %collective-permute-start.11 = (f32[64,1024]{1,0:T(8,128)S(1)}, f32[64,1024]{1,0:T(8,128)S(1)}, u32[]{:S(2)}, u32[]{:S(2)}) collective-permute-start(f32[64,1024]{1,0:T(8,128)S(1)} %get-tuple-element.53.refs_1_), channel_id=1, source_target_pairs={{0,1},{1,0},{2,3},{3,2},{4,5},{5,4},{6,7},{7,6},{8,9},{9,8},{10,11... | collective-permute-start | bytes 786440 | tf_op jit(solution)/shard_map/ppermute | solution.py:293
  40.5 8.3 %collective-permute-start.20 = (f32[64,1024]{1,0:T(8,128)S(1)}, f32[64,1024]{1,0:T(8,128)S(1)}, u32[]{:S(2)}, u32[]{:S(2)}) collective-permute-start(f32[64,1024]{1,0:T(8,128)S(1)} %collective-permute-done.12.refs_4_), channel_id=1, source_target_pairs={{0,4},{1,5},{2,6},{3,7},{4,0},{5,1},{6,2},{7,3},{8,12},{9,13},{10,... | collective-permute-start | bytes 786440 | tf_op jit(solution)/shard_map/ppermute | solution.py:293
  41.8 8.0 %collective-permute-start.21 = (f32[64,1024]{1,0:T(8,128)S(1)}, f32[64,1024]{1,0:T(8,128)S(1)}, u32[]{:S(2)}, u32[]{:S(2)}) collective-permute-start(f32[64,1024]{1,0:T(8,128)S(1)} %collective-permute-done.17.refs_9_), channel_id=1, source_target_pairs={{0,2},{1,3},{2,0},{3,1},{4,6},{5,7},{6,4},{7,5},{8,10},{9,11},{10,... | collective-permute-start | bytes 786440 | tf_op jit(solution)/shard_map/ppermute | solution.py:293
  43.3 6.5 %collective-permute-start.14 = (f32[64,1024]{1,0:T(8,128)S(1)}, f32[64,1024]{1,0:T(8,128)S(1)}, u32[]{:S(2)}, u32[]{:S(2)}) collective-permute-start(f32[64,1024]{1,0:T(8,128)S(1)} %collective-permute-done.12.refs_4_), channel_id=1, source_target_pairs={{0,1},{1,0},{2,3},{3,2},{4,5},{5,4},{6,7},{7,6},{8,9},{9,8},{10,11... | collective-permute-start | bytes 786440 | tf_op jit(solution)/shard_map/ppermute | solution.py:293
  43.3 9.9 %collective-permute-start.19 = (f32[64,1024]{1,0:T(8,128)S(1)}, f32[64,1024]{1,0:T(8,128)S(1)}, u32[]{:S(2)}, u32[]{:S(2)}) collective-permute-start(f32[64,1024]{1,0:T(8,128)S(1)} %collective-permute-done.17.refs_9_), channel_id=1, source_target_pairs={{0,1},{1,0},{2,3},{3,2},{4,5},{5,4},{6,7},{7,6},{8,9},{9,8},{10,11... | collective-permute-start | bytes 786440 | tf_op jit(solution)/shard_map/ppermute | solution.py:293
  43.8 9.5 %collective-permute-start.15 = (f32[64,1024]{1,0:T(8,128)S(1)}, f32[64,1024]{1,0:T(8,128)S(1)}, u32[]{:S(2)}, u32[]{:S(2)}) collective-permute-start(f32[64,1024]{1,0:T(8,128)S(1)} %collective-permute-done.13.refs_5_), channel_id=1, source_target_pairs={{0,1},{1,0},{2,3},{3,2},{4,5},{5,4},{6,7},{7,6},{8,9},{9,8},{10,11... | collective-permute-start | bytes 786440 | tf_op jit(solution)/shard_map/ppermute | solution.py:293
  48.8 8.6 %collective-permute-start.18 = (f32[64,1024]{1,0:T(8,128)S(1)}, f32[64,1024]{1,0:T(8,128)S(1)}, u32[]{:S(2)}, u32[]{:S(2)}) collective-permute-start(f32[64,1024]{1,0:T(8,128)S(1)} %collective-permute-done.16.refs_8_), channel_id=1, source_target_pairs={{0,1},{1,0},{2,3},{3,2},{4,5},{5,4},{6,7},{7,6},{8,9},{9,8},{10,11... | collective-permute-start | bytes 786440 | tf_op jit(solution)/shard_map/ppermute | solution.py:293
  49.8 9.1 %collective-permute-start.22 = (f32[64,1024]{1,0:T(8,128)S(1)}, f32[64,1024]{1,0:T(8,128)S(1)}, u32[]{:S(2)}, u32[]{:S(2)}) collective-permute-start(f32[64,1024]{1,0:T(8,128)S(1)} %collective-permute-done.20.refs_12_), channel_id=1, source_target_pairs={{0,1},{1,0},{2,3},{3,2},{4,5},{5,4},{6,7},{7,6},{8,9},{9,8},{10,11... | collective-permute-start | bytes 786440 | tf_op jit(solution)/shard_map/ppermute | solution.py:293
  49.8 9.1 %collective-permute-start.23 = (f32[64,1024]{1,0:T(8,128)S(1)}, f32[64,1024]{1,0:T(8,128)S(1)}, u32[]{:S(2)}, u32[]{:S(2)}) collective-permute-start(f32[64,1024]{1,0:T(8,128)S(1)} %collective-permute-done.21.refs_13_), channel_id=1, source_target_pairs={{0,1},{1,0},{2,3},{3,2},{4,5},{5,4},{6,7},{7,6},{8,9},{9,8},{10,11... | collective-permute-start | bytes 786440 | tf_op jit(solution)/shard_map/ppermute | solution.py:293
  53.2 5.9 %collective-permute-start.24 = (f32[72,256]{1,0:T(8,128)S(1)}, f32[72,256]{1,0:T(8,128)S(1)}, u32[]{:S(2)}, u32[]{:S(2)}) collective-permute-start(f32[72,256]{1,0:T(8,128)S(1)} %get-tuple-element.54.refs_0_), channel_id=1, source_target_pairs={{0,8},{1,9},{2,10},{3,11},{4,12},{5,13},{6,14},{7,15},{8,0},{9,1},... | collective-permute-start | bytes 221192 | tf_op jit(solution)/shard_map/ppermute | solution.py:293
  53.3 9.2 %collective-permute-start.25 = (f32[72,256]{1,0:T(8,128)S(1)}, f32[72,256]{1,0:T(8,128)S(1)}, u32[]{:S(2)}, u32[]{:S(2)}) collective-permute-start(f32[72,256]{1,0:T(8,128)S(1)} %get-tuple-element.54.refs_0_), channel_id=1, source_target_pairs={{0,16},{1,17},{2,18},{3,19},{4,20},{5,21},{6,22},{7,23},{8,24},{9,... | collective-permute-start | bytes 221192 | tf_op jit(solution)/shard_map/ppermute | solution.py:293
  57.4 6.3 %collective-permute-start.26 = (f32[72,256]{1,0:T(8,128)S(1)}, f32[72,256]{1,0:T(8,128)S(1)}, u32[]{:S(2)}, u32[]{:S(2)}) collective-permute-start(f32[72,256]{1,0:T(8,128)S(1)} %get-tuple-element.54.refs_0_), channel_id=1, source_target_pairs={{0,24},{1,25},{2,26},{3,27},{4,28},{5,29},{6,30},{7,31},{8,16},{9,... | collective-permute-start | bytes 221192 | tf_op jit(solution)/shard_map/ppermute | solution.py:293
  65.5 29.8 %copy-start.1 = (bf16[1024,512]{1,0:T(8,128)(2,1)S(1)}, bf16[1024,512]{1,0:T(8,128)(2,1)}, u32[]{:S(2)}) copy-start(bf16[1024,512]{1,0:T(8,128)(2,1)} %wq.3) | copy-start | bytes 3145732
  65.5 29.8 %copy-start.2 = (bf16[1024,512]{1,0:T(8,128)(2,1)S(1)}, bf16[1024,512]{1,0:T(8,128)(2,1)}, u32[]{:S(2)}) copy-start(bf16[1024,512]{1,0:T(8,128)(2,1)} %wk.3) | copy-start | bytes 3145732
  65.5 6.8 %collective-permute-start.34 = (f32[1,128,256]{2,1,0:T(8,128)S(1)}, f32[1,128,256]{2,1,0:T(8,128)S(1)}, u32[]{:S(2)}, u32[]{:S(2)}) collective-permute-start(f32[1,128,256]{2,1,0:T(8,128)S(1)} %get-tuple-element.67), channel_id=1, source_target_pairs={{0,8},{1,9},{2,10},{3,11},{4,12},{5,13},{6,14},{7,15},{8,0},{9,1},... | collective-permute-start | bytes 393224 | tf_op jit(solution)/shard_map/ppermute | solution.py:293
  66.8 11.9 %collective-permute-start.35 = (f32[1,128,256]{2,1,0:T(8,128)S(1)}, f32[1,128,256]{2,1,0:T(8,128)S(1)}, u32[]{:S(2)}, u32[]{:S(2)}) collective-permute-start(f32[1,128,256]{2,1,0:T(8,128)S(1)} %get-tuple-element.68), channel_id=1, source_target_pairs={{0,16},{1,17},{2,18},{3,19},{4,20},{5,21},{6,22},{7,23},{8,24},{9,... | collective-permute-start | bytes 393224 | tf_op jit(solution)/shard_map/ppermute | solution.py:293
  68.4 10.3 %collective-permute-start.36 = (f32[1,128,256]{2,1,0:T(8,128)S(1)}, f32[1,128,256]{2,1,0:T(8,128)S(1)}, u32[]{:S(2)}, u32[]{:S(2)}) collective-permute-start(f32[1,128,256]{2,1,0:T(8,128)S(1)} %get-tuple-element.69), channel_id=1, source_target_pairs={{0,24},{1,25},{2,26},{3,27},{4,28},{5,29},{6,30},{7,31},{8,16},{9,... | collective-permute-start | bytes 393224 | tf_op jit(solution)/shard_map/ppermute | solution.py:293
  70.6 15.5 %collective-permute-start.27 = (f32[192,128]{1,0:T(8,128)S(1)}, f32[192,128]{1,0:T(8,128)S(1)}, u32[]{:S(2)}, u32[]{:S(2)}) collective-permute-start(f32[192,128]{1,0:T(8,128)S(1)} %get-tuple-element.57), channel_id=1, source_target_pairs={{0,1},{1,0},{2,3},{3,2},{4,5},{5,4},{6,7},{7,6},{8,9},{9,8},{10,11... | collective-permute-start | bytes 294920 | tf_op jit(solution)/shard_map/ppermute | solution.py:293
  70.7 16.6 %collective-permute-start.28 = (f32[192,128]{1,0:T(8,128)S(1)}, f32[192,128]{1,0:T(8,128)S(1)}, u32[]{:S(2)}, u32[]{:S(2)}) collective-permute-start(f32[192,128]{1,0:T(8,128)S(1)} %get-tuple-element.58), channel_id=1, source_target_pairs={{0,2},{1,3},{2,0},{3,1},{4,6},{5,7},{6,4},{7,5},{8,10},{9,11},{10,... | collective-permute-start | bytes 294920 | tf_op jit(solution)/shard_map/ppermute | solution.py:293
  78.8 4.0 %collective-permute-start.37 = (f32[2,32,128]{2,1,0:T(8,128)S(1)}, f32[2,32,128]{2,1,0:T(8,128)S(1)}, u32[]{:S(2)}, u32[]{:S(2)}) collective-permute-start(f32[2,32,128]{2,1,0:T(8,128)S(1)} %get-tuple-element.71), channel_id=1, source_target_pairs={{0,2},{1,3},{2,0},{3,1},{4,6},{5,7},{6,4},{7,5},{8,10},{9,11},{10,... | collective-permute-start | bytes 98312 | tf_op jit(solution)/shard_map/ppermute | solution.py:293
  80.2 3.9 %collective-permute-start.38 = (f32[2,32,128]{2,1,0:T(8,128)S(1)}, f32[2,32,128]{2,1,0:T(8,128)S(1)}, u32[]{:S(2)}, u32[]{:S(2)}) collective-permute-start(f32[2,32,128]{2,1,0:T(8,128)S(1)} %get-tuple-element.72), channel_id=1, source_target_pairs={{0,4},{1,5},{2,6},{3,7},{4,0},{5,1},{6,2},{7,3},{8,12},{9,13},{10,... | collective-permute-start | bytes 98312 | tf_op jit(solution)/shard_map/ppermute | solution.py:293
  81.3 4.8 %collective-permute-start.39 = (f32[2,32,128]{2,1,0:T(8,128)S(1)}, f32[2,32,128]{2,1,0:T(8,128)S(1)}, u32[]{:S(2)}, u32[]{:S(2)}) collective-permute-start(f32[2,32,128]{2,1,0:T(8,128)S(1)} %get-tuple-element.73), channel_id=1, source_target_pairs={{0,6},{1,7},{2,4},{3,5},{4,2},{5,3},{6,0},{7,1},{8,14},{9,15},{10,... | collective-permute-start | bytes 98312 | tf_op jit(solution)/shard_map/ppermute | solution.py:293
  82.8 6.6 %collective-permute-start.29 = (f32[192,128]{1,0:T(8,128)S(1)}, f32[192,128]{1,0:T(8,128)S(1)}, u32[]{:S(2)}, u32[]{:S(2)}) collective-permute-start(f32[192,128]{1,0:T(8,128)S(1)} %get-tuple-element.59), channel_id=1, source_target_pairs={{0,3},{1,2},{2,1},{3,0},{4,7},{5,6},{6,5},{7,4},{8,11},{9,10},{10,... | collective-permute-start | bytes 294920 | tf_op jit(solution)/shard_map/ppermute | solution.py:293
  84.1 5.4 %collective-permute-start.30 = (f32[192,128]{1,0:T(8,128)S(1)}, f32[192,128]{1,0:T(8,128)S(1)}, u32[]{:S(2)}, u32[]{:S(2)}) collective-permute-start(f32[192,128]{1,0:T(8,128)S(1)} %get-tuple-element.60), channel_id=1, source_target_pairs={{0,4},{1,5},{2,6},{3,7},{4,0},{5,1},{6,2},{7,3},{8,12},{9,13},{10,... | collective-permute-start | bytes 294920 | tf_op jit(solution)/shard_map/ppermute | solution.py:293
  86.1 9.1 %collective-permute-start.31 = (f32[192,128]{1,0:T(8,128)S(1)}, f32[192,128]{1,0:T(8,128)S(1)}, u32[]{:S(2)}, u32[]{:S(2)}) collective-permute-start(f32[192,128]{1,0:T(8,128)S(1)} %get-tuple-element.61), channel_id=1, source_target_pairs={{0,5},{1,4},{2,7},{3,6},{4,1},{5,0},{6,3},{7,2},{8,13},{9,12},{10,... | collective-permute-start | bytes 294920 | tf_op jit(solution)/shard_map/ppermute | solution.py:293
  86.1 9.1 %collective-permute-start.32 = (f32[192,128]{1,0:T(8,128)S(1)}, f32[192,128]{1,0:T(8,128)S(1)}, u32[]{:S(2)}, u32[]{:S(2)}) collective-permute-start(f32[192,128]{1,0:T(8,128)S(1)} %get-tuple-element.62), channel_id=1, source_target_pairs={{0,6},{1,7},{2,4},{3,5},{4,2},{5,3},{6,0},{7,1},{8,14},{9,15},{10,... | collective-permute-start | bytes 294920 | tf_op jit(solution)/shard_map/ppermute | solution.py:293
  87.3 8.0 %collective-permute-start.33 = (f32[192,128]{1,0:T(8,128)S(1)}, f32[192,128]{1,0:T(8,128)S(1)}, u32[]{:S(2)}, u32[]{:S(2)}) collective-permute-start(f32[192,128]{1,0:T(8,128)S(1)} %get-tuple-element.63), channel_id=1, source_target_pairs={{0,7},{1,6},{2,5},{3,4},{4,3},{5,2},{6,1},{7,0},{8,15},{9,14},{10,... | collective-permute-start | bytes 294920 | tf_op jit(solution)/shard_map/ppermute | solution.py:293
  89.4 7.5 %collective-permute-start.40 = (f32[4,32,128]{2,1,0:T(8,128)S(1)}, f32[4,32,128]{2,1,0:T(8,128)S(1)}, u32[]{:S(2)}, u32[]{:S(2)}) collective-permute-start(f32[4,32,128]{2,1,0:T(8,128)S(1)} %pad_maximum_fusion), channel_id=1, source_target_pairs={{0,1},{1,0},{2,3},{3,2},{4,5},{5,4},{6,7},{7,6},{8,9},{9,8},{10,11... | collective-permute-start | bytes 196616 | tf_op jit(solution)/shard_map/ppermute | solution.py:293
